TPU v7x, 32 devices: a whole 2x2x4 slice. The times are simulated.
32 devices in a mesh: pipe: 2 (over y), dp: 4 (over z), tensor: 4 (over x, core).
Axes of the slice: x: 2, y: 2, z: 4, core: 2. Of those that a mesh axis runs over, the one named last changes fastest.
Arguments:
- saved: bfloat16 [2, 2, 256, 1024], P('pipe', None, 'dp'), may hold values from -6 to 6
- top_grad: bfloat16 [2, 256, 1024], P(None, 'dp'), may hold values from -6 to 6
- gain: bfloat16 [2, 1024], P('pipe', 'dp'), may hold values from 0.25 to 1.75
- w_query: bfloat16 [2, 1024, 1536], P('pipe', 'dp', 'tensor'), may hold values from -0.1875 to 0.1875
- w_latent: bfloat16 [2, 1024, 576], P('pipe', 'dp'), may hold values from -0.1875 to 0.1875
- compressed_gain: bfloat16 [2, 512], P('pipe', 'dp'), may hold values from 0.25 to 1.75
- expand_weight: bfloat16 [2, 512, 2048], P('pipe', 'dp', 'tensor'), may hold values from -0.25 to 0.25
- w_output: bfloat16 [2, 1024, 1024], P('pipe', 'tensor', 'dp'), may hold values from -0.1875 to 0.1875
Outputs:
- input_grad: bfloat16 [2, 2, 256, 1024], P('pipe', None, ('dp', 'tensor'))
- grad_gain: float32 [2, 1024], P('pipe', 'dp')
- grad_query: float32 [2, 1024, 1536], P('pipe', 'dp', 'tensor')
- grad_latent: float32 [2, 1024, 576], P('pipe', 'dp')
- grad_latent_gain: float32 [2, 512], P('pipe', 'dp')
- grad_expand: float32 [2, 512, 2048], P('pipe', 'dp', 'tensor')
- grad_output: float32 [2, 1024, 1024], P('pipe', 'tensor', 'dp')
All inputs are finite; a program needn't handle non-finite values.
Results may differ from a plain program's by a relative error of at most 0.04.
Values may be sent and summed in bfloat16 or wider, within the bound.
No kernel may reach another device: no remote copies, remote signals or barrier semaphores. Data moves between devices by JAX's collectives and lax.ppermute only.
A program may use at most 64 MiB of HBM per device.

v0:
```python
import jax
import jax.numpy as jnp
import numpy as np
from jax import lax
from jax.experimental import pallas as pl
from jax.experimental.pallas import tpu as pltpu
from jax.sharding import PartitionSpec as P


NOPE = 128
ROPE = 64
VDIM = 128
COMPRESSED_RANK = 512


EPS = 1e-06


def passed_along(value, axis, steps):
    count = lax.axis_size(axis)
    first, last = (max(0, -steps), min(count, count - steps))
    return lax.ppermute(value, axis, [(source, source + steps) for source in range(first, last)])


def root_mean_scale(values, scale):
    return values * lax.rsqrt(jnp.mean(values * values, axis=-1, keepdims=True) + EPS) * scale


def rotary_angles(values):
    length = values.shape[0]
    half = values.shape[-1] // 2
    freq = jnp.exp(-jnp.log(10000.0) * jnp.arange(half, dtype=jnp.float32) / half)
    angle = jnp.arange(length, dtype=jnp.float32)[:, None] * freq[None, :]
    cosine = jnp.cos(angle)[:, None, :]
    sine = jnp.sin(angle)[:, None, :]
    first = values[..., :half]
    second = values[..., half:]
    return jnp.concatenate(
        [first * cosine - second * sine, second * cosine + first * sine], axis=-1
    )


def branch(normed, w_q, w_lat, latent_norm_gain, w_exp, w_out):
    length = normed.shape[0]
    heads = w_q.shape[1] // (NOPE + ROPE)
    rounded = normed.astype(jnp.bfloat16)
    query = jnp.dot(rounded, w_q, preferred_element_type=jnp.float32).reshape(
        length, heads, NOPE + ROPE
    )
    latent_state = jnp.dot(rounded, w_lat, preferred_element_type=jnp.float32)
    compressed_state = root_mean_scale(latent_state[:, :COMPRESSED_RANK], latent_norm_gain).astype(
        jnp.bfloat16
    )
    rotary_key_part = rotary_angles(latent_state[:, None, COMPRESSED_RANK:])[:, 0, :]
    expanded = jnp.dot(compressed_state, w_exp, preferred_element_type=jnp.float32).reshape(
        length, heads, NOPE + VDIM
    )
    key_nope = expanded[:, :, :NOPE]
    values = expanded[:, :, NOPE:].astype(jnp.bfloat16)
    query_rope = rotary_angles(query[:, :, NOPE:])
    scores = jnp.einsum("qhd,khd->hqk", query[:, :, :NOPE], key_nope) + jnp.einsum(
        "qhd,kd->hqk", query_rope, rotary_key_part
    )
    scores = scores * (NOPE + ROPE) ** (-0.5)
    causal = jnp.arange(length)[:, None] >= jnp.arange(length)[None, :]
    scores = jnp.where(causal[None], scores, -1e30)
    weights = jax.nn.softmax(scores, axis=-1).astype(jnp.bfloat16)
    mixed = jnp.einsum("hqk,khd->qhd", weights.astype(jnp.float32), values.astype(jnp.float32))
    mixed = mixed.astype(jnp.bfloat16).reshape(length, heads * VDIM)
    return jnp.dot(mixed, w_out, preferred_element_type=jnp.float32)


def plain_shards(saved, top_grad, gain, w_query, w_latent, compressed_gain, expand_weight, w_output):
    gathered = (
        lax.all_gather(gain, "dp", axis=1, tiled=True),
        lax.all_gather(w_query, "dp", axis=1, tiled=True),
        lax.all_gather(w_latent, "dp", axis=1, tiled=True),
        lax.all_gather(compressed_gain, "dp", axis=1, tiled=True),
        lax.all_gather(expand_weight, "dp", axis=1, tiled=True),
        lax.all_gather(w_output, "dp", axis=2, tiled=True),
    )
    gain32 = gathered[0][0].astype(jnp.float32)
    query_all = gathered[1][0]
    latent_all = gathered[2][0]
    lgain32 = gathered[3][0].astype(jnp.float32)
    expand_all = gathered[4][0]
    output_all = gathered[5][0]
    sections = lax.axis_size("pipe")
    section_index = lax.axis_index("pipe")
    tensor_count = lax.axis_size("tensor")
    tensor_rank = lax.axis_index("tensor")
    micro_count = saved.shape[1]
    length = saved.shape[2]
    width = saved.shape[3]
    share = length // tensor_count

    def compute(normed, upstream):
        _, pull = jax.vjp(lambda value: branch(value, query_all, latent_all, lgain32, expand_all, output_all), normed)
        return pull(upstream.astype(jnp.float32))[0]

    def skip(normed, upstream):
        return jnp.zeros_like(normed)

    gain_total = jnp.zeros((width,), jnp.float32)
    results = jnp.zeros((micro_count, share, width), jnp.bfloat16)
    stored = jnp.zeros((micro_count, length, width), jnp.bfloat16)
    received = jnp.zeros((length, width), jnp.bfloat16)
    for tick in range(sections + micro_count - 1):
        micro = tick - (sections - 1 - section_index)
        active = jnp.logical_and(micro >= 0, micro < micro_count)
        picked = jnp.clip(micro, 0, micro_count - 1)
        x_rows = lax.dynamic_index_in_dim(saved[0], picked, 0, keepdims=False)
        top_rows = lax.dynamic_index_in_dim(top_grad, picked, 0, keepdims=False)
        arrived = received
        upstream = jnp.where(section_index == sections - 1, top_rows, arrived)
        x_float = x_rows.astype(jnp.float32)
        normed, norm_pull = jax.vjp(root_mean_scale, x_float, gain32)
        branch_grad = lax.cond(active, compute, skip, normed, upstream)
        d_normed = lax.psum(branch_grad.astype(jnp.bfloat16), "tensor").astype(jnp.float32)
        dx_norm, d_gain = norm_pull(d_normed)
        dx = (upstream.astype(jnp.float32) + dx_norm).astype(jnp.bfloat16)
        gain_total = gain_total + jnp.where(active, d_gain, 0.0)
        mine = lax.dynamic_slice_in_dim(dx, tensor_rank * share, share, 0)
        chosen = (jnp.arange(micro_count) == micro)[:, None, None]
        results = jnp.where(chosen, mine[None], results)
        stored = jnp.where(chosen, upstream[None], stored)
        received = passed_along(dx, "pipe", -1)
    totals = (
        jnp.zeros(query_all.shape, jnp.float32),
        jnp.zeros(latent_all.shape, jnp.float32),
        jnp.zeros(lgain32.shape, jnp.float32),
        jnp.zeros(expand_all.shape, jnp.float32),
        jnp.zeros(output_all.shape, jnp.float32),
    )
    for micro_index in range(micro_count):
        normed_again = root_mean_scale(saved[0, micro_index].astype(jnp.float32), gain32)
        _, weight_pull = jax.vjp(
            lambda w_q, w_lat, lat_gain, w_exp, w_out: branch(
                normed_again, w_q, w_lat, lat_gain, w_exp, w_out
            ),
            query_all,
            latent_all,
            lgain32,
            expand_all,
            output_all,
        )
        cotangents = weight_pull(stored[micro_index].astype(jnp.float32))
        totals = tuple(
            (total + piece.astype(jnp.float32) for total, piece in zip(totals, cotangents))
        )
    gain_part = jnp.where(tensor_rank == 0, gain_total, 0.0)
    grad_q, grad_lat, grad_lg, grad_e, grad_o = totals
    out_q, part_lat, part_lg, out_e, out_o, part_gain = (
        lax.psum_scatter(grad_q.astype(jnp.bfloat16), "dp", scatter_dimension=0, tiled=True).astype(
            jnp.float32
        ),
        lax.psum_scatter(
            grad_lat.astype(jnp.bfloat16), "dp", scatter_dimension=0, tiled=True
        ).astype(jnp.float32),
        lax.psum_scatter(
            grad_lg.astype(jnp.bfloat16), "dp", scatter_dimension=0, tiled=True
        ).astype(jnp.float32),
        lax.psum_scatter(grad_e.astype(jnp.bfloat16), "dp", scatter_dimension=0, tiled=True).astype(
            jnp.float32
        ),
        lax.psum_scatter(grad_o.astype(jnp.bfloat16), "dp", scatter_dimension=1, tiled=True).astype(
            jnp.float32
        ),
        lax.psum_scatter(
            gain_part.astype(jnp.bfloat16), "dp", scatter_dimension=0, tiled=True
        ).astype(jnp.float32),
    )
    out_lat, out_lg, out_gain = (
        lax.psum(part_lat.astype(jnp.bfloat16), "tensor").astype(jnp.float32),
        lax.psum(part_lg.astype(jnp.bfloat16), "tensor").astype(jnp.float32),
        lax.psum(part_gain.astype(jnp.bfloat16), "tensor").astype(jnp.float32),
    )
    return (
        results[None],
        out_gain[None],
        out_q[None],
        out_lat[None],
        out_lg[None],
        out_e[None],
        out_o[None],
    )


F32 = jnp.float32
BF16 = jnp.bfloat16


def mm(a, b):
    return lax.dot_general(a, b, (((1,), (0,)), ((), ())), preferred_element_type=F32)


def mm_nt(a, b):
    return lax.dot_general(a, b, (((1,), (1,)), ((), ())), preferred_element_type=F32)


def mm_tn(a, b):
    return lax.dot_general(a, b, (((0,), (0,)), ((), ())), preferred_element_type=F32)


def turned(values):
    half = values.shape[1] // 2
    return jnp.concatenate([values[:, half:], values[:, :half]], axis=1)


def rotate(values, cosine, sine):
    return values * cosine + turned(values) * sine


def rotate_back(values, cosine, sine):
    return values * cosine - turned(values) * sine


class Plan:
    def __init__(self, saved, w_query, w_latent, expand_weight, n_pipe, n_dp, n_tensor):
        self.n_pipe, self.n, self.nt = n_pipe, n_dp, n_tensor
        self.micro, self.length, self.width = saved.shape[1:]
        self.rows = self.micro * self.length
        self.share = self.length // n_tensor
        self.heads = w_query.shape[2] // (NOPE + ROPE)
        self.rank = expand_weight.shape[1] * n_dp
        self.latent = w_latent.shape[2]
        self.wcol = self.width // n_dp
        self.ccol = self.rank // n_dp
        self.qcol = self.heads * (NOPE + ROPE)
        self.hcol = self.heads * VDIM
        self.rope_all = self.heads * ROPE
        self.o_mixed = 0
        self.o_q = self.o_mixed + self.hcol
        self.o_kn = self.o_q + self.qcol
        self.o_kr = self.o_kn + self.heads * NOPE
        self.pay = self.o_kr + ROPE
        self.o_dv = self.heads * self.length
        self.o_up = self.o_dv + self.hcol
        self.tail = self.o_up
        self.own = self.micro * self.share
        self.half = self.rows // 2
        self.spare = -self.latent % 128
        self.lrow = self.rank // max(self.spare, 1)
        self.grow = self.width // max(self.spare, 1)
        self.chunk = self.width + self.latent + self.spare

    def fits(self):
        aligned = self.wcol % 256 == 0 and self.ccol % 128 == 0 and self.rope_all % 128 == 0
        whole = (self.heads * self.length) % 128 == 0 and self.latent % 32 == 0
        if self.spare == 0 or self.rank % self.spare or self.wcol % self.spare:
            return False
        room = 2 * (self.lrow + self.grow) <= self.half
        few = self.n & (self.n - 1) == 0 and self.rows <= 512
        return aligned and whole and room and few and self.nt % 2 == 0 and self.share % 16 == 0


def share_rows(plan, core):
    at = 0
    for chip in range(plan.nt // 2):
        for m in range(plan.micro):
            start = m * plan.length + (2 * chip + core) * plan.share
            yield pl.multiple_of(start, plan.share), slice(at, at + plan.share)
            at += plan.share


def assemble_latent(plan, core, lat_own, lat_other, w_s):
    part = plan.latent // 2
    for k in range(plan.n):
        w_s[k, pl.ds(pl.multiple_of(core * part, 16), part), :] = lat_own[k][...]
        w_s[k, pl.ds(pl.multiple_of((1 - core) * part, 16), part), :] = lat_other[k][...]


def forward_body(plan, ranks, x, gains, wq, lat_own, lat_other, wexp, cosine, sine, outs):
    (sent, pay, v_ref, p_ref, chat_ref, rc_ref, gain_ref, cgain_ref, x_own, wlat, g_s, cg_s, n_s, c_s) = outs
    n = plan.n
    j, t = ranks[0], ranks[1]
    core = lax.rem(t, 2)
    assemble_latent(plan, core, lat_own, lat_other, wlat)
    for k in range(n):
        src = j ^ k
        g_s[src] = gains[k][:, : plan.wcol].astype(F32)
        cg_s[src] = gains[k][:, plan.wcol :].astype(F32)
    xf = x[...].astype(F32)
    scale = lax.rsqrt(jnp.mean(xf * xf, axis=1, keepdims=True) + EPS)
    for b in range(n):
        block = xf[:, b * plan.wcol : (b + 1) * plan.wcol] * scale * g_s[b]
        rounded = block.astype(BF16)
        n_s[b] = rounded
        gain_ref[:, b * plan.wcol : (b + 1) * plan.wcol] = g_s[b]
        cgain_ref[:, b * plan.ccol : (b + 1) * plan.ccol] = cg_s[b]
    query = jnp.zeros((plan.rows, plan.qcol), F32)
    latent = jnp.zeros((plan.rows, plan.latent), F32)
    for k in range(n):
        query = query + mm(n_s[j ^ k], wq[k][...])
        latent = latent + mm_nt(n_s[j ^ k], wlat[k])
    low = latent[:, : plan.rank]
    rc = lax.rsqrt(jnp.mean(low * low, axis=1, keepdims=True) + EPS)
    chat = low * rc
    chat_ref[...] = chat
    rc_ref[...] = rc
    comp = (chat * cgain_ref[...]).astype(BF16)
    for b in range(n):
        c_s[b] = comp[:, b * plan.ccol : (b + 1) * plan.ccol]
    expanded = jnp.zeros((plan.rows, plan.heads * (NOPE + VDIM)), F32)
    for k in range(n):
        expanded = expanded + mm(c_s[j ^ k], wexp[k][...])
    cos, sin = cosine[...], sine[...]
    kr = rotate(latent[:, plan.rank :], cos, sin).astype(BF16)
    row = lax.broadcasted_iota(jnp.int32, (plan.rows, plan.rows), 0)
    col = lax.broadcasted_iota(jnp.int32, (plan.rows, plan.rows), 1)
    keep = row >= col
    for m in range(1, plan.micro):
        keep = keep & ((row < m * plan.length) | (col >= m * plan.length))
    qn_all, qr_all, kn_all, mixed_all = [], [], [], []
    for h in range(plan.heads):
        q_at = h * (NOPE + ROPE)
        e_at = h * (NOPE + VDIM)
        qn = query[:, q_at : q_at + NOPE].astype(BF16)
        qr = rotate(query[:, q_at + NOPE : q_at + NOPE + ROPE], cos, sin).astype(BF16)
        kn = expanded[:, e_at : e_at + NOPE].astype(BF16)
        v = expanded[:, e_at + NOPE : e_at + NOPE + VDIM].astype(BF16)
        scores = (mm_nt(qn, kn) + mm_nt(qr, kr)) * (NOPE + ROPE) ** (-0.5)
        scores = jnp.where(keep, scores, -1e30)
        top = jnp.max(scores, axis=1, keepdims=True)
        e = jnp.exp(scores - top)
        p = e / jnp.sum(e, axis=1, keepdims=True)
        p_ref[h] = p
        mixed = mm(p.astype(BF16), v).astype(BF16)
        v_ref[:, h * VDIM : (h + 1) * VDIM] = v
        qn_all.append(qn)
        qr_all.append(qr)
        kn_all.append(kn)
        mixed_all.append(mixed)
    qr_cat = jnp.concatenate(qr_all, axis=1)
    for k in range(n):
        sent[k][:, : plan.wcol] = n_s[j ^ k]
        sent[k][:, plan.wcol :] = c_s[j ^ k]
    for h in range(plan.heads):
        pay[:, plan.o_mixed + h * VDIM : plan.o_mixed + (h + 1) * VDIM] = mixed_all[h]
        pay[:, plan.o_q + h * NOPE : plan.o_q + (h + 1) * NOPE] = qn_all[h]
        pay[:, plan.o_kn + h * NOPE : plan.o_kn + (h + 1) * NOPE] = kn_all[h]
    pay[:, plan.o_q + plan.heads * NOPE : plan.o_kn] = qr_cat
    pay[:, plan.o_kr :] = kr
    for start, at in share_rows(plan, core):
        x_own[at, :] = x[pl.ds(start, plan.share), :]


def key_parts(plan, pay, h):
    qn = pay[:, plan.o_q + h * NOPE : plan.o_q + (h + 1) * NOPE]
    kn = pay[:, plan.o_kn + h * NOPE : plan.o_kn + (h + 1) * NOPE]
    qr = pay[:, plan.o_q + plan.heads * NOPE : plan.o_kn][:, h * ROPE : (h + 1) * ROPE]
    return qn, kn, qr, pay[:, plan.o_kr :]


def query_cotangent(ds, kn, kr, cos, sin):
    return [mm(ds, kn).astype(BF16), rotate_back(mm(ds, kr), cos, sin).astype(BF16)]


def backward_body(plan, last, ranks, top, pieces, pay, v_ref, p_ref, chat_ref, rc_ref, cgain_ref,
                  wq, wlat, wexp, wout, cosine, sine, outs):
    chunks, up_own, tail, ups, up_s, u_s, d_s, dn_s, dl_s = outs
    n = plan.n
    j, t, is_top = ranks[0], ranks[1], ranks[2]
    core = lax.rem(t, 2)
    if pieces:
        @pl.when(is_top == 1)
        def _():
            up_s[...] = top[...]

        @pl.when(is_top == 0)
        def _():
            for piece, side in zip(pieces, (core, 1 - core)):
                for start, at in share_rows(plan, side):
                    up_s[pl.ds(start, plan.share), :] = piece[at, :]

        up_ref = up_s
    else:
        up_ref = top
    for start, at in share_rows(plan, core):
        up_own[at, :] = up_ref[pl.ds(start, plan.share), :]
    for b in range(n):
        u_s[b] = up_ref[:, b * plan.wcol : (b + 1) * plan.wcol]
    dmixed = jnp.zeros((plan.rows, plan.hcol), F32)
    for k in range(n):
        dmixed = dmixed + mm_nt(u_s[j ^ k], wout[k][...])
    dmixed = dmixed.astype(BF16)
    cos, sin = cosine[...], sine[...]
    dq, dexp, dvs, dss = [], [], [], []
    dkr = jnp.zeros((plan.rows, ROPE), F32)
    scale = (NOPE + ROPE) ** (-0.5)
    for h in range(plan.heads):
        qn, kn, qr, kr = key_parts(plan, pay, h)
        v = v_ref[:, h * VDIM : (h + 1) * VDIM]
        p = p_ref[h]
        dm = dmixed[:, h * VDIM : (h + 1) * VDIM]
        dp = mm_nt(dm, v)
        ds = (p * (dp - jnp.sum(dp * p, axis=1, keepdims=True)) * scale).astype(BF16)
        dv = mm_tn(p.astype(BF16), dm).astype(BF16)
        dq.extend(query_cotangent(ds, kn, kr, cos, sin))
        dkr = dkr + mm_tn(ds, qr)
        dexp.extend([mm_tn(ds, qn).astype(BF16), dv])
        dvs.append(dv)
        dss.append(ds)
    dq = jnp.concatenate(dq, axis=1)
    dexp = jnp.concatenate(dexp, axis=1)
    for k in range(n):
        d_s[j ^ k] = mm_nt(dexp, wexp[k][...])
    dcomp = jnp.concatenate([d_s[b] for b in range(n)], axis=1)
    chat = chat_ref[...]
    dchat = dcomp * cgain_ref[...]
    dlow = rc_ref[...] * (dchat - chat * jnp.mean(dchat * chat, axis=1, keepdims=True))
    dlatent = jnp.concatenate([dlow, rotate_back(dkr, cos, sin)], axis=1).astype(BF16)
    for k in range(n):
        dn_s[j ^ k] = (mm_nt(dq, wq[k][...]) + mm(dlatent, wlat[k])).astype(BF16)
    if last:
        dl_s[:, : plan.latent] = dlatent
        dl_s[:, plan.latent :] = jnp.zeros((plan.rows, plan.spare), BF16)
    for chunk, side in zip(chunks, (core, 1 - core)):
        for start, at in share_rows(plan, side):
            for b in range(n):
                chunk[at, b * plan.wcol : (b + 1) * plan.wcol] = dn_s[b, pl.ds(start, plan.share), :]
            if last:
                chunk[at, plan.width :] = dl_s[pl.ds(start, plan.share), :]
        if last:
            put_split(plan, chunk, plan.width + plan.latent, 0, jnp.sum(dcomp * chat, axis=0, keepdims=True))
    if last:
        small = []
        for ds in dss:
            rows = [
                ds[m * plan.length : (m + 1) * plan.length, m * plan.length : (m + 1) * plan.length]
                for m in range(plan.micro)
            ]
            small.append(jnp.concatenate(rows, axis=0))
        ds_cat = jnp.concatenate(small, axis=1)
        tail[:, : plan.o_dv] = ds_cat
        for h in range(plan.heads):
            tail[:, plan.o_dv + h * VDIM : plan.o_dv + (h + 1) * VDIM] = dvs[h]
        for k in range(n):
            ups[k][...] = u_s[j ^ k]


def put_split(plan, ref, col, row, values):
    count = values.shape[1] // plan.spare
    high = values.astype(BF16)
    low = (values - high.astype(F32)).astype(BF16)
    for i in range(count):
        piece = slice(i * plan.spare, (i + 1) * plan.spare)
        ref[row + i : row + i + 1, col : col + plan.spare] = high[:, piece]
        ref[row + count + i : row + count + i + 1, col : col + plan.spare] = low[:, piece]


def norm_body(plan, last, ranks, pieces, up_own, x_own, gain_ref, dx_ref, dl_ref, dx_s):
    total = pieces[0][...].astype(F32)
    for piece in pieces[1:]:
        total = total + piece[...].astype(F32)
    dn = total[:, : plan.width]
    x = x_own[...].astype(F32)
    scale = lax.rsqrt(jnp.mean(x * x, axis=1, keepdims=True) + EPS)
    xhat = x * scale
    dhat = dn * gain_ref[...]
    dx = scale * (dhat - xhat * jnp.mean(dhat * xhat, axis=1, keepdims=True))
    dx = (up_own[...].astype(F32) + dx).astype(BF16)
    if not last:
        dx_ref[...] = dx
        return
    dx_s[...] = dx
    at = pl.multiple_of(lax.div(ranks[1], 2) * plan.own, plan.own)
    dx_ref[...] = dx_s[pl.ds(at, plan.own), :]
    rest = total[:, plan.width :]
    dl_ref[...] = rest.astype(BF16)
    lgain = rest[: plan.lrow, plan.latent :] + rest[plan.lrow : 2 * plan.lrow, plan.latent :]
    high = lgain.astype(BF16)
    dl_ref[: plan.lrow, plan.latent :] = high
    dl_ref[plan.lrow : 2 * plan.lrow, plan.latent :] = (lgain - high.astype(F32)).astype(BF16)
    put_split(plan, dl_ref, plan.latent, 2 * plan.lrow, jnp.sum(dn * xhat, axis=0, keepdims=True))


def gradient_body(plan, sent, pays, tails, ups, cosine, sine, outs):
    g_q, g_exp, g_out, a_n, a_c, a_m, a_u, a_dq, a_de = outs
    cos, sin = cosine[...], sine[...]
    for k in range(plan.n):
        at = slice(k * plan.rows, (k + 1) * plan.rows)
        pay, tail = pays[k], tails[k]
        a_n[at, :] = sent[k][:, : plan.wcol]
        a_c[at, :] = sent[k][:, plan.wcol :]
        a_m[at, :] = pay[:, plan.o_mixed : plan.o_q]
        a_u[at, :] = ups[k][...]
        for h in range(plan.heads):
            qn, kn, _, kr = key_parts(plan, pay, h)
            for m in range(plan.micro):
                part = slice(m * plan.length, (m + 1) * plan.length)
                rows = slice(k * plan.rows + m * plan.length, k * plan.rows + (m + 1) * plan.length)
                ds = tail[part, : plan.o_dv][:, h * plan.length : (h + 1) * plan.length]
                dqn, dqr = query_cotangent(ds, kn[part], kr[part], cos[part], sin[part])
                q_at = h * (NOPE + ROPE)
                a_dq[rows, q_at : q_at + NOPE] = dqn
                a_dq[rows, q_at + NOPE : q_at + NOPE + ROPE] = dqr
                e_at = h * (NOPE + VDIM)
                a_de[rows, e_at : e_at + NOPE] = mm_tn(ds, qn[part]).astype(BF16)
                a_de[rows, e_at + NOPE : e_at + NOPE + VDIM] = tail[part, plan.o_dv + h * VDIM : plan.o_dv + (h + 1) * VDIM]
    g_q[...] = mm_tn(a_n[...], a_dq[...])
    g_exp[...] = mm_tn(a_c[...], a_de[...])
    g_out[...] = mm_tn(a_m[...], a_u[...])


def latent_gradient_body(plan, ranks, sent, dl_own, dl_other, outs):
    g_gain, g_lat, g_lg, a_n, a_dl, m_s, l_s = outs
    n = plan.n
    j, t = ranks[0], ranks[1]
    core = lax.rem(t, 2)
    lgain = jnp.zeros((plan.lrow, plan.spare), F32)
    ggain = jnp.zeros((plan.grow, plan.spare), F32)
    for k in range(n):
        a_n[k * plan.rows : (k + 1) * plan.rows, :] = sent[k][:, : plan.wcol]
        for block, side in ((dl_own[k], core), (dl_other[k], 1 - core)):
            for start, part in share_rows(plan, side):
                a_dl[pl.ds(pl.multiple_of(k * plan.rows + start, plan.share), plan.share), :] = block[part, : plan.latent]
            extra = block[:, plan.latent :].astype(F32)
            if side is core:
                lgain = lgain + extra[: plan.lrow] + extra[plan.lrow : 2 * plan.lrow]
            at_gain = 2 * plan.lrow
            ggain = ggain + extra[at_gain : at_gain + plan.grow] + extra[at_gain + plan.grow : at_gain + 2 * plan.grow]
    wide, low = plan.wcol // plan.spare, plan.ccol // plan.spare
    for b in range(n):
        for i in range(wide):
            m_s[b, :, i * plan.spare : (i + 1) * plan.spare] = ggain[b * wide + i : b * wide + i + 1, :]
        for i in range(low):
            l_s[b, :, i * plan.spare : (i + 1) * plan.spare] = lgain[b * low + i : b * low + i + 1, :]
    g_gain[...] = m_s[j]
    g_lg[...] = l_s[j]
    g_lat[...] = mm_tn(a_dl[...], a_n[...])


def grouped(counts_in, refs):
    out, at = [], 0
    for count in counts_in:
        if count is None:
            out.append(refs[at])
            at += 1
        else:
            out.append(list(refs[at : at + count]))
            at += count
    return out


def kernel_call(body, groups, out_groups, scratch, flops):
    def flat(items):
        return [leaf for item in items for leaf in (item if isinstance(item, list) else [item])]

    counts = [len(g) if isinstance(g, list) else None for g in groups + out_groups] + [None] * len(scratch)

    def kernel(*refs):
        body(*grouped(counts, refs))

    outs = flat(out_groups)
    vmem = pl.BlockSpec(memory_space=pltpu.VMEM)
    ins = flat(groups)
    call = pl.pallas_call(
        kernel,
        in_specs=[pl.BlockSpec(memory_space=pltpu.SMEM)] + [vmem] * (len(ins) - 1),
        out_specs=[vmem] * len(outs),
        out_shape=outs,
        scratch_shapes=scratch,
        compiler_params=pltpu.CompilerParams(vmem_limit_bytes=20 << 20),
        cost_estimate=pl.CostEstimate(flops=flops, bytes_accessed=4 << 20, transcendentals=0),
    )
    got = call(*ins)
    result, at = [], 0
    for g in out_groups:
        if isinstance(g, list):
            result.append(list(got[at : at + len(g)]))
            at += len(g)
        else:
            result.append(got[at])
            at += 1
    return result


def flipped(value, axis, count, bit):
    return lax.ppermute(value, axis, [(i, i ^ bit) for i in range(count)])


def gathered(value, axis, count):
    blocks = {0: value}
    bit = count // 2
    while bit:
        found = sorted(blocks)
        blocks.update({k | bit: flipped(blocks[k], axis, count, bit) for k in found})
        bit //= 2
    return [blocks[k] for k in range(count)]


def handed(values, axis, count):
    return [values[0]] + [flipped(values[k], axis, count, k) for k in range(1, count)]


def token_shards(plan, saved, top_grad, gain, w_query, w_latent, compressed_gain, expand_weight, w_output):
    n, nt, rows = plan.n, plan.nt, plan.rows
    j = lax.axis_index("dp")
    t = lax.axis_index("tensor")
    section = lax.axis_index("pipe")
    is_top = (section == plan.n_pipe - 1).astype(jnp.int32)
    ranks = jnp.stack([j, t, is_top]).astype(jnp.int32)
    part = plan.latent // 2
    half_rows = lax.dynamic_slice_in_dim(w_latent[0].T, lax.rem(t, 2) * part, part, 0)
    gains = gathered(jnp.concatenate([gain, compressed_gain], axis=1), "dp", n)
    lat_own = gathered(half_rows, "dp", n)
    lat_other = [flipped(block, "tensor", nt, 1) for block in lat_own]
    wq = gathered(w_query[0], "dp", n)
    wexp = gathered(expand_weight[0], "dp", n)
    wout = gathered(w_output[0], "dp", n)
    x = saved[0].reshape(rows, plan.width)
    top = top_grad.reshape(rows, plan.width)
    freq = 10000.0 ** (-np.arange(ROPE // 2) / (ROPE // 2))
    angle = np.tile(np.arange(plan.length)[:, None] * freq[None, :], (plan.micro, 1))
    cosine = jnp.asarray(np.concatenate([np.cos(angle), np.cos(angle)], axis=1), F32)
    sine = jnp.asarray(np.concatenate([-np.sin(angle), np.sin(angle)], axis=1), F32)

    def shape(dims, kind=BF16):
        return jax.ShapeDtypeStruct(dims, kind)

    def prepare(ranks, *refs):
        count = len(refs) // 2
        for source, target in zip(refs[:count], refs[count:]):
            target[...] = source[...]

    local = [x, top, wq[0], wexp[0], wout[0], cosine, sine]
    copied = kernel_call(prepare, [ranks] + local, [shape(v.shape, v.dtype) for v in local], [], 10**4)
    x, top, wq[0], wexp[0], wout[0], cosine, sine = copied

    def forward(ranks, x, gains, wq, lo, lt, we, cosine, sine, *outs):
        forward_body(plan, ranks, x, gains, wq, lo, lt, we, cosine, sine, outs)

    sent, pay, v, p, chat, rc, gain32, cgain32, x_own, wlat = kernel_call(
        forward,
        [ranks, x, gains, wq, lat_own, lat_other, wexp, cosine, sine],
        [
            [shape((rows, plan.wcol + plan.ccol))] * n,
            shape((rows, plan.pay)),
            shape((rows, plan.hcol)),
            shape((plan.heads, rows, rows), F32),
            shape((rows, plan.rank), F32),
            shape((rows, 1), F32),
            shape((1, plan.width), F32),
            shape((1, plan.rank), F32),
            shape((plan.half, plan.width)),
            shape((n, plan.latent, plan.wcol)),
        ],
        [
            pltpu.VMEM((n, 1, plan.wcol), F32),
            pltpu.VMEM((n, 1, plan.ccol), F32),
            pltpu.VMEM((n, rows, plan.wcol), BF16),
            pltpu.VMEM((n, rows, plan.ccol), BF16),
        ],
        5 * 10**8,
    )
    pieces = []
    for tick in range(plan.n_pipe):
        last = tick == plan.n_pipe - 1

        def backward(ranks, top, pieces, pay, v, p, chat, rc, cg, wq, wl, we, wo, cosine, sine, *outs):
            outs = list(outs)
            if not last:
                outs[2:2] = [None, None]
            backward_body(plan, last, ranks, top, pieces, pay, v, p, chat, rc, cg, wq, wl, we, wo, cosine, sine, outs)

        chunk = plan.chunk if last else plan.width
        out_groups = [[shape((plan.half, chunk))] * 2, shape((plan.half, plan.width))]
        if last:
            out_groups += [shape((rows, plan.tail)), [shape((rows, plan.wcol))] * n]
        got = kernel_call(
            backward,
            [ranks, top, pieces, pay, v, p, chat, rc, cgain32, wq, wlat, wexp, wout, cosine, sine],
            out_groups,
            [
                pltpu.VMEM((rows, plan.width), BF16),
                pltpu.VMEM((n, rows, plan.wcol), BF16),
                pltpu.VMEM((n, rows, plan.ccol), F32),
                pltpu.VMEM((n, rows, plan.wcol), BF16),
                pltpu.VMEM((rows, plan.latent + plan.spare), BF16),
            ],
            10**9,
        )
        (kept, given), up_own = got[0], got[1]
        chip = kept + flipped(given, "tensor", nt, 1)
        sums = [chip]
        for k in range(1, nt // 2):
            pairs = [(i, (i + 2 * k) % nt) for i in range(nt)]
            sums.append(lax.ppermute(chip, "tensor", pairs))
        norm_out = [shape((plan.own if last else plan.half, plan.width))]
        if last:
            tail, ups = got[2], got[3]
            norm_out.append(shape((plan.half, plan.latent + plan.spare)))

        def norm(ranks, sums, up_own, x_own, gain32, *rest):
            dx, dl, dx_s = rest if last else (rest[0], None, rest[1])
            norm_body(plan, last, ranks, sums, up_own, x_own, gain32, dx, dl, dx_s)

        got = kernel_call(
            norm, [ranks, sums, up_own, x_own, gain32], norm_out, [pltpu.VMEM((plan.half, plan.width), BF16)], 10**6
        )
        dx = got[0]
        if not last:
            below = lax.ppermute(dx, "pipe", [(s, s - 1) for s in range(1, plan.n_pipe)])
            pieces = [below, flipped(below, "tensor", nt, 1)]
    dl_own = gathered(got[1], "dp", n)
    dl_other = [flipped(block, "tensor", nt, 1) for block in dl_own]
    sent = handed(sent, "dp", n)
    pays = gathered(pay, "dp", n)
    tails = gathered(tail, "dp", n)
    ups = handed(ups, "dp", n)

    def gradients(ranks, sent, pays, tails, ups, cosine, sine, *outs):
        gradient_body(plan, sent, pays, tails, ups, cosine, sine, outs)

    def latent_gradients(ranks, sent, dl_own, dl_other, *outs):
        latent_gradient_body(plan, ranks, sent, dl_own, dl_other, outs)

    every = n * rows
    g_q, g_exp, g_out = kernel_call(
        gradients,
        [ranks, sent, pays, tails, ups, cosine, sine],
        [
            shape((plan.wcol, plan.qcol), F32),
            shape((plan.ccol, plan.heads * (NOPE + VDIM)), F32),
            shape((plan.hcol, plan.wcol), F32),
        ],
        [
            pltpu.VMEM((every, plan.wcol), BF16),
            pltpu.VMEM((every, plan.ccol), BF16),
            pltpu.VMEM((every, plan.hcol), BF16),
            pltpu.VMEM((every, plan.wcol), BF16),
            pltpu.VMEM((every, plan.qcol), BF16),
            pltpu.VMEM((every, plan.heads * (NOPE + VDIM)), BF16),
        ],
        10**9,
    )
    g_gain, g_lat, g_lg = kernel_call(
        latent_gradients,
        [ranks, sent, dl_own, dl_other],
        [shape((1, plan.wcol), F32), shape((plan.latent, plan.wcol), F32), shape((1, plan.ccol), F32)],
        [
            pltpu.VMEM((every, plan.wcol), BF16),
            pltpu.VMEM((every, plan.latent), BF16),
            pltpu.VMEM((n, 1, plan.wcol), F32),
            pltpu.VMEM((n, 1, plan.ccol), F32),
        ],
        10**9,
    )
    results = dx.reshape(plan.micro, plan.share, plan.width)
    return results[None], g_gain, g_q[None], g_lat.T[None], g_lg, g_exp[None], g_out[None]


def shards(saved, top_grad, gain, w_query, w_latent, compressed_gain, expand_weight, w_output):
    args = (saved, top_grad, gain, w_query, w_latent, compressed_gain, expand_weight, w_output)
    sizes = [lax.axis_size(axis) for axis in ("pipe", "dp", "tensor")]
    plan = Plan(saved, w_query, w_latent, expand_weight, *sizes)
    if plan.fits():
        return token_shards(plan, *args)
    return plain_shards(*args)


def solution(mesh):
    in_specs = (
        P("pipe", None, "dp", None),
        P(None, "dp", None),
        P("pipe", "dp"),
        P("pipe", "dp", "tensor"),
        P("pipe", "dp", None),
        P("pipe", "dp"),
        P("pipe", "dp", "tensor"),
        P("pipe", "tensor", "dp"),
    )
    out_specs = (
        P("pipe", None, ("dp", "tensor"), None),
        P("pipe", "dp"),
        P("pipe", "dp", "tensor"),
        P("pipe", "dp", None),
        P("pipe", "dp"),
        P("pipe", "dp", "tensor"),
        P("pipe", "tensor", "dp"),
    )
    return jax.shard_map(shards, mesh=mesh, in_specs=in_specs, out_specs=out_specs, check_vma=False)
```

profile of v0, /device:TPU:0, one launch (start us, length us, event | category | flops | bytes accessed | tf_op | source)
XLA Modules:
  0.0 137.6 jit_solution(5908498927855180767)
XLA Ops:
  0.6 4.1 %collective-permute-start.14 = (bf16[128,512]{1,0:T(8,128)(2,1)}, bf16[128,512]{1,0:T(8,128)(2,1)S(1)}, u32[]{:S(2)}, u32[]{:S(2)}) collective-permute-start(bf16[128,512]{1,0:T(8,128)(2,1)} %bitcast.24), channel_id=1, source_target_pairs={{0,8},{4,12},{8,0},{12,4},{1,9},{5,13},{9,1},{13,5},{2,10},{6,14},... | collective-permute-start | bytes 393224 | tf_op jit(solution)/shard_map/ppermute | solution.py:580
  4.8 1.6 %collective-permute-start.13 = (bf16[128,512]{1,0:T(8,128)(2,1)}, bf16[128,512]{1,0:T(8,128)(2,1)S(1)}, u32[]{:S(2)}, u32[]{:S(2)}) collective-permute-start(bf16[128,512]{1,0:T(8,128)(2,1)} %bitcast.25), channel_id=1, source_target_pairs={{0,4},{4,0},{8,12},{12,8},{1,5},{5,1},{9,13},{13,9},{2,6},{6,2},{1... | collective-permute-start | bytes 393224 | tf_op jit(solution)/shard_map/ppermute | solution.py:580
  6.4 0.4 collective-permute-start.7
  6.8 2.6 %collective-permute-start.17 = (bf16[256,256]{1,0:T(8,128)(2,1)}, bf16[256,256]{1,0:T(8,128)(2,1)S(1)}, u32[]{:S(2)}, u32[]{:S(2)}) collective-permute-start(bf16[256,256]{1,0:T(8,128)(2,1)} %bitcast.27), channel_id=1, source_target_pairs={{0,8},{4,12},{8,0},{12,4},{1,9},{5,13},{9,1},{13,5},{2,10},{6,14},... | collective-permute-start | bytes 393224 | tf_op jit(solution)/shard_map/ppermute | solution.py:580
  9.4 0.7 constant_dynamic-update-slice_fusion.1
  10.0 0.7 constant_dynamic-update-slice_fusion.refs_2_
  10.7 0.3 collective-permute-start.1
  11.0 12.3 %collective-permute-done.1.refs_4_ = bf16[1,384]{1,0:T(2,128)(2,1)S(1)} collective-permute-done((bf16[1,384]{1,0:T(2,128)(2,1)S(1)}, bf16[1,384]{1,0:T(2,128)(2,1)S(1)}, u32[]{:S(2)}, u32[]{:S(2)}) %collective-permute-start.1) | collective-permute-done | bytes 800 | tf_op jit(solution)/shard_map/ppermute | solution.py:580
  23.3 0.8 collective-permute-start
  24.1 2.8 %collective-permute-done.refs_3_ = bf16[1,384]{1,0:T(2,128)(2,1)S(1)} collective-permute-done((bf16[1,384]{1,0:T(2,128)(2,1)S(1)}, bf16[1,384]{1,0:T(2,128)(2,1)S(1)}, u32[]{:S(2)}, u32[]{:S(2)}) %collective-permute-start) | collective-permute-done | bytes 800 | tf_op jit(solution)/shard_map/ppermute | solution.py:580
  26.9 0.8 collective-permute-start.2
  27.7 2.8 %collective-permute-done.2.refs_5_ = bf16[1,384]{1,0:T(2,128)(2,1)S(1)} collective-permute-done((bf16[1,384]{1,0:T(2,128)(2,1)S(1)}, bf16[1,384]{1,0:T(2,128)(2,1)S(1)}, u32[]{:S(2)}, u32[]{:S(2)}) %collective-permute-start.2) | collective-permute-done | bytes 800 | tf_op jit(solution)/shard_map/ppermute | solution.py:580
  30.5 0.8 collective-permute-start.6
  31.3 3.3 %collective-permute-start.4 = (bf16[256,384]{1,0:T(8,128)(2,1)}, bf16[256,384]{1,0:T(8,128)(2,1)S(1)}, u32[]{:S(2)}, u32[]{:S(2)}) collective-permute-start(bf16[256,384]{1,0:T(8,128)(2,1)} %bitcast.21), channel_id=1, source_target_pairs={{0,8},{4,12},{8,0},{12,4},{1,9},{5,13},{9,1},{13,5},{2,10},{6,14},... | collective-permute-start | bytes 589832 | tf_op jit(solution)/shard_map/ppermute | solution.py:580
  34.7 2.0 %collective-permute-start.8 = (bf16[288,256]{1,0:T(8,128)(2,1)S(1)}, bf16[288,256]{1,0:T(8,128)(2,1)S(1)}, u32[]{:S(2)}, u32[]{:S(2)}) collective-permute-start(bf16[288,256]{1,0:T(8,128)(2,1)S(1)} %collective-permute-done.7.refs_12_), channel_id=1, source_target_pairs={{0,4},{4,0},{8,12},{12,8},{1,5},{5,1},{9,13},{13,9},{2,6},{6,2},{1... | collective-permute-start | bytes 442376 | tf_op jit(solution)/shard_map/ppermute | solution.py:580
  36.7 1.3 collective-permute-start.15
  38.0 2.4 %collective-permute-done.4.refs_8_.refs_10_.refs_12_ = bf16[256,384]{1,0:T(8,128)(2,1)S(1)} collective-permute-done((bf16[256,384]{1,0:T(8,128)(2,1)}, bf16[256,384]{1,0:T(8,128)(2,1)S(1)}, u32[]{:S(2)}, u32[]{:S(2)}) %collective-permute-start.4) | collective-permute-done | bytes 196640 | tf_op jit(solution)/shard_map/ppermute | solution.py:580
  40.4 2.7 %collective-permute-start.5 = (bf16[256,384]{1,0:T(8,128)(2,1)S(1)}, bf16[256,384]{1,0:T(8,128)(2,1)S(1)}, u32[]{:S(2)}, u32[]{:S(2)}) collective-permute-start(bf16[256,384]{1,0:T(8,128)(2,1)S(1)} %collective-permute-done.4.refs_8_.refs_10_.refs_12_), channel_id=1, source_target_pairs={{0,4},{4,0},{8,12},{12,8},{1,5},{5,1},{9,13},{13,9},{2,6},{6,2},{1... | collective-permute-start | bytes 589832 | tf_op jit(solution)/shard_map/ppermute | solution.py:580
  43.1 1.3 collective-permute-done.3.refs_7_.refs_9_.refs_11_
  44.4 3.1 %collective-permute-done.8.refs_13_ = bf16[288,256]{1,0:T(8,128)(2,1)S(1)} collective-permute-done((bf16[288,256]{1,0:T(8,128)(2,1)S(1)}, bf16[288,256]{1,0:T(8,128)(2,1)S(1)}, u32[]{:S(2)}, u32[]{:S(2)}) %collective-permute-start.8) | collective-permute-done | bytes 147488 | tf_op jit(solution)/shard_map/ppermute | solution.py:580
  47.5 2.8 %collective-permute-done.15.refs_21_.refs_16_.refs_18_ = bf16[128,512]{1,0:T(8,128)(2,1)S(1)} collective-permute-done((bf16[128,512]{1,0:T(8,128)(2,1)S(1)}, bf16[128,512]{1,0:T(8,128)(2,1)S(1)}, u32[]{:S(2)}, u32[]{:S(2)}) %collective-permute-start.15) | collective-permute-done | bytes 131104 | tf_op jit(solution)/shard_map/ppermute | solution.py:580
  50.3 2.5 %collective-permute-start.16 = (bf16[256,256]{1,0:T(8,128)(2,1)}, bf16[256,256]{1,0:T(8,128)(2,1)S(1)}, u32[]{:S(2)}, u32[]{:S(2)}) collective-permute-start(bf16[256,256]{1,0:T(8,128)(2,1)} %bitcast.28), channel_id=1, source_target_pairs={{0,4},{4,0},{8,12},{12,8},{1,5},{5,1},{9,13},{13,9},{2,6},{6,2},{1... | collective-permute-start | bytes 393224 | tf_op jit(solution)/shard_map/ppermute | solution.py:580
  52.9 0.9 copy-done.1
  53.8 0.9 copy-done.2
  54.8 0.9 copy-done.3
  55.7 0.9 copy-done.4
  56.6 0.9 copy-done.5
  57.5 0.8 copy-done.6
  58.3 0.8 copy-done.7
  59.2 0.6 shard_map.153
  59.8 2.7 %shard_map.154 = (bf16[128,384]{1,0:T(8,128)(2,1)S(1)}, bf16[128,384]{1,0:T(8,128)(2,1)S(1)}, bf16[128,384]{1,0:T(8,128)(2,1)S(1)}, bf16[128,384]{1,0:T(8,128)(2...) custom-call(s32[3]{0:T(128)S(1)} %pad_add_fusion.refs_0_, ...), custom_call_target="tpu_custom_call" | custom-call | flops 500000000 | bytes 4194304 | tf_op jit(solution)/shard_map/pallas_call | solution.py:567
  62.6 2.7 %shard_map.155 = (bf16[64,1024]{1,0:T(8,128)(2,1)S(1)}, bf16[64,1024]{1,0:T(8,128)(2,1)S(1)}, bf16[64,1024]{1,0:T(8,128)(2,1)S(1)}) custom-call(s32[3]{0:T(128)S(1)} %pad_add_fusion.refs_0_, bf16[128,1024]{1,0:T(8,128)(2,1)S(1)} %get-tuple-element.46.refs_1_, bf16[128,960]{1,0:T(8,128)(2,1)S(1)} %get-tuple-element.52.refs_2_.refs_4_.refs_5_, ...), custom_call_target="tpu_custom_call" | custom-call | flops 1000000000 | bytes 4194304 | tf_op jit(solution)/shard_map/pallas_call | solution.py:567
  65.4 1.3 collective-permute-done.19
  66.8 1.6 %collective-permute-start.20 = (bf16[64,1024]{1,0:T(8,128)(2,1)S(1)}, bf16[64,1024]{1,0:T(8,128)(2,1)S(1)}, u32[]{:S(2)}, u32[]{:S(2)}) collective-permute-start(bf16[64,1024]{1,0:T(8,128)(2,1)S(1)} %add.10.refs_1_), channel_id=1, source_target_pairs={{0,2},{1,3},{2,0},{3,1},{4,6},{5,7},{6,4},{7,5},{8,10},{9,11},{10,... | collective-permute-start | bytes 393224 | tf_op jit(solution)/shard_map/ppermute | solution.py:689
  68.3 4.1 %collective-permute-done.20.refs_2_ = bf16[64,1024]{1,0:T(8,128)(2,1)S(1)} collective-permute-done((bf16[64,1024]{1,0:T(8,128)(2,1)S(1)}, bf16[64,1024]{1,0:T(8,128)(2,1)S(1)}, u32[]{:S(2)}, u32[]{:S(2)}) %collective-permute-start.20) | collective-permute-done | bytes 131104 | tf_op jit(solution)/shard_map/ppermute | solution.py:689
  72.4 0.8 shard_map.156
  73.2 1.3 collective-permute-start.21
  74.5 5.6 %collective-permute-done.21.refs_2_ = bf16[64,1024]{1,0:T(8,128)(2,1)S(1)} collective-permute-done((bf16[64,1024]{1,0:T(8,128)(2,1)S(1)}, bf16[64,1024]{1,0:T(8,128)(2,1)S(1)}, u32[]{:S(2)}, u32[]{:S(2)}) %collective-permute-start.21) | collective-permute-done | bytes 131104 | tf_op jit(solution)/shard_map/ppermute | solution.py:704
  80.0 1.3 collective-permute-done.22.refs_3_
  81.4 2.8 %shard_map.157 = (bf16[64,1664]{1,0:T(8,128)(2,1)S(1)}, bf16[64,1664]{1,0:T(8,128)(2,1)S(1)}, bf16[64,1024]{1,0:T(8,128)(2,1)S(1)}, bf16[128,384]{1,0:T(8,128)(2...) custom-call(s32[3]{0:T(128)S(1)} %pad_add_fusion.refs_0_, ...), custom_call_target="tpu_custom_call" | custom-call | flops 1000000000 | bytes 4194304 | tf_op jit(solution)/shard_map/pallas_call | solution.py:567
  84.2 0.2 collective-permute-start.23
  84.4 2.1 %collective-permute-start.36 = (bf16[128,960]{1,0:T(8,128)(2,1)S(1)}, bf16[128,960]{1,0:T(8,128)(2,1)S(1)}, u32[]{:S(2)}, u32[]{:S(2)}) collective-permute-start(bf16[128,960]{1,0:T(8,128)(2,1)S(1)} %get-tuple-element.52.refs_2_.refs_4_.refs_5_), channel_id=1, source_target_pairs={{0,8},{4,12},{8,0},{12,4},{1,9},{5,13},{9,1},{13,5},{2,10},{6,14},... | collective-permute-start | bytes 737288 | tf_op jit(solution)/shard_map/ppermute | solution.py:580
  86.5 1.6 %collective-permute-start.24 = (bf16[64,1664]{1,0:T(8,128)(2,1)S(1)}, bf16[64,1664]{1,0:T(8,128)(2,1)S(1)}, u32[]{:S(2)}, u32[]{:S(2)}) collective-permute-start(bf16[64,1664]{1,0:T(8,128)(2,1)S(1)} %add.11.refs_1_), channel_id=1, source_target_pairs={{0,2},{1,3},{2,0},{3,1},{4,6},{5,7},{6,4},{7,5},{8,10},{9,11},{10,... | collective-permute-start | bytes 638984 | tf_op jit(solution)/shard_map/ppermute | solution.py:689
  88.1 1.2 collective-permute-start.35
  89.3 0.8 collective-permute-start.25
  90.1 9.5 %collective-permute-done.36.refs_7_ = bf16[128,960]{1,0:T(8,128)(2,1)S(1)} collective-permute-done((bf16[128,960]{1,0:T(8,128)(2,1)S(1)}, bf16[128,960]{1,0:T(8,128)(2,1)S(1)}, u32[]{:S(2)}, u32[]{:S(2)}) %collective-permute-start.36) | collective-permute-done | bytes 245792 | tf_op jit(solution)/shard_map/ppermute | solution.py:580
  99.6 3.0 %collective-permute-start.26 = (bf16[128,384]{1,0:T(8,128)(2,1)S(1)}, bf16[128,384]{1,0:T(8,128)(2,1)S(1)}, u32[]{:S(2)}, u32[]{:S(2)}) collective-permute-start(bf16[128,384]{1,0:T(8,128)(2,1)S(1)} %get-tuple-element.71), channel_id=1, source_target_pairs={{0,8},{4,12},{8,0},{12,4},{1,9},{5,13},{9,1},{13,5},{2,10},{6,14},... | collective-permute-start | bytes 294920 | tf_op jit(solution)/shard_map/ppermute | solution.py:580
  102.6 1.4 %collective-permute-done.25.refs_2_ = bf16[128,384]{1,0:T(8,128)(2,1)S(1)} collective-permute-done((bf16[128,384]{1,0:T(8,128)(2,1)S(1)}, bf16[128,384]{1,0:T(8,128)(2,1)S(1)}, u32[]{:S(2)}, u32[]{:S(2)}) %collective-permute-start.25) | collective-permute-done | bytes 98336 | tf_op jit(solution)/shard_map/ppermute | solution.py:580
  104.0 5.8 %collective-permute-start.27 = (bf16[128,384]{1,0:T(8,128)(2,1)S(1)}, bf16[128,384]{1,0:T(8,128)(2,1)S(1)}, u32[]{:S(2)}, u32[]{:S(2)}) collective-permute-start(bf16[128,384]{1,0:T(8,128)(2,1)S(1)} %get-tuple-element.72), channel_id=1, source_target_pairs={{0,12},{4,8},{8,4},{12,0},{1,13},{5,9},{9,5},{13,1},{2,14},{6,10},... | collective-permute-start | bytes 294920 | tf_op jit(solution)/shard_map/ppermute | solution.py:580
  109.8 1.4 %shard_map.158 = (bf16[32,1024]{1,0:T(8,128)(2,1)}, bf16[64,640]{1,0:T(8,128)(2,1)S(1)}) custom-call(s32[3]{0:T(128)S(1)} %pad_add_fusion.refs_0_, bf16[64,1664]{1,0:T(8,128)(2,1)S(1)} %add.11.refs_1_, bf16[64,1664]{1,0:T(8,128)(2,1)S(1)} %collective-permute-done.24.refs_2_, bf16[64,1024]{1,0:T(8,128)(2,1)S(1)} %get-tuple-element.67.refs_3_, ...), custom_call_target="tpu_custom_call" | custom-call | flops 1000000 | bytes 4194304 | tf_op jit(solution)/shard_map/pallas_call | solution.py:567
  111.2 2.9 %collective-permute-start.29 = (bf16[64,640]{1,0:T(8,128)(2,1)S(1)}, bf16[64,640]{1,0:T(8,128)(2,1)S(1)}, u32[]{:S(2)}, u32[]{:S(2)}) collective-permute-start(bf16[64,640]{1,0:T(8,128)(2,1)S(1)} %get-tuple-element.73.refs_5_), channel_id=1, source_target_pairs={{0,8},{4,12},{8,0},{12,4},{1,9},{5,13},{9,1},{13,5},{2,10},{6,14},... | collective-permute-start | bytes 245768 | tf_op jit(solution)/shard_map/ppermute | solution.py:580
  114.2 5.4 %collective-permute-start.41 = (bf16[128,256]{1,0:T(8,128)(2,1)S(1)}, bf16[128,256]{1,0:T(8,128)(2,1)S(1)}, u32[]{:S(2)}, u32[]{:S(2)}) collective-permute-start(bf16[128,256]{1,0:T(8,128)(2,1)S(1)} %get-tuple-element.77), channel_id=1, source_target_pairs={{0,4},{4,0},{8,12},{12,8},{1,5},{5,1},{9,13},{13,9},{2,6},{6,2},{1... | collective-permute-start | bytes 196616 | tf_op jit(solution)/shard_map/ppermute | solution.py:580
  119.5 0.3 collective-permute-start.42
  119.8 2.0 %collective-permute-start.38 = (bf16[128,384]{1,0:T(8,128)(2,1)S(1)}, bf16[128,384]{1,0:T(8,128)(2,1)S(1)}, u32[]{:S(2)}, u32[]{:S(2)}) collective-permute-start(bf16[128,384]{1,0:T(8,128)(2,1)S(1)} %get-tuple-element.75.refs_9_), channel_id=1, source_target_pairs={{0,4},{4,0},{8,12},{12,8},{1,5},{5,1},{9,13},{13,9},{2,6},{6,2},{1... | collective-permute-start | bytes 294920 | tf_op jit(solution)/shard_map/ppermute | solution.py:580
  121.9 1.6 %collective-permute-done.41.refs_14_ = bf16[128,256]{1,0:T(8,128)(2,1)S(1)} collective-permute-done((bf16[128,256]{1,0:T(8,128)(2,1)S(1)}, bf16[128,256]{1,0:T(8,128)(2,1)S(1)}, u32[]{:S(2)}, u32[]{:S(2)}) %collective-permute-start.41) | collective-permute-done | bytes 65568 | tf_op jit(solution)/shard_map/ppermute | solution.py:580
  123.5 0.9 collective-permute-start.28
  124.4 1.2 collective-permute-start.30
  125.6 0.2 collective-permute-done.42.refs_15_
  125.7 2.0 %collective-permute-start.43 = (bf16[128,256]{1,0:T(8,128)(2,1)S(1)}, bf16[128,256]{1,0:T(8,128)(2,1)S(1)}, u32[]{:S(2)}, u32[]{:S(2)}) collective-permute-start(bf16[128,256]{1,0:T(8,128)(2,1)S(1)} %get-tuple-element.79), channel_id=1, source_target_pairs={{0,12},{4,8},{8,4},{12,0},{1,13},{5,9},{9,5},{13,1},{2,14},{6,10},... | collective-permute-start | bytes 196616 | tf_op jit(solution)/shard_map/ppermute | solution.py:580
  127.7 4.0 %collective-permute-done.43.refs_16_ = bf16[128,256]{1,0:T(8,128)(2,1)S(1)} collective-permute-done((bf16[128,256]{1,0:T(8,128)(2,1)S(1)}, bf16[128,256]{1,0:T(8,128)(2,1)S(1)}, u32[]{:S(2)}, u32[]{:S(2)}) %collective-permute-start.43) | collective-permute-done | bytes 65568 | tf_op jit(solution)/shard_map/ppermute | solution.py:580
  131.8 0.5 collective-permute-start.33
  132.4 0.4 collective-permute-start.34
  132.8 2.9 %shard_map.160 = (f32[256,384]{1,0:T(8,128)}, f32[128,512]{1,0:T(8,128)}, f32[256,256]{1,0:T(8,128)}) custom-call(s32[3]{0:T(128)S(1)} %pad_add_fusion.refs_0_, bf16[128,384]{1,0:T(8,128)(2,1)S(1)} %get-tuple-element.69.refs_1_, bf16[128,384]{1,0:T(8,128)(2,1)S(1)} %collective-permute-done.25.refs_2_, bf16[128,384]{1,0:T(8,128)(2,1)S(1)} %collective-permute-done.26.refs_3_, ...), custom_call_target="tpu_custom_call" | custom-call | flops 1000000000 | bytes 4194304 | tf_op jit(solution)/shard_map/pallas_call | solution.py:567
  135.7 1.9 %shard_map.159 = (f32[1,256]{1,0:T(1,128)}, f32[576,256]{1,0:T(8,128)}, f32[1,128]{1,0:T(1,128)}) custom-call(s32[3]{0:T(128)S(1)} %pad_add_fusion.refs_0_, bf16[128,384]{1,0:T(8,128)(2,1)S(1)} %get-tuple-element.69.refs_1_, bf16[128,384]{1,0:T(8,128)(2,1)S(1)} %collective-permute-done.25.refs_2_, bf16[128,384]{1,0:T(8,128)(2,1)S(1)} %collective-permute-done.26.refs_3_, ...), custom_call_target="tpu_custom_call" | custom-call | flops 1000000000 | bytes 4194304 | tf_op jit(solution)/shard_map/pallas_call | solution.py:567
  (54 shorter events, 0.6 us)
Async XLA Ops:
  0.6 5.7 %copy-start = (bf16[1,256,576]{1,2,0:T(8,128)(2,1)S(1)}, bf16[1,256,576]{1,2,0:T(8,128)(2,1)}, u32[]{:S(2)}) copy-start(bf16[1,256,576]{1,2,0:T(8,128)(2,1)} %param.14) | copy-start | bytes 884740
  0.6 30.6 %collective-permute-start.14 = (bf16[128,512]{1,0:T(8,128)(2,1)}, bf16[128,512]{1,0:T(8,128)(2,1)S(1)}, u32[]{:S(2)}, u32[]{:S(2)}) collective-permute-start(bf16[128,512]{1,0:T(8,128)(2,1)} %bitcast.24), channel_id=1, source_target_pairs={{0,8},{4,12},{8,0},{12,4},{1,9},{5,13},{9,1},{13,5},{2,10},{6,14},... | collective-permute-start | bytes 393224 | tf_op jit(solution)/shard_map/ppermute | solution.py:580
  4.8 29.8 %collective-permute-start.13 = (bf16[128,512]{1,0:T(8,128)(2,1)}, bf16[128,512]{1,0:T(8,128)(2,1)S(1)}, u32[]{:S(2)}, u32[]{:S(2)}) collective-permute-start(bf16[128,512]{1,0:T(8,128)(2,1)} %bitcast.25), channel_id=1, source_target_pairs={{0,4},{4,0},{8,12},{12,8},{1,5},{5,1},{9,13},{13,9},{2,6},{6,2},{1... | collective-permute-start | bytes 393224 | tf_op jit(solution)/shard_map/ppermute | solution.py:580
  6.4 28.3 %collective-permute-start.7 = (bf16[288,256]{1,0:T(8,128)(2,1)S(1)}, bf16[288,256]{1,0:T(8,128)(2,1)S(1)}, u32[]{:S(2)}, u32[]{:S(2)}) collective-permute-start(bf16[288,256]{1,0:T(8,128)(2,1)S(1)} %dynamic-slice_bitcast_fusion.refs_10_), channel_id=1, source_target_pairs={{0,8},{4,12},{8,0},{12,4},{1,9},{5,13},{9,1},{13,5},{2,10},{6,14},... | collective-permute-start | bytes 442376 | tf_op jit(solution)/shard_map/ppermute | solution.py:580
  6.8 27.8 %collective-permute-start.17 = (bf16[256,256]{1,0:T(8,128)(2,1)}, bf16[256,256]{1,0:T(8,128)(2,1)S(1)}, u32[]{:S(2)}, u32[]{:S(2)}) collective-permute-start(bf16[256,256]{1,0:T(8,128)(2,1)} %bitcast.27), channel_id=1, source_target_pairs={{0,8},{4,12},{8,0},{12,4},{1,9},{5,13},{9,1},{13,5},{2,10},{6,14},... | collective-permute-start | bytes 393224 | tf_op jit(solution)/shard_map/ppermute | solution.py:580
  10.7 12.6 %collective-permute-start.1 = (bf16[1,384]{1,0:T(2,128)(2,1)S(1)}, bf16[1,384]{1,0:T(2,128)(2,1)S(1)}, u32[]{:S(2)}, u32[]{:S(2)}) collective-permute-start(bf16[1,384]{1,0:T(2,128)(2,1)S(1)} %constant_dynamic-update-slice_fusion.refs_2_), channel_id=1, source_target_pairs={{0,8},{4,12},{8,0},{12,4},{1,9},{5,13},{9,1},{13,5},{2,10},{6,14},... | collective-permute-start | bytes 2312 | tf_op jit(solution)/shard_map/ppermute | solution.py:580
  23.3 3.6 %collective-permute-start = (bf16[1,384]{1,0:T(2,128)(2,1)S(1)}, bf16[1,384]{1,0:T(2,128)(2,1)S(1)}, u32[]{:S(2)}, u32[]{:S(2)}) collective-permute-start(bf16[1,384]{1,0:T(2,128)(2,1)S(1)} %constant_dynamic-update-slice_fusion.refs_2_), channel_id=1, source_target_pairs={{0,4},{4,0},{8,12},{12,8},{1,5},{5,1},{9,13},{13,9},{2,6},{6,2},{1... | collective-permute-start | bytes 2312 | tf_op jit(solution)/shard_map/ppermute | solution.py:580
  26.9 3.6 %collective-permute-start.2 = (bf16[1,384]{1,0:T(2,128)(2,1)S(1)}, bf16[1,384]{1,0:T(2,128)(2,1)S(1)}, u32[]{:S(2)}, u32[]{:S(2)}) collective-permute-start(bf16[1,384]{1,0:T(2,128)(2,1)S(1)} %collective-permute-done.1.refs_4_), channel_id=1, source_target_pairs={{0,4},{4,0},{8,12},{12,8},{1,5},{5,1},{9,13},{13,9},{2,6},{6,2},{1... | collective-permute-start | bytes 2312 | tf_op jit(solution)/shard_map/ppermute | solution.py:580
  30.5 6.2 %collective-permute-start.6 = (bf16[288,256]{1,0:T(8,128)(2,1)S(1)}, bf16[288,256]{1,0:T(8,128)(2,1)S(1)}, u32[]{:S(2)}, u32[]{:S(2)}) collective-permute-start(bf16[288,256]{1,0:T(8,128)(2,1)S(1)} %dynamic-slice_bitcast_fusion.refs_10_), channel_id=1, source_target_pairs={{0,4},{4,0},{8,12},{12,8},{1,5},{5,1},{9,13},{13,9},{2,6},{6,2},{1... | collective-permute-start | bytes 442376 | tf_op jit(solution)/shard_map/ppermute | solution.py:580
  31.3 9.2 %collective-permute-start.4 = (bf16[256,384]{1,0:T(8,128)(2,1)}, bf16[256,384]{1,0:T(8,128)(2,1)S(1)}, u32[]{:S(2)}, u32[]{:S(2)}) collective-permute-start(bf16[256,384]{1,0:T(8,128)(2,1)} %bitcast.21), channel_id=1, source_target_pairs={{0,8},{4,12},{8,0},{12,4},{1,9},{5,13},{9,1},{13,5},{2,10},{6,14},... | collective-permute-start | bytes 589832 | tf_op jit(solution)/shard_map/ppermute | solution.py:580
  34.6 2.1 %collective-permute-start.9 = (bf16[288,256]{1,0:T(8,128)(2,1)S(1)}, bf16[288,256]{1,0:T(8,128)(2,1)S(1)}, u32[]{:S(2)}, u32[]{:S(2)}) collective-permute-start(bf16[288,256]{1,0:T(8,128)(2,1)S(1)} %dynamic-slice_bitcast_fusion.refs_10_), channel_id=1, source_target_pairs={{0,1},{1,0},{2,3},{3,2},{4,5},{5,4},{6,7},{7,6},{8,9},{9,8},{10,11... | collective-permute-start | bytes 442376 | tf_op jit(solution)/shard_map/ppermute | solution.py:580
  34.6 9.8 %collective-permute-start.3 = (bf16[256,384]{1,0:T(8,128)(2,1)}, bf16[256,384]{1,0:T(8,128)(2,1)S(1)}, u32[]{:S(2)}, u32[]{:S(2)}) collective-permute-start(bf16[256,384]{1,0:T(8,128)(2,1)} %bitcast.22), channel_id=1, source_target_pairs={{0,4},{4,0},{8,12},{12,8},{1,5},{5,1},{9,13},{13,9},{2,6},{6,2},{1... | collective-permute-start | bytes 589832 | tf_op jit(solution)/shard_map/ppermute | solution.py:580
  34.7 12.8 %collective-permute-start.8 = (bf16[288,256]{1,0:T(8,128)(2,1)S(1)}, bf16[288,256]{1,0:T(8,128)(2,1)S(1)}, u32[]{:S(2)}, u32[]{:S(2)}) collective-permute-start(bf16[288,256]{1,0:T(8,128)(2,1)S(1)} %collective-permute-done.7.refs_12_), channel_id=1, source_target_pairs={{0,4},{4,0},{8,12},{12,8},{1,5},{5,1},{9,13},{13,9},{2,6},{6,2},{1... | collective-permute-start | bytes 442376 | tf_op jit(solution)/shard_map/ppermute | solution.py:580
  36.7 16.1 %collective-permute-start.11 = (bf16[288,256]{1,0:T(8,128)(2,1)S(1)}, bf16[288,256]{1,0:T(8,128)(2,1)S(1)}, u32[]{:S(2)}, u32[]{:S(2)}) collective-permute-start(bf16[288,256]{1,0:T(8,128)(2,1)S(1)} %collective-permute-done.7.refs_12_), channel_id=1, source_target_pairs={{0,1},{1,0},{2,3},{3,2},{4,5},{5,4},{6,7},{7,6},{8,9},{9,8},{10,11... | collective-permute-start | bytes 442376 | tf_op jit(solution)/shard_map/ppermute | solution.py:580
  36.7 13.6 %collective-permute-start.15 = (bf16[128,512]{1,0:T(8,128)(2,1)S(1)}, bf16[128,512]{1,0:T(8,128)(2,1)S(1)}, u32[]{:S(2)}, u32[]{:S(2)}) collective-permute-start(bf16[128,512]{1,0:T(8,128)(2,1)S(1)} %collective-permute-done.14.refs_20_.refs_15_.refs_17_), channel_id=1, source_target_pairs={{0,4},{4,0},{8,12},{12,8},{1,5},{5,1},{9,13},{13,9},{2,6},{6,2},{1... | collective-permute-start | bytes 393224 | tf_op jit(solution)/shard_map/ppermute | solution.py:580
  40.4 19.4 %collective-permute-start.5 = (bf16[256,384]{1,0:T(8,128)(2,1)S(1)}, bf16[256,384]{1,0:T(8,128)(2,1)S(1)}, u32[]{:S(2)}, u32[]{:S(2)}) collective-permute-start(bf16[256,384]{1,0:T(8,128)(2,1)S(1)} %collective-permute-done.4.refs_8_.refs_10_.refs_12_), channel_id=1, source_target_pairs={{0,4},{4,0},{8,12},{12,8},{1,5},{5,1},{9,13},{13,9},{2,6},{6,2},{1... | collective-permute-start | bytes 589832 | tf_op jit(solution)/shard_map/ppermute | solution.py:580
  44.4 15.4 %collective-permute-start.10 = (bf16[288,256]{1,0:T(8,128)(2,1)S(1)}, bf16[288,256]{1,0:T(8,128)(2,1)S(1)}, u32[]{:S(2)}, u32[]{:S(2)}) collective-permute-start(bf16[288,256]{1,0:T(8,128)(2,1)S(1)} %collective-permute-done.6.refs_11_), channel_id=1, source_target_pairs={{0,1},{1,0},{2,3},{3,2},{4,5},{5,4},{6,7},{7,6},{8,9},{9,8},{10,11... | collective-permute-start | bytes 442376 | tf_op jit(solution)/shard_map/ppermute | solution.py:580
  47.5 12.4 %collective-permute-start.12 = (bf16[288,256]{1,0:T(8,128)(2,1)S(1)}, bf16[288,256]{1,0:T(8,128)(2,1)S(1)}, u32[]{:S(2)}, u32[]{:S(2)}) collective-permute-start(bf16[288,256]{1,0:T(8,128)(2,1)S(1)} %collective-permute-done.8.refs_13_), channel_id=1, source_target_pairs={{0,1},{1,0},{2,3},{3,2},{4,5},{5,4},{6,7},{7,6},{8,9},{9,8},{10,11... | collective-permute-start | bytes 442376 | tf_op jit(solution)/shard_map/ppermute | solution.py:580
  50.3 12.3 %collective-permute-start.16 = (bf16[256,256]{1,0:T(8,128)(2,1)}, bf16[256,256]{1,0:T(8,128)(2,1)S(1)}, u32[]{:S(2)}, u32[]{:S(2)}) collective-permute-start(bf16[256,256]{1,0:T(8,128)(2,1)} %bitcast.28), channel_id=1, source_target_pairs={{0,4},{4,0},{8,12},{12,8},{1,5},{5,1},{9,13},{13,9},{2,6},{6,2},{1... | collective-permute-start | bytes 393224 | tf_op jit(solution)/shard_map/ppermute | solution.py:580
  52.8 9.8 %collective-permute-start.18 = (bf16[256,256]{1,0:T(8,128)(2,1)S(1)}, bf16[256,256]{1,0:T(8,128)(2,1)S(1)}, u32[]{:S(2)}, u32[]{:S(2)}) collective-permute-start(bf16[256,256]{1,0:T(8,128)(2,1)S(1)} %collective-permute-done.17.refs_19_.refs_21_), channel_id=1, source_target_pairs={{0,4},{4,0},{8,12},{12,8},{1,5},{5,1},{9,13},{13,9},{2,6},{6,2},{1... | collective-permute-start | bytes 393224 | tf_op jit(solution)/shard_map/ppermute | solution.py:580
  52.9 1.0 copy-start.1
  53.8 0.9 copy-start.2
  54.8 0.9 copy-start.3
  55.7 0.9 copy-start.4
  56.6 0.9 copy-start.5
  57.5 0.8 copy-start.6
  58.3 0.8 copy-start.7
  65.3 1.4 %collective-permute-start.19 = (bf16[64,1024]{1,0:T(8,128)(2,1)S(1)}, bf16[64,1024]{1,0:T(8,128)(2,1)S(1)}, u32[]{:S(2)}, u32[]{:S(2)}) collective-permute-start(bf16[64,1024]{1,0:T(8,128)(2,1)S(1)} %get-tuple-element.61), channel_id=1, source_target_pairs={{0,1},{1,0},{2,3},{3,2},{4,5},{5,4},{6,7},{7,6},{8,9},{9,8},{10,11... | collective-permute-start | bytes 393224 | tf_op jit(solution)/shard_map/ppermute | solution.py:580
  66.8 5.6 %collective-permute-start.20 = (bf16[64,1024]{1,0:T(8,128)(2,1)S(1)}, bf16[64,1024]{1,0:T(8,128)(2,1)S(1)}, u32[]{:S(2)}, u32[]{:S(2)}) collective-permute-start(bf16[64,1024]{1,0:T(8,128)(2,1)S(1)} %add.10.refs_1_), channel_id=1, source_target_pairs={{0,2},{1,3},{2,0},{3,1},{4,6},{5,7},{6,4},{7,5},{8,10},{9,11},{10,... | collective-permute-start | bytes 393224 | tf_op jit(solution)/shard_map/ppermute | solution.py:689
  73.2 6.9 %collective-permute-start.21 = (bf16[64,1024]{1,0:T(8,128)(2,1)S(1)}, bf16[64,1024]{1,0:T(8,128)(2,1)S(1)}, u32[]{:S(2)}, u32[]{:S(2)}) collective-permute-start(bf16[64,1024]{1,0:T(8,128)(2,1)S(1)} %shard_map.156), channel_id=1, source_target_pairs={{16,0},{17,1},{18,2},{19,3},{20,4},{21,5},{22,6},{23,7},{24,8},{25... | collective-permute-start | bytes 393224 | tf_op jit(solution)/shard_map/ppermute | solution.py:704
  80.0 1.3 collective-permute-start.22
  84.2 2.3 %collective-permute-start.23 = (bf16[64,1664]{1,0:T(8,128)(2,1)S(1)}, bf16[64,1664]{1,0:T(8,128)(2,1)S(1)}, u32[]{:S(2)}, u32[]{:S(2)}) collective-permute-start(bf16[64,1664]{1,0:T(8,128)(2,1)S(1)} %get-tuple-element.66), channel_id=1, source_target_pairs={{0,1},{1,0},{2,3},{3,2},{4,5},{5,4},{6,7},{7,6},{8,9},{9,8},{10,11... | collective-permute-start | bytes 638984 | tf_op jit(solution)/shard_map/ppermute | solution.py:580
  84.4 15.2 %collective-permute-start.36 = (bf16[128,960]{1,0:T(8,128)(2,1)S(1)}, bf16[128,960]{1,0:T(8,128)(2,1)S(1)}, u32[]{:S(2)}, u32[]{:S(2)}) collective-permute-start(bf16[128,960]{1,0:T(8,128)(2,1)S(1)} %get-tuple-element.52.refs_2_.refs_4_.refs_5_), channel_id=1, source_target_pairs={{0,8},{4,12},{8,0},{12,4},{1,9},{5,13},{9,1},{13,5},{2,10},{6,14},... | collective-permute-start | bytes 737288 | tf_op jit(solution)/shard_map/ppermute | solution.py:580
  86.5 23.3 %collective-permute-start.24 = (bf16[64,1664]{1,0:T(8,128)(2,1)S(1)}, bf16[64,1664]{1,0:T(8,128)(2,1)S(1)}, u32[]{:S(2)}, u32[]{:S(2)}) collective-permute-start(bf16[64,1664]{1,0:T(8,128)(2,1)S(1)} %add.11.refs_1_), channel_id=1, source_target_pairs={{0,2},{1,3},{2,0},{3,1},{4,6},{5,7},{6,4},{7,5},{8,10},{9,11},{10,... | collective-permute-start | bytes 638984 | tf_op jit(solution)/shard_map/ppermute | solution.py:689
  88.1 31.5 %collective-permute-start.35 = (bf16[128,960]{1,0:T(8,128)(2,1)S(1)}, bf16[128,960]{1,0:T(8,128)(2,1)S(1)}, u32[]{:S(2)}, u32[]{:S(2)}) collective-permute-start(bf16[128,960]{1,0:T(8,128)(2,1)S(1)} %get-tuple-element.52.refs_2_.refs_4_.refs_5_), channel_id=1, source_target_pairs={{0,4},{4,0},{8,12},{12,8},{1,5},{5,1},{9,13},{13,9},{2,6},{6,2},{1... | collective-permute-start | bytes 737288 | tf_op jit(solution)/shard_map/ppermute | solution.py:580
  89.3 14.7 %collective-permute-start.25 = (bf16[128,384]{1,0:T(8,128)(2,1)S(1)}, bf16[128,384]{1,0:T(8,128)(2,1)S(1)}, u32[]{:S(2)}, u32[]{:S(2)}) collective-permute-start(bf16[128,384]{1,0:T(8,128)(2,1)S(1)} %get-tuple-element.70), channel_id=1, source_target_pairs={{0,4},{4,0},{8,12},{12,8},{1,5},{5,1},{9,13},{13,9},{2,6},{6,2},{1... | collective-permute-start | bytes 294920 | tf_op jit(solution)/shard_map/ppermute | solution.py:580
  99.6 20.3 %collective-permute-start.37 = (bf16[128,960]{1,0:T(8,128)(2,1)S(1)}, bf16[128,960]{1,0:T(8,128)(2,1)S(1)}, u32[]{:S(2)}, u32[]{:S(2)}) collective-permute-start(bf16[128,960]{1,0:T(8,128)(2,1)S(1)} %collective-permute-done.36.refs_7_), channel_id=1, source_target_pairs={{0,4},{4,0},{8,12},{12,8},{1,5},{5,1},{9,13},{13,9},{2,6},{6,2},{1... | collective-permute-start | bytes 737288 | tf_op jit(solution)/shard_map/ppermute | solution.py:580
  99.6 11.7 %collective-permute-start.26 = (bf16[128,384]{1,0:T(8,128)(2,1)S(1)}, bf16[128,384]{1,0:T(8,128)(2,1)S(1)}, u32[]{:S(2)}, u32[]{:S(2)}) collective-permute-start(bf16[128,384]{1,0:T(8,128)(2,1)S(1)} %get-tuple-element.71), channel_id=1, source_target_pairs={{0,8},{4,12},{8,0},{12,4},{1,9},{5,13},{9,1},{13,5},{2,10},{6,14},... | collective-permute-start | bytes 294920 | tf_op jit(solution)/shard_map/ppermute | solution.py:580
  104.0 10.2 %collective-permute-start.27 = (bf16[128,384]{1,0:T(8,128)(2,1)S(1)}, bf16[128,384]{1,0:T(8,128)(2,1)S(1)}, u32[]{:S(2)}, u32[]{:S(2)}) collective-permute-start(bf16[128,384]{1,0:T(8,128)(2,1)S(1)} %get-tuple-element.72), channel_id=1, source_target_pairs={{0,12},{4,8},{8,4},{12,0},{1,13},{5,9},{9,5},{13,1},{2,14},{6,10},... | collective-permute-start | bytes 294920 | tf_op jit(solution)/shard_map/ppermute | solution.py:580
  109.8 12.0 %collective-permute-start.39 = (bf16[128,384]{1,0:T(8,128)(2,1)S(1)}, bf16[128,384]{1,0:T(8,128)(2,1)S(1)}, u32[]{:S(2)}, u32[]{:S(2)}) collective-permute-start(bf16[128,384]{1,0:T(8,128)(2,1)S(1)} %get-tuple-element.75.refs_9_), channel_id=1, source_target_pairs={{0,8},{4,12},{8,0},{12,4},{1,9},{5,13},{9,1},{13,5},{2,10},{6,14},... | collective-permute-start | bytes 294920 | tf_op jit(solution)/shard_map/ppermute | solution.py:580
  111.2 13.1 %collective-permute-start.29 = (bf16[64,640]{1,0:T(8,128)(2,1)S(1)}, bf16[64,640]{1,0:T(8,128)(2,1)S(1)}, u32[]{:S(2)}, u32[]{:S(2)}) collective-permute-start(bf16[64,640]{1,0:T(8,128)(2,1)S(1)} %get-tuple-element.73.refs_5_), channel_id=1, source_target_pairs={{0,8},{4,12},{8,0},{12,4},{1,9},{5,13},{9,1},{13,5},{2,10},{6,14},... | collective-permute-start | bytes 245768 | tf_op jit(solution)/shard_map/ppermute | solution.py:580
  114.2 9.4 %collective-permute-start.41 = (bf16[128,256]{1,0:T(8,128)(2,1)S(1)}, bf16[128,256]{1,0:T(8,128)(2,1)S(1)}, u32[]{:S(2)}, u32[]{:S(2)}) collective-permute-start(bf16[128,256]{1,0:T(8,128)(2,1)S(1)} %get-tuple-element.77), channel_id=1, source_target_pairs={{0,4},{4,0},{8,12},{12,8},{1,5},{5,1},{9,13},{13,9},{2,6},{6,2},{1... | collective-permute-start | bytes 196616 | tf_op jit(solution)/shard_map/ppermute | solution.py:580
  119.5 6.2 %collective-permute-start.42 = (bf16[128,256]{1,0:T(8,128)(2,1)S(1)}, bf16[128,256]{1,0:T(8,128)(2,1)S(1)}, u32[]{:S(2)}, u32[]{:S(2)}) collective-permute-start(bf16[128,256]{1,0:T(8,128)(2,1)S(1)} %get-tuple-element.78), channel_id=1, source_target_pairs={{0,8},{4,12},{8,0},{12,4},{1,9},{5,13},{9,1},{13,5},{2,10},{6,14},... | collective-permute-start | bytes 196616 | tf_op jit(solution)/shard_map/ppermute | solution.py:580
  119.8 12.0 %collective-permute-start.38 = (bf16[128,384]{1,0:T(8,128)(2,1)S(1)}, bf16[128,384]{1,0:T(8,128)(2,1)S(1)}, u32[]{:S(2)}, u32[]{:S(2)}) collective-permute-start(bf16[128,384]{1,0:T(8,128)(2,1)S(1)} %get-tuple-element.75.refs_9_), channel_id=1, source_target_pairs={{0,4},{4,0},{8,12},{12,8},{1,5},{5,1},{9,13},{13,9},{2,6},{6,2},{1... | collective-permute-start | bytes 294920 | tf_op jit(solution)/shard_map/ppermute | solution.py:580
  121.8 11.0 %collective-permute-start.40 = (bf16[128,384]{1,0:T(8,128)(2,1)S(1)}, bf16[128,384]{1,0:T(8,128)(2,1)S(1)}, u32[]{:S(2)}, u32[]{:S(2)}) collective-permute-start(bf16[128,384]{1,0:T(8,128)(2,1)S(1)} %collective-permute-done.39.refs_11_), channel_id=1, source_target_pairs={{0,4},{4,0},{8,12},{12,8},{1,5},{5,1},{9,13},{13,9},{2,6},{6,2},{1... | collective-permute-start | bytes 294920 | tf_op jit(solution)/shard_map/ppermute | solution.py:580
  123.5 8.8 %collective-permute-start.28 = (bf16[64,640]{1,0:T(8,128)(2,1)S(1)}, bf16[64,640]{1,0:T(8,128)(2,1)S(1)}, u32[]{:S(2)}, u32[]{:S(2)}) collective-permute-start(bf16[64,640]{1,0:T(8,128)(2,1)S(1)} %get-tuple-element.73.refs_5_), channel_id=1, source_target_pairs={{0,4},{4,0},{8,12},{12,8},{1,5},{5,1},{9,13},{13,9},{2,6},{6,2},{1... | collective-permute-start | bytes 245768 | tf_op jit(solution)/shard_map/ppermute | solution.py:580
  124.4 8.0 %collective-permute-start.30 = (bf16[64,640]{1,0:T(8,128)(2,1)S(1)}, bf16[64,640]{1,0:T(8,128)(2,1)S(1)}, u32[]{:S(2)}, u32[]{:S(2)}) collective-permute-start(bf16[64,640]{1,0:T(8,128)(2,1)S(1)} %collective-permute-done.29.refs_7_), channel_id=1, source_target_pairs={{0,4},{4,0},{8,12},{12,8},{1,5},{5,1},{9,13},{13,9},{2,6},{6,2},{1... | collective-permute-start | bytes 245768 | tf_op jit(solution)/shard_map/ppermute | solution.py:580
  125.7 6.1 %collective-permute-start.43 = (bf16[128,256]{1,0:T(8,128)(2,1)S(1)}, bf16[128,256]{1,0:T(8,128)(2,1)S(1)}, u32[]{:S(2)}, u32[]{:S(2)}) collective-permute-start(bf16[128,256]{1,0:T(8,128)(2,1)S(1)} %get-tuple-element.79), channel_id=1, source_target_pairs={{0,12},{4,8},{8,4},{12,0},{1,13},{5,9},{9,5},{13,1},{2,14},{6,10},... | collective-permute-start | bytes 196616 | tf_op jit(solution)/shard_map/ppermute | solution.py:580
  131.8 3.9 %collective-permute-start.31 = (bf16[64,640]{1,0:T(8,128)(2,1)S(1)}, bf16[64,640]{1,0:T(8,128)(2,1)S(1)}, u32[]{:S(2)}, u32[]{:S(2)}) collective-permute-start(bf16[64,640]{1,0:T(8,128)(2,1)S(1)} %get-tuple-element.73.refs_5_), channel_id=1, source_target_pairs={{0,1},{1,0},{2,3},{3,2},{4,5},{5,4},{6,7},{7,6},{8,9},{9,8},{10,11... | collective-permute-start | bytes 245768 | tf_op jit(solution)/shard_map/ppermute | solution.py:580
  131.8 3.9 %collective-permute-start.33 = (bf16[64,640]{1,0:T(8,128)(2,1)S(1)}, bf16[64,640]{1,0:T(8,128)(2,1)S(1)}, u32[]{:S(2)}, u32[]{:S(2)}) collective-permute-start(bf16[64,640]{1,0:T(8,128)(2,1)S(1)} %collective-permute-done.29.refs_7_), channel_id=1, source_target_pairs={{0,1},{1,0},{2,3},{3,2},{4,5},{5,4},{6,7},{7,6},{8,9},{9,8},{10,11... | collective-permute-start | bytes 245768 | tf_op jit(solution)/shard_map/ppermute | solution.py:580
  132.3 3.4 %collective-permute-start.32 = (bf16[64,640]{1,0:T(8,128)(2,1)S(1)}, bf16[64,640]{1,0:T(8,128)(2,1)S(1)}, u32[]{:S(2)}, u32[]{:S(2)}) collective-permute-start(bf16[64,640]{1,0:T(8,128)(2,1)S(1)} %collective-permute-done.28.refs_6_), channel_id=1, source_target_pairs={{0,1},{1,0},{2,3},{3,2},{4,5},{5,4},{6,7},{7,6},{8,9},{9,8},{10,11... | collective-permute-start | bytes 245768 | tf_op jit(solution)/shard_map/ppermute | solution.py:580
  132.4 3.3 %collective-permute-start.34 = (bf16[64,640]{1,0:T(8,128)(2,1)S(1)}, bf16[64,640]{1,0:T(8,128)(2,1)S(1)}, u32[]{:S(2)}, u32[]{:S(2)}) collective-permute-start(bf16[64,640]{1,0:T(8,128)(2,1)S(1)} %collective-permute-done.30.refs_8_), channel_id=1, source_target_pairs={{0,1},{1,0},{2,3},{3,2},{4,5},{5,4},{6,7},{7,6},{8,9},{9,8},{10,11... | collective-permute-start | bytes 245768 | tf_op jit(solution)/shard_map/ppermute | solution.py:580
where the time goes:
time: 138 us
  starting transfers between devices  56.6 us (41%)
  waiting for transfers between devices  56.5 us (41%)
  Pallas kernels  15.7 us (11%)
  local copies, waits for them, and re-layouts  7.68 us (6%)
    ppermute x41, starting transfers between devices, flipped(): return lax.ppermute(value, axis, [(i, i ^ bit) for i in range(count)])  52.2 us
    ppermute x41, waiting for transfers between devices, flipped(): return lax.ppermute(value, axis, [(i, i ^ bit) for i in range(count)])  46.9 us
    pallas_call x8, Pallas kernels, kernel_call(): got = call(*ins)  15.7 us
    unnamed x17, local copies, waits for them, and re-layouts  7 us
    ppermute x1, waiting for transfers between devices, token_shards(): lax.ppermute(dx, 'pipe', [(s, s - 1) for s in range(1, plan.n_pipe)])  5.56 us
    ppermute x2, waiting for transfers between devices, token_shards(): sums.append(lax.ppermute(chip, 'tensor', pairs))  4.06 us
    ppermute x2, starting transfers between devices, token_shards(): sums.append(lax.ppermute(chip, 'tensor', pairs))  3.11 us
  transfers between devices with their start and end apart: 44, of which 16 were waited for; matrix products, arithmetic and copies ran while one was open for 1% of the time, Pallas kernels for 6%

commit v1 on v0

--- a/solution.py
+++ b/solution.py
@@ -239,6 +239,7 @@
         self.tail = self.o_up
         self.own = self.micro * self.share
         self.half = self.rows // 2
+        self.part = self.latent // n_tensor
         self.spare = -self.latent % 128
         self.lrow = self.rank // max(self.spare, 1)
         self.grow = self.width // max(self.spare, 1)
@@ -246,11 +247,11 @@
 
     def fits(self):
         aligned = self.wcol % 256 == 0 and self.ccol % 128 == 0 and self.rope_all % 128 == 0
-        whole = (self.heads * self.length) % 128 == 0 and self.latent % 32 == 0
+        whole = (self.heads * self.length) % 128 == 0 and self.latent % (16 * self.nt) == 0
         if self.spare == 0 or self.rank % self.spare or self.wcol % self.spare:
             return False
         room = 2 * (self.lrow + self.grow) <= self.half
-        few = self.n & (self.n - 1) == 0 and self.rows <= 512
+        few = self.n & (self.n - 1) == 0 and self.nt & (self.nt - 1) == 0 and self.rows <= 512
         return aligned and whole and room and few and self.nt % 2 == 0 and self.share % 16 == 0
 
 
@@ -263,23 +264,31 @@
             at += plan.share
 
 
-def assemble_latent(plan, core, lat_own, lat_other, w_s):
-    part = plan.latent // 2
+def piece_body(plan, ranks, w_lat, gain, cgain, piece):
+    at = pl.multiple_of(ranks[1] * plan.part, 16)
+    piece[: plan.part, :] = w_lat[pl.ds(at, plan.part), :]
+    piece[plan.part : plan.part + 1, :] = gain[...]
+    piece[plan.part + 1 : plan.part + 2, : plan.ccol] = cgain[...]
+
+
+def assemble_latent(plan, t, lat, w_s):
     for k in range(plan.n):
-        w_s[k, pl.ds(pl.multiple_of(core * part, 16), part), :] = lat_own[k][...]
-        w_s[k, pl.ds(pl.multiple_of((1 - core) * part, 16), part), :] = lat_other[k][...]
-
-
-def forward_body(plan, ranks, x, gains, wq, lat_own, lat_other, wexp, cosine, sine, outs):
+        for i in range(plan.nt):
+            to = pl.ds(pl.multiple_of((t ^ i) * plan.part, 16), plan.part)
+            w_s[k, to, :] = lat[i][k * (plan.part + 16) : k * (plan.part + 16) + plan.part, :]
+
+
+def forward_body(plan, ranks, x, wq, lat, wexp, table, outs):
     (sent, pay, v_ref, p_ref, chat_ref, rc_ref, gain_ref, cgain_ref, x_own, wlat, g_s, cg_s, n_s, c_s) = outs
     n = plan.n
     j, t = ranks[0], ranks[1]
     core = lax.rem(t, 2)
-    assemble_latent(plan, core, lat_own, lat_other, wlat)
+    assemble_latent(plan, t, lat, wlat)
     for k in range(n):
         src = j ^ k
-        g_s[src] = gains[k][:, : plan.wcol].astype(F32)
-        cg_s[src] = gains[k][:, plan.wcol :].astype(F32)
+        both = lat[0][k * (plan.part + 16) + plan.part : (k + 1) * (plan.part + 16), :].astype(F32)
+        g_s[src] = both[:1]
+        cg_s[src] = both[1:2, : plan.ccol]
     xf = x[...].astype(F32)
     scale = lax.rsqrt(jnp.mean(xf * xf, axis=1, keepdims=True) + EPS)
     for b in range(n):
@@ -304,7 +313,7 @@
     expanded = jnp.zeros((plan.rows, plan.heads * (NOPE + VDIM)), F32)
     for k in range(n):
         expanded = expanded + mm(c_s[j ^ k], wexp[k][...])
-    cos, sin = cosine[...], sine[...]
+    cos, sin = table[:, :ROPE], table[:, ROPE:]
     kr = rotate(latent[:, plan.rank :], cos, sin).astype(BF16)
     row = lax.broadcasted_iota(jnp.int32, (plan.rows, plan.rows), 0)
     col = lax.broadcasted_iota(jnp.int32, (plan.rows, plan.rows), 1)
@@ -333,8 +342,9 @@
         mixed_all.append(mixed)
     qr_cat = jnp.concatenate(qr_all, axis=1)
     for k in range(n):
-        sent[k][:, : plan.wcol] = n_s[j ^ k]
-        sent[k][:, plan.wcol :] = c_s[j ^ k]
+        for start, at in share_rows(plan, core):
+            sent[k][at, : plan.wcol] = n_s[j ^ k, pl.ds(start, plan.share), :]
+            sent[k][at, plan.wcol :] = c_s[j ^ k, pl.ds(start, plan.share), :]
     for h in range(plan.heads):
         pay[:, plan.o_mixed + h * VDIM : plan.o_mixed + (h + 1) * VDIM] = mixed_all[h]
         pay[:, plan.o_q + h * NOPE : plan.o_q + (h + 1) * NOPE] = qn_all[h]
@@ -357,7 +367,7 @@
 
 
 def backward_body(plan, last, ranks, top, pieces, pay, v_ref, p_ref, chat_ref, rc_ref, cgain_ref,
-                  wq, wlat, wexp, wout, cosine, sine, outs):
+                  wq, wlat, wexp, wout, table, outs):
     chunks, up_own, tail, ups, up_s, u_s, d_s, dn_s, dl_s = outs
     n = plan.n
     j, t, is_top = ranks[0], ranks[1], ranks[2]
@@ -384,7 +394,7 @@
     for k in range(n):
         dmixed = dmixed + mm_nt(u_s[j ^ k], wout[k][...])
     dmixed = dmixed.astype(BF16)
-    cos, sin = cosine[...], sine[...]
+    cos, sin = table[:, :ROPE], table[:, ROPE:]
     dq, dexp, dvs, dss = [], [], [], []
     dkr = jnp.zeros((plan.rows, ROPE), F32)
     scale = (NOPE + ROPE) ** (-0.5)
@@ -436,7 +446,8 @@
         for h in range(plan.heads):
             tail[:, plan.o_dv + h * VDIM : plan.o_dv + (h + 1) * VDIM] = dvs[h]
         for k in range(n):
-            ups[k][...] = u_s[j ^ k]
+            for start, at in share_rows(plan, core):
+                ups[k][at, :] = u_s[j ^ k, pl.ds(start, plan.share), :]
 
 
 def put_split(plan, ref, col, row, values):
@@ -475,16 +486,17 @@
     put_split(plan, dl_ref, plan.latent, 2 * plan.lrow, jnp.sum(dn * xhat, axis=0, keepdims=True))
 
 
-def gradient_body(plan, sent, pays, tails, ups, cosine, sine, outs):
-    g_q, g_exp, g_out, a_n, a_c, a_m, a_u, a_dq, a_de = outs
-    cos, sin = cosine[...], sine[...]
+def gradient_body(plan, ranks, sent, sent_o, pays, tails, table, outs):
+    g_q, g_exp, a_n, a_c, a_dq, a_de = outs
+    cos, sin = table[:, :ROPE], table[:, ROPE:]
+    core = lax.rem(ranks[1], 2)
     for k in range(plan.n):
-        at = slice(k * plan.rows, (k + 1) * plan.rows)
         pay, tail = pays[k], tails[k]
-        a_n[at, :] = sent[k][:, : plan.wcol]
-        a_c[at, :] = sent[k][:, plan.wcol :]
-        a_m[at, :] = pay[:, plan.o_mixed : plan.o_q]
-        a_u[at, :] = ups[k][...]
+        for side, block in ((core, sent[k]), (1 - core, sent_o[k])):
+            for start, part in share_rows(plan, side):
+                to = pl.ds(pl.multiple_of(k * plan.rows + start, plan.share), plan.share)
+                a_n[to, :] = block[part, : plan.wcol]
+                a_c[to, :] = block[part, plan.wcol :]
         for h in range(plan.heads):
             qn, kn, _, kr = key_parts(plan, pay, h)
             for m in range(plan.micro):
@@ -500,20 +512,23 @@
                 a_de[rows, e_at + NOPE : e_at + NOPE + VDIM] = tail[part, plan.o_dv + h * VDIM : plan.o_dv + (h + 1) * VDIM]
     g_q[...] = mm_tn(a_n[...], a_dq[...])
     g_exp[...] = mm_tn(a_c[...], a_de[...])
-    g_out[...] = mm_tn(a_m[...], a_u[...])
-
-
-def latent_gradient_body(plan, ranks, sent, dl_own, dl_other, outs):
-    g_gain, g_lat, g_lg, a_n, a_dl, m_s, l_s = outs
+
+
+def latent_gradient_body(plan, ranks, sent, sent_o, pays, ups, ups_o, dl_own, dl_other, outs):
+    g_gain, g_lat, g_lg, g_out, a_n, a_m, a_u, a_dl, m_s, l_s = outs
     n = plan.n
     j, t = ranks[0], ranks[1]
     core = lax.rem(t, 2)
     lgain = jnp.zeros((plan.lrow, plan.spare), F32)
     ggain = jnp.zeros((plan.grow, plan.spare), F32)
     for k in range(n):
-        a_n[k * plan.rows : (k + 1) * plan.rows, :] = sent[k][:, : plan.wcol]
-        for block, side in ((dl_own[k], core), (dl_other[k], 1 - core)):
+        a_m[k * plan.rows : (k + 1) * plan.rows, :] = pays[k][:, plan.o_mixed : plan.o_q]
+        mine, theirs = (dl_own[k], sent[k], ups[k], core), (dl_other[k], sent_o[k], ups_o[k], 1 - core)
+        for block, rows, up, side in (mine, theirs):
             for start, part in share_rows(plan, side):
+                to = pl.ds(pl.multiple_of(k * plan.rows + start, plan.share), plan.share)
+                a_n[to, :] = rows[part, : plan.wcol]
+                a_u[to, :] = up[part, :]
                 a_dl[pl.ds(pl.multiple_of(k * plan.rows + start, plan.share), plan.share), :] = block[part, : plan.latent]
             extra = block[:, plan.latent :].astype(F32)
             if side is core:
@@ -529,6 +544,7 @@
     g_gain[...] = m_s[j]
     g_lg[...] = l_s[j]
     g_lat[...] = mm_tn(a_dl[...], a_n[...])
+    g_out[...] = mm_tn(a_m[...], a_u[...])
 
 
 def grouped(counts_in, refs):
@@ -601,11 +617,22 @@
     section = lax.axis_index("pipe")
     is_top = (section == plan.n_pipe - 1).astype(jnp.int32)
     ranks = jnp.stack([j, t, is_top]).astype(jnp.int32)
-    part = plan.latent // 2
-    half_rows = lax.dynamic_slice_in_dim(w_latent[0].T, lax.rem(t, 2) * part, part, 0)
-    gains = gathered(jnp.concatenate([gain, compressed_gain], axis=1), "dp", n)
-    lat_own = gathered(half_rows, "dp", n)
-    lat_other = [flipped(block, "tensor", nt, 1) for block in lat_own]
+
+    def shape(dims, kind=BF16):
+        return jax.ShapeDtypeStruct(dims, kind)
+
+    def pick(ranks, w_lat, gain, cgain, piece):
+        piece_body(plan, ranks, w_lat, gain, cgain, piece)
+
+    def stack(ranks, blocks, target):
+        for k, block in enumerate(blocks):
+            target[k * (plan.part + 16) : (k + 1) * (plan.part + 16), :] = block[...]
+
+    tall = plan.part + 16
+    (piece,) = kernel_call(pick, [ranks, w_latent[0].T, gain, compressed_gain], [shape((tall, plan.wcol))], [], 10**4)
+    blocks = gathered(piece, "dp", n)
+    (stacked,) = kernel_call(stack, [ranks, blocks], [shape((n * tall, plan.wcol))], [], 10**4)
+    lat = gathered(stacked, "tensor", nt)
     wq = gathered(w_query[0], "dp", n)
     wexp = gathered(expand_weight[0], "dp", n)
     wout = gathered(w_output[0], "dp", n)
@@ -613,29 +640,29 @@
     top = top_grad.reshape(rows, plan.width)
     freq = 10000.0 ** (-np.arange(ROPE // 2) / (ROPE // 2))
     angle = np.tile(np.arange(plan.length)[:, None] * freq[None, :], (plan.micro, 1))
-    cosine = jnp.asarray(np.concatenate([np.cos(angle), np.cos(angle)], axis=1), F32)
-    sine = jnp.asarray(np.concatenate([-np.sin(angle), np.sin(angle)], axis=1), F32)
-
-    def shape(dims, kind=BF16):
-        return jax.ShapeDtypeStruct(dims, kind)
+    cos, sin = np.cos(angle), np.sin(angle)
+    table = jnp.asarray(np.concatenate([cos, cos, -sin, sin], axis=1), F32)
 
     def prepare(ranks, *refs):
         count = len(refs) // 2
         for source, target in zip(refs[:count], refs[count:]):
             target[...] = source[...]
 
-    local = [x, top, wq[0], wexp[0], wout[0], cosine, sine]
-    copied = kernel_call(prepare, [ranks] + local, [shape(v.shape, v.dtype) for v in local], [], 10**4)
-    x, top, wq[0], wexp[0], wout[0], cosine, sine = copied
-
-    def forward(ranks, x, gains, wq, lo, lt, we, cosine, sine, *outs):
-        forward_body(plan, ranks, x, gains, wq, lo, lt, we, cosine, sine, outs)
+    def local(values):
+        shapes = [shape(v.shape, v.dtype) for v in values]
+        return kernel_call(prepare, [ranks] + values, shapes, [], 10**4)
+
+    x, wq[0], wexp[0], table = local([x, wq[0], wexp[0], table])
+    top, wout[0] = local([top, wout[0]])
+
+    def forward(ranks, x, wq, lat, we, table, *outs):
+        forward_body(plan, ranks, x, wq, lat, we, table, outs)
 
     sent, pay, v, p, chat, rc, gain32, cgain32, x_own, wlat = kernel_call(
         forward,
-        [ranks, x, gains, wq, lat_own, lat_other, wexp, cosine, sine],
+        [ranks, x, wq, lat, wexp, table],
         [
-            [shape((rows, plan.wcol + plan.ccol))] * n,
+            [shape((plan.half, plan.wcol + plan.ccol))] * n,
             shape((rows, plan.pay)),
             shape((rows, plan.hcol)),
             shape((plan.heads, rows, rows), F32),
@@ -658,19 +685,19 @@
     for tick in range(plan.n_pipe):
         last = tick == plan.n_pipe - 1
 
-        def backward(ranks, top, pieces, pay, v, p, chat, rc, cg, wq, wl, we, wo, cosine, sine, *outs):
+        def backward(ranks, top, pieces, pay, v, p, chat, rc, cg, wq, wl, we, wo, table, *outs):
             outs = list(outs)
             if not last:
                 outs[2:2] = [None, None]
-            backward_body(plan, last, ranks, top, pieces, pay, v, p, chat, rc, cg, wq, wl, we, wo, cosine, sine, outs)
+            backward_body(plan, last, ranks, top, pieces, pay, v, p, chat, rc, cg, wq, wl, we, wo, table, outs)
 
         chunk = plan.chunk if last else plan.width
         out_groups = [[shape((plan.half, chunk))] * 2, shape((plan.half, plan.width))]
         if last:
-            out_groups += [shape((rows, plan.tail)), [shape((rows, plan.wcol))] * n]
+            out_groups += [shape((rows, plan.tail)), [shape((plan.half, plan.wcol))] * n]
         got = kernel_call(
             backward,
-            [ranks, top, pieces, pay, v, p, chat, rc, cgain32, wq, wlat, wexp, wout, cosine, sine],
+            [ranks, top, pieces, pay, v, p, chat, rc, cgain32, wq, wlat, wexp, wout, table],
             out_groups,
             [
                 pltpu.VMEM((rows, plan.width), BF16),
@@ -706,40 +733,43 @@
     dl_own = gathered(got[1], "dp", n)
     dl_other = [flipped(block, "tensor", nt, 1) for block in dl_own]
     sent = handed(sent, "dp", n)
+    sent_o = [flipped(block, "tensor", nt, 1) for block in sent]
     pays = gathered(pay, "dp", n)
     tails = gathered(tail, "dp", n)
     ups = handed(ups, "dp", n)
-
-    def gradients(ranks, sent, pays, tails, ups, cosine, sine, *outs):
-        gradient_body(plan, sent, pays, tails, ups, cosine, sine, outs)
-
-    def latent_gradients(ranks, sent, dl_own, dl_other, *outs):
-        latent_gradient_body(plan, ranks, sent, dl_own, dl_other, outs)
+    ups_o = [flipped(block, "tensor", nt, 1) for block in ups]
+
+    def gradients(ranks, sent, sent_o, pays, tails, table, *outs):
+        gradient_body(plan, ranks, sent, sent_o, pays, tails, table, outs)
+
+    def latent_gradients(ranks, sent, sent_o, pays, ups, ups_o, dl_own, dl_other, *outs):
+        latent_gradient_body(plan, ranks, sent, sent_o, pays, ups, ups_o, dl_own, dl_other, outs)
 
     every = n * rows
-    g_q, g_exp, g_out = kernel_call(
+    g_q, g_exp = kernel_call(
         gradients,
-        [ranks, sent, pays, tails, ups, cosine, sine],
+        [ranks, sent, sent_o, pays, tails, table],
+        [shape((plan.wcol, plan.qcol), F32), shape((plan.ccol, plan.heads * (NOPE + VDIM)), F32)],
         [
-            shape((plan.wcol, plan.qcol), F32),
-            shape((plan.ccol, plan.heads * (NOPE + VDIM)), F32),
+            pltpu.VMEM((every, plan.wcol), BF16),
+            pltpu.VMEM((every, plan.ccol), BF16),
+            pltpu.VMEM((every, plan.qcol), BF16),
+            pltpu.VMEM((every, plan.heads * (NOPE + VDIM)), BF16),
+        ],
+        10**9,
+    )
+    g_gain, g_lat, g_lg, g_out = kernel_call(
+        latent_gradients,
+        [ranks, sent, sent_o, pays, ups, ups_o, dl_own, dl_other],
+        [
+            shape((1, plan.wcol), F32),
+            shape((plan.latent, plan.wcol), F32),
+            shape((1, plan.ccol), F32),
             shape((plan.hcol, plan.wcol), F32),
         ],
         [
             pltpu.VMEM((every, plan.wcol), BF16),
-            pltpu.VMEM((every, plan.ccol), BF16),
             pltpu.VMEM((every, plan.hcol), BF16),
-            pltpu.VMEM((every, plan.wcol), BF16),
-            pltpu.VMEM((every, plan.qcol), BF16),
-            pltpu.VMEM((every, plan.heads * (NOPE + VDIM)), BF16),
-        ],
-        10**9,
-    )
-    g_gain, g_lat, g_lg = kernel_call(
-        latent_gradients,
-        [ranks, sent, dl_own, dl_other],
-        [shape((1, plan.wcol), F32), shape((plan.latent, plan.wcol), F32), shape((1, plan.ccol), F32)],
-        [
             pltpu.VMEM((every, plan.wcol), BF16),
             pltpu.VMEM((every, plan.latent), BF16),
             pltpu.VMEM((n, 1, plan.wcol), F32),

time: 138 us -> 139 us (level)
  waiting for transfers between devices: 56.5 us -> 67.7 us
  starting transfers between devices: 56.6 us -> 49.6 us
  local copies, waits for them, and re-layouts: 7.68 us -> 3.22 us
  Pallas kernels: 15.7 us -> 17.3 us
    ppermute x41 -> x45, waiting for transfers between devices: 46.9 us -> 57.1 us  [flipped(): return lax.ppermute(value, axis, [(i, i ^ bit) for i in range(count)])]
    ppermute x41 -> x45, starting transfers between devices: 52.2 us -> 47.1 us  [flipped(): return lax.ppermute(value, axis, [(i, i ^ bit) for i in range(count)])]
    unnamed x17 -> x18, local copies, waits for them, and re-layouts: 7 us -> 3.22 us
    ppermute x2, starting transfers between devices: 3.11 us -> 1.19 us  [token_shards(): sums.append(lax.ppermute(chip, 'tensor', pairs))]
    pallas_call x8 -> x11, Pallas kernels: 15.7 us -> 17.3 us  [kernel_call(): got = call(*ins)]
  transfers between devices with their start and end apart: 44 -> 48, of which waited for: 16 -> 24; matrix products, arithmetic and copies ran while one was open for 1% -> 0% of each run, Pallas kernels for 6% -> 6%
where the time goes in v1:
time: 139 us
  waiting for transfers between devices  67.7 us (49%)
  starting transfers between devices  49.6 us (36%)
  Pallas kernels  17.3 us (12%)
  local copies, waits for them, and re-layouts  3.22 us (2%)
    ppermute x45, waiting for transfers between devices, flipped(): return lax.ppermute(value, axis, [(i, i ^ bit) for i in range(count)])  57.1 us
    ppermute x45, starting transfers between devices, flipped(): return lax.ppermute(value, axis, [(i, i ^ bit) for i in range(count)])  47.1 us
    pallas_call x11, Pallas kernels, kernel_call(): got = call(*ins)  17.3 us
    ppermute x1, waiting for transfers between devices, token_shards(): lax.ppermute(dx, 'pipe', [(s, s - 1) for s in range(1, plan.n_pipe)])  5.56 us
    ppermute x2, waiting for transfers between devices, token_shards(): sums.append(lax.ppermute(chip, 'tensor', pairs))  5.01 us
    unnamed x18, local copies, waits for them, and re-layouts  3.22 us
  transfers between devices with their start and end apart: 48, of which 24 were waited for; matrix products, arithmetic and copies ran while one was open for 0% of the time, Pallas kernels for 6%

profile of v1, /device:TPU:0, one launch (start us, length us, event | category | flops | bytes accessed | tf_op | source)
XLA Modules:
  0.0 138.9 jit_solution(13900721562680249263)
XLA Ops:
  0.7 1.0 copy-done
  1.7 0.7 copy-done.7
  2.4 0.7 copy-done.8
  3.0 0.6 shard_map.146.refs_1_
  3.6 4.1 %collective-permute-start.4 = (bf16[160,256]{1,0:T(8,128)(2,1)S(1)}, bf16[160,256]{1,0:T(8,128)(2,1)S(1)}, u32[]{:S(2)}, u32[]{:S(2)}) collective-permute-start(bf16[160,256]{1,0:T(8,128)(2,1)S(1)} %shard_map.146.refs_1_), channel_id=1, source_target_pairs={{0,8},{4,12},{8,0},{12,4},{1,9},{5,13},{9,1},{13,5},{2,10},{6,14},... | collective-permute-start | bytes 245768 | tf_op jit(solution)/shard_map/ppermute | solution.py:596
  7.7 1.6 %collective-permute-start.3 = (bf16[160,256]{1,0:T(8,128)(2,1)S(1)}, bf16[160,256]{1,0:T(8,128)(2,1)S(1)}, u32[]{:S(2)}, u32[]{:S(2)}) collective-permute-start(bf16[160,256]{1,0:T(8,128)(2,1)S(1)} %shard_map.146.refs_1_), channel_id=1, source_target_pairs={{0,4},{4,0},{8,12},{12,8},{1,5},{5,1},{9,13},{13,9},{2,6},{6,2},{1... | collective-permute-start | bytes 245768 | tf_op jit(solution)/shard_map/ppermute | solution.py:596
  9.3 2.2 %collective-permute-done.4.refs_3_ = bf16[160,256]{1,0:T(8,128)(2,1)S(1)} collective-permute-done((bf16[160,256]{1,0:T(8,128)(2,1)S(1)}, bf16[160,256]{1,0:T(8,128)(2,1)S(1)}, u32[]{:S(2)}, u32[]{:S(2)}) %collective-permute-start.4) | collective-permute-done | bytes 81952 | tf_op jit(solution)/shard_map/ppermute | solution.py:596
  11.5 1.2 collective-permute-start.5
  12.7 3.2 %collective-permute-done.5.refs_4_ = bf16[160,256]{1,0:T(8,128)(2,1)S(1)} collective-permute-done((bf16[160,256]{1,0:T(8,128)(2,1)S(1)}, bf16[160,256]{1,0:T(8,128)(2,1)S(1)}, u32[]{:S(2)}, u32[]{:S(2)}) %collective-permute-start.5) | collective-permute-done | bytes 81952 | tf_op jit(solution)/shard_map/ppermute | solution.py:596
  15.9 0.6 shard_map.147.refs_6_
  16.5 1.9 %collective-permute-start.7 = (bf16[640,256]{1,0:T(8,128)(2,1)S(1)}, bf16[640,256]{1,0:T(8,128)(2,1)S(1)}, u32[]{:S(2)}, u32[]{:S(2)}) collective-permute-start(bf16[640,256]{1,0:T(8,128)(2,1)S(1)} %shard_map.147.refs_6_), channel_id=1, source_target_pairs={{0,2},{1,3},{2,0},{3,1},{4,6},{5,7},{6,4},{7,5},{8,10},{9,11},{10,... | collective-permute-start | bytes 983048 | tf_op jit(solution)/shard_map/ppermute | solution.py:596
  18.4 2.2 %collective-permute-start.10 = (bf16[128,512]{1,0:T(8,128)(2,1)}, bf16[128,512]{1,0:T(8,128)(2,1)S(1)}, u32[]{:S(2)}, u32[]{:S(2)}) collective-permute-start(bf16[128,512]{1,0:T(8,128)(2,1)} %bitcast.27), channel_id=1, source_target_pairs={{0,8},{4,12},{8,0},{12,4},{1,9},{5,13},{9,1},{13,5},{2,10},{6,14},... | collective-permute-start | bytes 393224 | tf_op jit(solution)/shard_map/ppermute | solution.py:596
  20.6 2.0 %collective-permute-start.9 = (bf16[128,512]{1,0:T(8,128)(2,1)}, bf16[128,512]{1,0:T(8,128)(2,1)S(1)}, u32[]{:S(2)}, u32[]{:S(2)}) collective-permute-start(bf16[128,512]{1,0:T(8,128)(2,1)} %bitcast.28), channel_id=1, source_target_pairs={{0,4},{4,0},{8,12},{12,8},{1,5},{5,1},{9,13},{13,9},{2,6},{6,2},{1... | collective-permute-start | bytes 393224 | tf_op jit(solution)/shard_map/ppermute | solution.py:596
  22.6 2.9 %collective-permute-start.13 = (bf16[256,256]{1,0:T(8,128)(2,1)}, bf16[256,256]{1,0:T(8,128)(2,1)S(1)}, u32[]{:S(2)}, u32[]{:S(2)}) collective-permute-start(bf16[256,256]{1,0:T(8,128)(2,1)} %bitcast.24), channel_id=1, source_target_pairs={{0,8},{4,12},{8,0},{12,4},{1,9},{5,13},{9,1},{13,5},{2,10},{6,14},... | collective-permute-start | bytes 393224 | tf_op jit(solution)/shard_map/ppermute | solution.py:596
  25.5 3.9 %collective-permute-done.10.refs_12_.refs_15_.refs_17_ = bf16[128,512]{1,0:T(8,128)(2,1)S(1)} collective-permute-done((bf16[128,512]{1,0:T(8,128)(2,1)}, bf16[128,512]{1,0:T(8,128)(2,1)S(1)}, u32[]{:S(2)}, u32[]{:S(2)}) %collective-permute-start.10) | collective-permute-done | bytes 131104 | tf_op jit(solution)/shard_map/ppermute | solution.py:596
  29.4 0.5 collective-permute-start.8
  29.9 5.4 %collective-permute-start = (bf16[256,384]{1,0:T(8,128)(2,1)}, bf16[256,384]{1,0:T(8,128)(2,1)S(1)}, u32[]{:S(2)}, u32[]{:S(2)}) collective-permute-start(bf16[256,384]{1,0:T(8,128)(2,1)} %bitcast.22), channel_id=1, source_target_pairs={{0,4},{4,0},{8,12},{12,8},{1,5},{5,1},{9,13},{13,9},{2,6},{6,2},{1... | collective-permute-start | bytes 589832 | tf_op jit(solution)/shard_map/ppermute | solution.py:596
  35.3 5.1 %collective-permute-done.13.refs_19_.refs_21_ = bf16[256,256]{1,0:T(8,128)(2,1)S(1)} collective-permute-done((bf16[256,256]{1,0:T(8,128)(2,1)}, bf16[256,256]{1,0:T(8,128)(2,1)S(1)}, u32[]{:S(2)}, u32[]{:S(2)}) %collective-permute-start.13) | collective-permute-done | bytes 131104 | tf_op jit(solution)/shard_map/ppermute | solution.py:596
  40.4 0.7 collective-permute-start.11
  41.2 1.3 collective-permute-start.2
  42.5 2.1 %collective-permute-done.refs_3_.refs_9_.refs_11_ = bf16[256,384]{1,0:T(8,128)(2,1)S(1)} collective-permute-done((bf16[256,384]{1,0:T(8,128)(2,1)}, bf16[256,384]{1,0:T(8,128)(2,1)S(1)}, u32[]{:S(2)}, u32[]{:S(2)}) %collective-permute-start) | collective-permute-done | bytes 196640 | tf_op jit(solution)/shard_map/ppermute | solution.py:596
  44.6 2.8 %collective-permute-done.11.refs_13_.refs_16_.refs_18_ = bf16[128,512]{1,0:T(8,128)(2,1)S(1)} collective-permute-done((bf16[128,512]{1,0:T(8,128)(2,1)S(1)}, bf16[128,512]{1,0:T(8,128)(2,1)S(1)}, u32[]{:S(2)}, u32[]{:S(2)}) %collective-permute-start.11) | collective-permute-done | bytes 131104 | tf_op jit(solution)/shard_map/ppermute | solution.py:596
  47.5 0.9 copy-done.4
  48.4 0.6 shard_map.144
  49.1 0.6 shard_map.145
  49.6 2.0 %collective-permute-done.2.refs_5_.refs_11_.refs_13_ = bf16[256,384]{1,0:T(8,128)(2,1)S(1)} collective-permute-done((bf16[256,384]{1,0:T(8,128)(2,1)S(1)}, bf16[256,384]{1,0:T(8,128)(2,1)S(1)}, u32[]{:S(2)}, u32[]{:S(2)}) %collective-permute-start.2) | collective-permute-done | bytes 196640 | tf_op jit(solution)/shard_map/ppermute | solution.py:596
  51.6 2.7 %shard_map.148 = (bf16[64,384]{1,0:T(8,128)(2,1)S(1)}, bf16[64,384]{1,0:T(8,128)(2,1)S(1)}, bf16[64,384]{1,0:T(8,128)(2,1)S(1)}, bf16[64,384]{1,0:T(8,128)(2,1)S...) custom-call(s32[3]{0:T(128)S(1)} %pad_add_fusion.refs_0_, ...), custom_call_target="tpu_custom_call" | custom-call | flops 500000000 | bytes 4194304 | tf_op jit(solution)/shard_map/pallas_call | solution.py:583
  54.4 2.8 %collective-permute-done.14.refs_20_.refs_22_ = bf16[256,256]{1,0:T(8,128)(2,1)S(1)} collective-permute-done((bf16[256,256]{1,0:T(8,128)(2,1)S(1)}, bf16[256,256]{1,0:T(8,128)(2,1)S(1)}, u32[]{:S(2)}, u32[]{:S(2)}) %collective-permute-start.14) | collective-permute-done | bytes 131104 | tf_op jit(solution)/shard_map/ppermute | solution.py:596
  57.2 2.7 %shard_map.149 = (bf16[64,1024]{1,0:T(8,128)(2,1)S(1)}, bf16[64,1024]{1,0:T(8,128)(2,1)S(1)}, bf16[64,1024]{1,0:T(8,128)(2,1)S(1)}) custom-call(s32[3]{0:T(128)S(1)} %pad_add_fusion.refs_0_, bf16[128,1024]{1,0:T(8,128)(2,1)S(1)} %get-tuple-element.45.refs_1_, bf16[128,960]{1,0:T(8,128)(2,1)S(1)} %get-tuple-element.50.refs_2_.refs_4_.refs_9_, ...), custom_call_target="tpu_custom_call" | custom-call | flops 1000000000 | bytes 4194304 | tf_op jit(solution)/shard_map/pallas_call | solution.py:583
  60.0 1.3 collective-permute-done.15
  61.4 0.6 collective-permute-start.16
  62.0 5.0 %collective-permute-done.16.refs_2_ = bf16[64,1024]{1,0:T(8,128)(2,1)S(1)} collective-permute-done((bf16[64,1024]{1,0:T(8,128)(2,1)S(1)}, bf16[64,1024]{1,0:T(8,128)(2,1)S(1)}, u32[]{:S(2)}, u32[]{:S(2)}) %collective-permute-start.16) | collective-permute-done | bytes 131104 | tf_op jit(solution)/shard_map/ppermute | solution.py:716
  67.0 0.8 shard_map.150
  67.7 1.3 collective-permute-start.17
  69.0 5.6 %collective-permute-done.17.refs_2_ = bf16[64,1024]{1,0:T(8,128)(2,1)S(1)} collective-permute-done((bf16[64,1024]{1,0:T(8,128)(2,1)S(1)}, bf16[64,1024]{1,0:T(8,128)(2,1)S(1)}, u32[]{:S(2)}, u32[]{:S(2)}) %collective-permute-start.17) | collective-permute-done | bytes 131104 | tf_op jit(solution)/shard_map/ppermute | solution.py:731
  74.6 1.3 collective-permute-done.18.refs_3_
  76.0 2.8 %shard_map.151 = (bf16[64,1664]{1,0:T(8,128)(2,1)S(1)}, bf16[64,1664]{1,0:T(8,128)(2,1)S(1)}, bf16[64,1024]{1,0:T(8,128)(2,1)S(1)}, bf16[128,384]{1,0:T(8,128)(2...) custom-call(s32[3]{0:T(128)S(1)} %pad_add_fusion.refs_0_, ...), custom_call_target="tpu_custom_call" | custom-call | flops 1000000000 | bytes 4194304 | tf_op jit(solution)/shard_map/pallas_call | solution.py:583
  79.0 1.6 %collective-permute-start.29 = (bf16[128,960]{1,0:T(8,128)(2,1)S(1)}, bf16[128,960]{1,0:T(8,128)(2,1)S(1)}, u32[]{:S(2)}, u32[]{:S(2)}) collective-permute-start(bf16[128,960]{1,0:T(8,128)(2,1)S(1)} %get-tuple-element.50.refs_2_.refs_4_.refs_9_), channel_id=1, source_target_pairs={{0,8},{4,12},{8,0},{12,4},{1,9},{5,13},{9,1},{13,5},{2,10},{6,14},... | collective-permute-start | bytes 737288 | tf_op jit(solution)/shard_map/ppermute | solution.py:596
  80.6 0.6 collective-permute-start.20
  81.2 2.5 %collective-permute-start.28 = (bf16[128,960]{1,0:T(8,128)(2,1)S(1)}, bf16[128,960]{1,0:T(8,128)(2,1)S(1)}, u32[]{:S(2)}, u32[]{:S(2)}) collective-permute-start(bf16[128,960]{1,0:T(8,128)(2,1)S(1)} %get-tuple-element.50.refs_2_.refs_4_.refs_9_), channel_id=1, source_target_pairs={{0,4},{4,0},{8,12},{12,8},{1,5},{5,1},{9,13},{13,9},{2,6},{6,2},{1... | collective-permute-start | bytes 737288 | tf_op jit(solution)/shard_map/ppermute | solution.py:596
  83.7 10.5 %collective-permute-done.29.refs_11_ = bf16[128,960]{1,0:T(8,128)(2,1)S(1)} collective-permute-done((bf16[128,960]{1,0:T(8,128)(2,1)S(1)}, bf16[128,960]{1,0:T(8,128)(2,1)S(1)}, u32[]{:S(2)}, u32[]{:S(2)}) %collective-permute-start.29) | collective-permute-done | bytes 245792 | tf_op jit(solution)/shard_map/ppermute | solution.py:596
  94.1 2.0 %collective-permute-start.21 = (bf16[64,384]{1,0:T(8,128)(2,1)S(1)}, bf16[64,384]{1,0:T(8,128)(2,1)S(1)}, u32[]{:S(2)}, u32[]{:S(2)}) collective-permute-start(bf16[64,384]{1,0:T(8,128)(2,1)S(1)} %get-tuple-element.68), channel_id=1, source_target_pairs={{0,4},{4,0},{8,12},{12,8},{1,5},{5,1},{9,13},{13,9},{2,6},{6,2},{1... | collective-permute-start | bytes 147464 | tf_op jit(solution)/shard_map/ppermute | solution.py:596
  96.2 1.0 collective-permute-start.22
  97.2 6.7 %collective-permute-done.21.refs_2_ = bf16[64,384]{1,0:T(8,128)(2,1)S(1)} collective-permute-done((bf16[64,384]{1,0:T(8,128)(2,1)S(1)}, bf16[64,384]{1,0:T(8,128)(2,1)S(1)}, u32[]{:S(2)}, u32[]{:S(2)}) %collective-permute-start.21) | collective-permute-done | bytes 49184 | tf_op jit(solution)/shard_map/ppermute | solution.py:596
  103.9 3.0 %collective-permute-start.23 = (bf16[64,384]{1,0:T(8,128)(2,1)S(1)}, bf16[64,384]{1,0:T(8,128)(2,1)S(1)}, u32[]{:S(2)}, u32[]{:S(2)}) collective-permute-start(bf16[64,384]{1,0:T(8,128)(2,1)S(1)} %get-tuple-element.70), channel_id=1, source_target_pairs={{0,12},{4,8},{8,4},{12,0},{1,13},{5,9},{9,5},{13,1},{2,14},{6,10},... | collective-permute-start | bytes 147464 | tf_op jit(solution)/shard_map/ppermute | solution.py:596
  106.9 2.8 %collective-permute-done.23.refs_4_ = bf16[64,384]{1,0:T(8,128)(2,1)S(1)} collective-permute-done((bf16[64,384]{1,0:T(8,128)(2,1)S(1)}, bf16[64,384]{1,0:T(8,128)(2,1)S(1)}, u32[]{:S(2)}, u32[]{:S(2)}) %collective-permute-start.23) | collective-permute-done | bytes 49184 | tf_op jit(solution)/shard_map/ppermute | solution.py:596
  109.8 0.5 collective-permute-start.26
  110.3 0.7 collective-permute-done.25.refs_6_
  111.2 1.4 %shard_map.152 = (bf16[32,1024]{1,0:T(8,128)(2,1)}, bf16[64,640]{1,0:T(8,128)(2,1)S(1)}) custom-call(s32[3]{0:T(128)S(1)} %pad_add_fusion.refs_0_, bf16[64,1664]{1,0:T(8,128)(2,1)S(1)} %add.7.refs_1_, bf16[64,1664]{1,0:T(8,128)(2,1)S(1)} %collective-permute-done.20.refs_2_, bf16[64,1024]{1,0:T(8,128)(2,1)S(1)} %get-tuple-element.65.refs_3_, ...), custom_call_target="tpu_custom_call" | custom-call | flops 1000000 | bytes 4194304 | tf_op jit(solution)/shard_map/pallas_call | solution.py:583
  112.6 2.8 %collective-permute-start.39 = (bf16[64,640]{1,0:T(8,128)(2,1)S(1)}, bf16[64,640]{1,0:T(8,128)(2,1)S(1)}, u32[]{:S(2)}, u32[]{:S(2)}) collective-permute-start(bf16[64,640]{1,0:T(8,128)(2,1)S(1)} %get-tuple-element.75.refs_21_), channel_id=1, source_target_pairs={{0,8},{4,12},{8,0},{12,4},{1,9},{5,13},{9,1},{13,5},{2,10},{6,14},... | collective-permute-start | bytes 245768 | tf_op jit(solution)/shard_map/ppermute | solution.py:596
  115.4 0.8 collective-permute-start.31
  116.2 2.8 %collective-permute-start.32 = (bf16[64,256]{1,0:T(8,128)(2,1)S(1)}, bf16[64,256]{1,0:T(8,128)(2,1)S(1)}, u32[]{:S(2)}, u32[]{:S(2)}) collective-permute-start(bf16[64,256]{1,0:T(8,128)(2,1)S(1)} %get-tuple-element.73), channel_id=1, source_target_pairs={{0,8},{4,12},{8,0},{12,4},{1,9},{5,13},{9,1},{13,5},{2,10},{6,14},... | collective-permute-start | bytes 98312 | tf_op jit(solution)/shard_map/ppermute | solution.py:596
  119.0 0.8 collective-permute-start.33
  119.8 0.5 collective-permute-done.31.refs_14_
  120.3 4.5 %collective-permute-done.32.refs_15_ = bf16[64,256]{1,0:T(8,128)(2,1)S(1)} collective-permute-done((bf16[64,256]{1,0:T(8,128)(2,1)S(1)}, bf16[64,256]{1,0:T(8,128)(2,1)S(1)}, u32[]{:S(2)}, u32[]{:S(2)}) %collective-permute-start.32) | collective-permute-done | bytes 32800 | tf_op jit(solution)/shard_map/ppermute | solution.py:596
  124.9 2.0 %collective-permute-start.47 = (bf16[128,384]{1,0:T(8,128)(2,1)S(1)}, bf16[128,384]{1,0:T(8,128)(2,1)S(1)}, u32[]{:S(2)}, u32[]{:S(2)}) collective-permute-start(bf16[128,384]{1,0:T(8,128)(2,1)S(1)} %collective-permute-done.46.refs_15_), channel_id=1, source_target_pairs={{0,4},{4,0},{8,12},{12,8},{1,5},{5,1},{9,13},{13,9},{2,6},{6,2},{1... | collective-permute-start | bytes 294920 | tf_op jit(solution)/shard_map/ppermute | solution.py:596
  127.0 2.0 %collective-permute-start.40 = (bf16[64,640]{1,0:T(8,128)(2,1)S(1)}, bf16[64,640]{1,0:T(8,128)(2,1)S(1)}, u32[]{:S(2)}, u32[]{:S(2)}) collective-permute-start(bf16[64,640]{1,0:T(8,128)(2,1)S(1)} %collective-permute-done.39.refs_23_), channel_id=1, source_target_pairs={{0,4},{4,0},{8,12},{12,8},{1,5},{5,1},{9,13},{13,9},{2,6},{6,2},{1... | collective-permute-start | bytes 245768 | tf_op jit(solution)/shard_map/ppermute | solution.py:596
  128.9 1.2 collective-permute-done.35.refs_18_
  130.3 1.0 collective-permute-done.36.refs_19_
  131.9 0.5 collective-permute-done.47.refs_16_
  132.3 0.9 collective-permute-done.38.refs_22_
  133.2 0.9 collective-permute-done.40.refs_24_
  134.1 2.7 %shard_map.154 = (f32[256,384]{1,0:T(8,128)}, f32[128,512]{1,0:T(8,128)}) custom-call(s32[3]{0:T(128)S(1)} %pad_add_fusion.refs_0_, bf16[64,384]{1,0:T(8,128)(2,1)S(1)} %get-tuple-element.67.refs_1_, bf16[64,384]{1,0:T(8,128)(2,1)S(1)} %collective-permute-done.21.refs_2_, bf16[64,384]{1,0:T(8,128)(2,1)S(1)} %collective-permute-done.22.refs_3_, ...), custom_call_target="tpu_custom_call" | custom-call | flops 1000000000 | bytes 4194304 | tf_op jit(solution)/shard_map/pallas_call | solution.py:583
  136.8 2.0 %shard_map.153 = (f32[1,256]{1,0:T(1,128)}, f32[576,256]{1,0:T(8,128)}, f32[1,128]{1,0:T(1,128)}, f32[256,256]{1,0:T(8,128)}) custom-call(s32[3]{0:T(128)S(1)} %pad_add_fusion.refs_0_, bf16[64,384]{1,0:T(8,128)(2,1)S(1)} %get-tuple-element.67.refs_1_, bf16[64,384]{1,0:T(8,128)(2,1)S(1)} %collective-permute-done.21.refs_2_, ...), custom_call_target="tpu_custom_call" | custom-call | flops 1000000000 | bytes 4194304 | tf_op jit(solution)/shard_map/pallas_call | solution.py:583
  (64 shorter events, 1.8 us)
Async XLA Ops:
  0.7 1.0 copy-start
  1.7 0.7 copy-start.7
  2.4 0.7 copy-start.8
  3.0 44.5 %copy-start.1 = (bf16[2,64,1024]{2,1,0:T(8,128)(2,1)S(1)}, bf16[2,64,1024]{2,1,0:T(8,128)(2,1)}, u32[]{:S(2)}) copy-start(bf16[2,64,1024]{2,1,0:T(8,128)(2,1)} %param.10) | copy-start | bytes 786436
  3.0 46.0 %copy-start.2 = (bf16[1,2,64,1024]{3,2,1,0:T(8,128)(2,1)S(1)}, bf16[1,2,64,1024]{3,2,1,0:T(8,128)(2,1)}, u32[]{:S(2)}) copy-start(bf16[1,2,64,1024]{3,2,1,0:T(8,128)(2,1)} %param.9) | copy-start | bytes 786436
  3.0 46.0 %copy-start.3 = (bf16[1,256,384]{2,1,0:T(8,128)(2,1)S(1)}, bf16[1,256,384]{2,1,0:T(8,128)(2,1)}, u32[]{:S(2)}) copy-start(bf16[1,256,384]{2,1,0:T(8,128)(2,1)} %param.12) | copy-start | bytes 589828
  3.0 46.0 %copy-start.5 = (bf16[1,128,512]{2,1,0:T(8,128)(2,1)S(1)}, bf16[1,128,512]{2,1,0:T(8,128)(2,1)}, u32[]{:S(2)}) copy-start(bf16[1,128,512]{2,1,0:T(8,128)(2,1)} %param.15) | copy-start | bytes 393220
  3.0 46.0 %copy-start.6 = (f32[128,128]{1,0:T(8,128)S(1)}, f32[128,128]{1,0:T(8,128)}, u32[]{:S(2)}) copy-start(f32[128,128]{1,0:T(8,128)} %constant.17.clone.refs_4_) | copy-start | bytes 196612
  3.6 7.9 %collective-permute-start.4 = (bf16[160,256]{1,0:T(8,128)(2,1)S(1)}, bf16[160,256]{1,0:T(8,128)(2,1)S(1)}, u32[]{:S(2)}, u32[]{:S(2)}) collective-permute-start(bf16[160,256]{1,0:T(8,128)(2,1)S(1)} %shard_map.146.refs_1_), channel_id=1, source_target_pairs={{0,8},{4,12},{8,0},{12,4},{1,9},{5,13},{9,1},{13,5},{2,10},{6,14},... | collective-permute-start | bytes 245768 | tf_op jit(solution)/shard_map/ppermute | solution.py:596
  7.7 5.0 %collective-permute-start.3 = (bf16[160,256]{1,0:T(8,128)(2,1)S(1)}, bf16[160,256]{1,0:T(8,128)(2,1)S(1)}, u32[]{:S(2)}, u32[]{:S(2)}) collective-permute-start(bf16[160,256]{1,0:T(8,128)(2,1)S(1)} %shard_map.146.refs_1_), channel_id=1, source_target_pairs={{0,4},{4,0},{8,12},{12,8},{1,5},{5,1},{9,13},{13,9},{2,6},{6,2},{1... | collective-permute-start | bytes 245768 | tf_op jit(solution)/shard_map/ppermute | solution.py:596
  11.5 4.4 %collective-permute-start.5 = (bf16[160,256]{1,0:T(8,128)(2,1)S(1)}, bf16[160,256]{1,0:T(8,128)(2,1)S(1)}, u32[]{:S(2)}, u32[]{:S(2)}) collective-permute-start(bf16[160,256]{1,0:T(8,128)(2,1)S(1)} %collective-permute-done.4.refs_3_), channel_id=1, source_target_pairs={{0,4},{4,0},{8,12},{12,8},{1,5},{5,1},{9,13},{13,9},{2,6},{6,2},{1... | collective-permute-start | bytes 245768 | tf_op jit(solution)/shard_map/ppermute | solution.py:596
  16.5 12.9 %collective-permute-start.7 = (bf16[640,256]{1,0:T(8,128)(2,1)S(1)}, bf16[640,256]{1,0:T(8,128)(2,1)S(1)}, u32[]{:S(2)}, u32[]{:S(2)}) collective-permute-start(bf16[640,256]{1,0:T(8,128)(2,1)S(1)} %shard_map.147.refs_6_), channel_id=1, source_target_pairs={{0,2},{1,3},{2,0},{3,1},{4,6},{5,7},{6,4},{7,5},{8,10},{9,11},{10,... | collective-permute-start | bytes 983048 | tf_op jit(solution)/shard_map/ppermute | solution.py:596
  18.4 11.0 %collective-permute-start.10 = (bf16[128,512]{1,0:T(8,128)(2,1)}, bf16[128,512]{1,0:T(8,128)(2,1)S(1)}, u32[]{:S(2)}, u32[]{:S(2)}) collective-permute-start(bf16[128,512]{1,0:T(8,128)(2,1)} %bitcast.27), channel_id=1, source_target_pairs={{0,8},{4,12},{8,0},{12,4},{1,9},{5,13},{9,1},{13,5},{2,10},{6,14},... | collective-permute-start | bytes 393224 | tf_op jit(solution)/shard_map/ppermute | solution.py:596
  20.6 9.3 %collective-permute-start.9 = (bf16[128,512]{1,0:T(8,128)(2,1)}, bf16[128,512]{1,0:T(8,128)(2,1)S(1)}, u32[]{:S(2)}, u32[]{:S(2)}) collective-permute-start(bf16[128,512]{1,0:T(8,128)(2,1)} %bitcast.28), channel_id=1, source_target_pairs={{0,4},{4,0},{8,12},{12,8},{1,5},{5,1},{9,13},{13,9},{2,6},{6,2},{1... | collective-permute-start | bytes 393224 | tf_op jit(solution)/shard_map/ppermute | solution.py:596
  22.6 18.6 %collective-permute-start.1 = (bf16[256,384]{1,0:T(8,128)(2,1)}, bf16[256,384]{1,0:T(8,128)(2,1)S(1)}, u32[]{:S(2)}, u32[]{:S(2)}) collective-permute-start(bf16[256,384]{1,0:T(8,128)(2,1)} %bitcast.21), channel_id=1, source_target_pairs={{0,8},{4,12},{8,0},{12,4},{1,9},{5,13},{9,1},{13,5},{2,10},{6,14},... | collective-permute-start | bytes 589832 | tf_op jit(solution)/shard_map/ppermute | solution.py:596
  22.6 17.8 %collective-permute-start.13 = (bf16[256,256]{1,0:T(8,128)(2,1)}, bf16[256,256]{1,0:T(8,128)(2,1)S(1)}, u32[]{:S(2)}, u32[]{:S(2)}) collective-permute-start(bf16[256,256]{1,0:T(8,128)(2,1)} %bitcast.24), channel_id=1, source_target_pairs={{0,8},{4,12},{8,0},{12,4},{1,9},{5,13},{9,1},{13,5},{2,10},{6,14},... | collective-permute-start | bytes 393224 | tf_op jit(solution)/shard_map/ppermute | solution.py:596
  29.4 22.2 %collective-permute-start.6 = (bf16[640,256]{1,0:T(8,128)(2,1)S(1)}, bf16[640,256]{1,0:T(8,128)(2,1)S(1)}, u32[]{:S(2)}, u32[]{:S(2)}) collective-permute-start(bf16[640,256]{1,0:T(8,128)(2,1)S(1)} %shard_map.147.refs_6_), channel_id=1, source_target_pairs={{0,1},{1,0},{2,3},{3,2},{4,5},{5,4},{6,7},{7,6},{8,9},{9,8},{10,11... | collective-permute-start | bytes 983048 | tf_op jit(solution)/shard_map/ppermute | solution.py:596
  29.4 22.2 %collective-permute-start.8 = (bf16[640,256]{1,0:T(8,128)(2,1)S(1)}, bf16[640,256]{1,0:T(8,128)(2,1)S(1)}, u32[]{:S(2)}, u32[]{:S(2)}) collective-permute-start(bf16[640,256]{1,0:T(8,128)(2,1)S(1)} %collective-permute-done.7.refs_8_), channel_id=1, source_target_pairs={{0,1},{1,0},{2,3},{3,2},{4,5},{5,4},{6,7},{7,6},{8,9},{9,8},{10,11... | collective-permute-start | bytes 983048 | tf_op jit(solution)/shard_map/ppermute | solution.py:596
  29.9 14.7 %collective-permute-start = (bf16[256,384]{1,0:T(8,128)(2,1)}, bf16[256,384]{1,0:T(8,128)(2,1)S(1)}, u32[]{:S(2)}, u32[]{:S(2)}) collective-permute-start(bf16[256,384]{1,0:T(8,128)(2,1)} %bitcast.22), channel_id=1, source_target_pairs={{0,4},{4,0},{8,12},{12,8},{1,5},{5,1},{9,13},{13,9},{2,6},{6,2},{1... | collective-permute-start | bytes 589832 | tf_op jit(solution)/shard_map/ppermute | solution.py:596
  40.4 7.0 %collective-permute-start.11 = (bf16[128,512]{1,0:T(8,128)(2,1)S(1)}, bf16[128,512]{1,0:T(8,128)(2,1)S(1)}, u32[]{:S(2)}, u32[]{:S(2)}) collective-permute-start(bf16[128,512]{1,0:T(8,128)(2,1)S(1)} %collective-permute-done.10.refs_12_.refs_15_.refs_17_), channel_id=1, source_target_pairs={{0,4},{4,0},{8,12},{12,8},{1,5},{5,1},{9,13},{13,9},{2,6},{6,2},{1... | collective-permute-start | bytes 393224 | tf_op jit(solution)/shard_map/ppermute | solution.py:596
  41.2 10.5 %collective-permute-start.2 = (bf16[256,384]{1,0:T(8,128)(2,1)S(1)}, bf16[256,384]{1,0:T(8,128)(2,1)S(1)}, u32[]{:S(2)}, u32[]{:S(2)}) collective-permute-start(bf16[256,384]{1,0:T(8,128)(2,1)S(1)} %collective-permute-done.1.refs_4_.refs_10_.refs_12_), channel_id=1, source_target_pairs={{0,4},{4,0},{8,12},{12,8},{1,5},{5,1},{9,13},{13,9},{2,6},{6,2},{1... | collective-permute-start | bytes 589832 | tf_op jit(solution)/shard_map/ppermute | solution.py:596
  44.6 9.8 %collective-permute-start.12 = (bf16[256,256]{1,0:T(8,128)(2,1)}, bf16[256,256]{1,0:T(8,128)(2,1)S(1)}, u32[]{:S(2)}, u32[]{:S(2)}) collective-permute-start(bf16[256,256]{1,0:T(8,128)(2,1)} %bitcast.25), channel_id=1, source_target_pairs={{0,4},{4,0},{8,12},{12,8},{1,5},{5,1},{9,13},{13,9},{2,6},{6,2},{1... | collective-permute-start | bytes 393224 | tf_op jit(solution)/shard_map/ppermute | solution.py:596
  47.4 9.8 %collective-permute-start.14 = (bf16[256,256]{1,0:T(8,128)(2,1)S(1)}, bf16[256,256]{1,0:T(8,128)(2,1)S(1)}, u32[]{:S(2)}, u32[]{:S(2)}) collective-permute-start(bf16[256,256]{1,0:T(8,128)(2,1)S(1)} %collective-permute-done.13.refs_19_.refs_21_), channel_id=1, source_target_pairs={{0,4},{4,0},{8,12},{12,8},{1,5},{5,1},{9,13},{13,9},{2,6},{6,2},{1... | collective-permute-start | bytes 393224 | tf_op jit(solution)/shard_map/ppermute | solution.py:596
  47.5 0.9 copy-start.4
  59.9 1.4 %collective-permute-start.15 = (bf16[64,1024]{1,0:T(8,128)(2,1)S(1)}, bf16[64,1024]{1,0:T(8,128)(2,1)S(1)}, u32[]{:S(2)}, u32[]{:S(2)}) collective-permute-start(bf16[64,1024]{1,0:T(8,128)(2,1)S(1)} %get-tuple-element.59), channel_id=1, source_target_pairs={{0,1},{1,0},{2,3},{3,2},{4,5},{5,4},{6,7},{7,6},{8,9},{9,8},{10,11... | collective-permute-start | bytes 393224 | tf_op jit(solution)/shard_map/ppermute | solution.py:596
  61.4 5.6 %collective-permute-start.16 = (bf16[64,1024]{1,0:T(8,128)(2,1)S(1)}, bf16[64,1024]{1,0:T(8,128)(2,1)S(1)}, u32[]{:S(2)}, u32[]{:S(2)}) collective-permute-start(bf16[64,1024]{1,0:T(8,128)(2,1)S(1)} %add.6.refs_1_), channel_id=1, source_target_pairs={{0,2},{1,3},{2,0},{3,1},{4,6},{5,7},{6,4},{7,5},{8,10},{9,11},{10,... | collective-permute-start | bytes 393224 | tf_op jit(solution)/shard_map/ppermute | solution.py:716
  67.7 6.9 %collective-permute-start.17 = (bf16[64,1024]{1,0:T(8,128)(2,1)S(1)}, bf16[64,1024]{1,0:T(8,128)(2,1)S(1)}, u32[]{:S(2)}, u32[]{:S(2)}) collective-permute-start(bf16[64,1024]{1,0:T(8,128)(2,1)S(1)} %shard_map.150), channel_id=1, source_target_pairs={{16,0},{17,1},{18,2},{19,3},{20,4},{21,5},{22,6},{23,7},{24,8},{25... | collective-permute-start | bytes 393224 | tf_op jit(solution)/shard_map/ppermute | solution.py:731
  74.6 1.3 collective-permute-start.18
  78.7 1.8 %collective-permute-start.19 = (bf16[64,1664]{1,0:T(8,128)(2,1)S(1)}, bf16[64,1664]{1,0:T(8,128)(2,1)S(1)}, u32[]{:S(2)}, u32[]{:S(2)}) collective-permute-start(bf16[64,1664]{1,0:T(8,128)(2,1)S(1)} %get-tuple-element.64), channel_id=1, source_target_pairs={{0,1},{1,0},{2,3},{3,2},{4,5},{5,4},{6,7},{7,6},{8,9},{9,8},{10,11... | collective-permute-start | bytes 638984 | tf_op jit(solution)/shard_map/ppermute | solution.py:596
  79.0 15.2 %collective-permute-start.29 = (bf16[128,960]{1,0:T(8,128)(2,1)S(1)}, bf16[128,960]{1,0:T(8,128)(2,1)S(1)}, u32[]{:S(2)}, u32[]{:S(2)}) collective-permute-start(bf16[128,960]{1,0:T(8,128)(2,1)S(1)} %get-tuple-element.50.refs_2_.refs_4_.refs_9_), channel_id=1, source_target_pairs={{0,8},{4,12},{8,0},{12,4},{1,9},{5,13},{9,1},{13,5},{2,10},{6,14},... | collective-permute-start | bytes 737288 | tf_op jit(solution)/shard_map/ppermute | solution.py:596
  80.6 30.4 %collective-permute-start.20 = (bf16[64,1664]{1,0:T(8,128)(2,1)S(1)}, bf16[64,1664]{1,0:T(8,128)(2,1)S(1)}, u32[]{:S(2)}, u32[]{:S(2)}) collective-permute-start(bf16[64,1664]{1,0:T(8,128)(2,1)S(1)} %add.7.refs_1_), channel_id=1, source_target_pairs={{0,2},{1,3},{2,0},{3,1},{4,6},{5,7},{6,4},{7,5},{8,10},{9,11},{10,... | collective-permute-start | bytes 638984 | tf_op jit(solution)/shard_map/ppermute | solution.py:716
  81.2 35.0 %collective-permute-start.28 = (bf16[128,960]{1,0:T(8,128)(2,1)S(1)}, bf16[128,960]{1,0:T(8,128)(2,1)S(1)}, u32[]{:S(2)}, u32[]{:S(2)}) collective-permute-start(bf16[128,960]{1,0:T(8,128)(2,1)S(1)} %get-tuple-element.50.refs_2_.refs_4_.refs_9_), channel_id=1, source_target_pairs={{0,4},{4,0},{8,12},{12,8},{1,5},{5,1},{9,13},{13,9},{2,6},{6,2},{1... | collective-permute-start | bytes 737288 | tf_op jit(solution)/shard_map/ppermute | solution.py:596
  94.1 24.9 %collective-permute-start.30 = (bf16[128,960]{1,0:T(8,128)(2,1)S(1)}, bf16[128,960]{1,0:T(8,128)(2,1)S(1)}, u32[]{:S(2)}, u32[]{:S(2)}) collective-permute-start(bf16[128,960]{1,0:T(8,128)(2,1)S(1)} %collective-permute-done.29.refs_11_), channel_id=1, source_target_pairs={{0,4},{4,0},{8,12},{12,8},{1,5},{5,1},{9,13},{13,9},{2,6},{6,2},{1... | collective-permute-start | bytes 737288 | tf_op jit(solution)/shard_map/ppermute | solution.py:596
  94.1 9.8 %collective-permute-start.21 = (bf16[64,384]{1,0:T(8,128)(2,1)S(1)}, bf16[64,384]{1,0:T(8,128)(2,1)S(1)}, u32[]{:S(2)}, u32[]{:S(2)}) collective-permute-start(bf16[64,384]{1,0:T(8,128)(2,1)S(1)} %get-tuple-element.68), channel_id=1, source_target_pairs={{0,4},{4,0},{8,12},{12,8},{1,5},{5,1},{9,13},{13,9},{2,6},{6,2},{1... | collective-permute-start | bytes 147464 | tf_op jit(solution)/shard_map/ppermute | solution.py:596
  96.2 10.8 %collective-permute-start.22 = (bf16[64,384]{1,0:T(8,128)(2,1)S(1)}, bf16[64,384]{1,0:T(8,128)(2,1)S(1)}, u32[]{:S(2)}, u32[]{:S(2)}) collective-permute-start(bf16[64,384]{1,0:T(8,128)(2,1)S(1)} %get-tuple-element.69), channel_id=1, source_target_pairs={{0,8},{4,12},{8,0},{12,4},{1,9},{5,13},{9,1},{13,5},{2,10},{6,14},... | collective-permute-start | bytes 147464 | tf_op jit(solution)/shard_map/ppermute | solution.py:596
  103.9 5.9 %collective-permute-start.23 = (bf16[64,384]{1,0:T(8,128)(2,1)S(1)}, bf16[64,384]{1,0:T(8,128)(2,1)S(1)}, u32[]{:S(2)}, u32[]{:S(2)}) collective-permute-start(bf16[64,384]{1,0:T(8,128)(2,1)S(1)} %get-tuple-element.70), channel_id=1, source_target_pairs={{0,12},{4,8},{8,4},{12,0},{1,13},{5,9},{9,5},{13,1},{2,14},{6,10},... | collective-permute-start | bytes 147464 | tf_op jit(solution)/shard_map/ppermute | solution.py:596
  106.9 2.9 %collective-permute-start.24 = (bf16[64,384]{1,0:T(8,128)(2,1)S(1)}, bf16[64,384]{1,0:T(8,128)(2,1)S(1)}, u32[]{:S(2)}, u32[]{:S(2)}) collective-permute-start(bf16[64,384]{1,0:T(8,128)(2,1)S(1)} %get-tuple-element.67.refs_1_), channel_id=1, source_target_pairs={{0,1},{1,0},{2,3},{3,2},{4,5},{5,4},{6,7},{7,6},{8,9},{9,8},{10,11... | collective-permute-start | bytes 147464 | tf_op jit(solution)/shard_map/ppermute | solution.py:596
  109.8 1.2 collective-permute-start.25
  109.8 2.8 %collective-permute-start.26 = (bf16[64,384]{1,0:T(8,128)(2,1)S(1)}, bf16[64,384]{1,0:T(8,128)(2,1)S(1)}, u32[]{:S(2)}, u32[]{:S(2)}) collective-permute-start(bf16[64,384]{1,0:T(8,128)(2,1)S(1)} %collective-permute-done.22.refs_3_), channel_id=1, source_target_pairs={{0,1},{1,0},{2,3},{3,2},{4,5},{5,4},{6,7},{7,6},{8,9},{9,8},{10,11... | collective-permute-start | bytes 147464 | tf_op jit(solution)/shard_map/ppermute | solution.py:596
  111.0 13.8 %collective-permute-start.46 = (bf16[128,384]{1,0:T(8,128)(2,1)S(1)}, bf16[128,384]{1,0:T(8,128)(2,1)S(1)}, u32[]{:S(2)}, u32[]{:S(2)}) collective-permute-start(bf16[128,384]{1,0:T(8,128)(2,1)S(1)} %get-tuple-element.77.refs_13_), channel_id=1, source_target_pairs={{0,8},{4,12},{8,0},{12,4},{1,9},{5,13},{9,1},{13,5},{2,10},{6,14},... | collective-permute-start | bytes 294920 | tf_op jit(solution)/shard_map/ppermute | solution.py:596
  111.0 4.4 %collective-permute-start.27 = (bf16[64,384]{1,0:T(8,128)(2,1)S(1)}, bf16[64,384]{1,0:T(8,128)(2,1)S(1)}, u32[]{:S(2)}, u32[]{:S(2)}) collective-permute-start(bf16[64,384]{1,0:T(8,128)(2,1)S(1)} %collective-permute-done.23.refs_4_), channel_id=1, source_target_pairs={{0,1},{1,0},{2,3},{3,2},{4,5},{5,4},{6,7},{7,6},{8,9},{9,8},{10,11... | collective-permute-start | bytes 147464 | tf_op jit(solution)/shard_map/ppermute | solution.py:596
  112.6 14.3 %collective-permute-start.39 = (bf16[64,640]{1,0:T(8,128)(2,1)S(1)}, bf16[64,640]{1,0:T(8,128)(2,1)S(1)}, u32[]{:S(2)}, u32[]{:S(2)}) collective-permute-start(bf16[64,640]{1,0:T(8,128)(2,1)S(1)} %get-tuple-element.75.refs_21_), channel_id=1, source_target_pairs={{0,8},{4,12},{8,0},{12,4},{1,9},{5,13},{9,1},{13,5},{2,10},{6,14},... | collective-permute-start | bytes 245768 | tf_op jit(solution)/shard_map/ppermute | solution.py:596
  115.4 4.9 %collective-permute-start.31 = (bf16[64,256]{1,0:T(8,128)(2,1)S(1)}, bf16[64,256]{1,0:T(8,128)(2,1)S(1)}, u32[]{:S(2)}, u32[]{:S(2)}) collective-permute-start(bf16[64,256]{1,0:T(8,128)(2,1)S(1)} %get-tuple-element.72), channel_id=1, source_target_pairs={{0,4},{4,0},{8,12},{12,8},{1,5},{5,1},{9,13},{13,9},{2,6},{6,2},{1... | collective-permute-start | bytes 98312 | tf_op jit(solution)/shard_map/ppermute | solution.py:596
  116.2 8.6 %collective-permute-start.32 = (bf16[64,256]{1,0:T(8,128)(2,1)S(1)}, bf16[64,256]{1,0:T(8,128)(2,1)S(1)}, u32[]{:S(2)}, u32[]{:S(2)}) collective-permute-start(bf16[64,256]{1,0:T(8,128)(2,1)S(1)} %get-tuple-element.73), channel_id=1, source_target_pairs={{0,8},{4,12},{8,0},{12,4},{1,9},{5,13},{9,1},{13,5},{2,10},{6,14},... | collective-permute-start | bytes 98312 | tf_op jit(solution)/shard_map/ppermute | solution.py:596
  119.0 7.9 %collective-permute-start.33 = (bf16[64,256]{1,0:T(8,128)(2,1)S(1)}, bf16[64,256]{1,0:T(8,128)(2,1)S(1)}, u32[]{:S(2)}, u32[]{:S(2)}) collective-permute-start(bf16[64,256]{1,0:T(8,128)(2,1)S(1)} %get-tuple-element.74), channel_id=1, source_target_pairs={{0,12},{4,8},{8,4},{12,0},{1,13},{5,9},{9,5},{13,1},{2,14},{6,10},... | collective-permute-start | bytes 98312 | tf_op jit(solution)/shard_map/ppermute | solution.py:596
  120.3 8.6 %collective-permute-start.34 = (bf16[64,256]{1,0:T(8,128)(2,1)S(1)}, bf16[64,256]{1,0:T(8,128)(2,1)S(1)}, u32[]{:S(2)}, u32[]{:S(2)}) collective-permute-start(bf16[64,256]{1,0:T(8,128)(2,1)S(1)} %get-tuple-element.71.refs_13_), channel_id=1, source_target_pairs={{0,1},{1,0},{2,3},{3,2},{4,5},{5,4},{6,7},{7,6},{8,9},{9,8},{10,11... | collective-permute-start | bytes 98312 | tf_op jit(solution)/shard_map/ppermute | solution.py:596
  124.9 6.7 %collective-permute-start.45 = (bf16[128,384]{1,0:T(8,128)(2,1)S(1)}, bf16[128,384]{1,0:T(8,128)(2,1)S(1)}, u32[]{:S(2)}, u32[]{:S(2)}) collective-permute-start(bf16[128,384]{1,0:T(8,128)(2,1)S(1)} %get-tuple-element.77.refs_13_), channel_id=1, source_target_pairs={{0,4},{4,0},{8,12},{12,8},{1,5},{5,1},{9,13},{13,9},{2,6},{6,2},{1... | collective-permute-start | bytes 294920 | tf_op jit(solution)/shard_map/ppermute | solution.py:596
  124.9 7.5 %collective-permute-start.47 = (bf16[128,384]{1,0:T(8,128)(2,1)S(1)}, bf16[128,384]{1,0:T(8,128)(2,1)S(1)}, u32[]{:S(2)}, u32[]{:S(2)}) collective-permute-start(bf16[128,384]{1,0:T(8,128)(2,1)S(1)} %collective-permute-done.46.refs_15_), channel_id=1, source_target_pairs={{0,4},{4,0},{8,12},{12,8},{1,5},{5,1},{9,13},{13,9},{2,6},{6,2},{1... | collective-permute-start | bytes 294920 | tf_op jit(solution)/shard_map/ppermute | solution.py:596
  126.9 6.3 %collective-permute-start.38 = (bf16[64,640]{1,0:T(8,128)(2,1)S(1)}, bf16[64,640]{1,0:T(8,128)(2,1)S(1)}, u32[]{:S(2)}, u32[]{:S(2)}) collective-permute-start(bf16[64,640]{1,0:T(8,128)(2,1)S(1)} %get-tuple-element.75.refs_21_), channel_id=1, source_target_pairs={{0,4},{4,0},{8,12},{12,8},{1,5},{5,1},{9,13},{13,9},{2,6},{6,2},{1... | collective-permute-start | bytes 245768 | tf_op jit(solution)/shard_map/ppermute | solution.py:596
  127.0 7.1 %collective-permute-start.40 = (bf16[64,640]{1,0:T(8,128)(2,1)S(1)}, bf16[64,640]{1,0:T(8,128)(2,1)S(1)}, u32[]{:S(2)}, u32[]{:S(2)}) collective-permute-start(bf16[64,640]{1,0:T(8,128)(2,1)S(1)} %collective-permute-done.39.refs_23_), channel_id=1, source_target_pairs={{0,4},{4,0},{8,12},{12,8},{1,5},{5,1},{9,13},{13,9},{2,6},{6,2},{1... | collective-permute-start | bytes 245768 | tf_op jit(solution)/shard_map/ppermute | solution.py:596
  128.9 1.2 collective-permute-start.35
  130.1 1.2 collective-permute-start.36
  131.3 5.5 %collective-permute-start.37 = (bf16[64,256]{1,0:T(8,128)(2,1)S(1)}, bf16[64,256]{1,0:T(8,128)(2,1)S(1)}, u32[]{:S(2)}, u32[]{:S(2)}) collective-permute-start(bf16[64,256]{1,0:T(8,128)(2,1)S(1)} %collective-permute-done.33.refs_16_), channel_id=1, source_target_pairs={{0,1},{1,0},{2,3},{3,2},{4,5},{5,4},{6,7},{7,6},{8,9},{9,8},{10,11... | collective-permute-start | bytes 98312 | tf_op jit(solution)/shard_map/ppermute | solution.py:596
  131.5 5.3 %collective-permute-start.41 = (bf16[64,640]{1,0:T(8,128)(2,1)S(1)}, bf16[64,640]{1,0:T(8,128)(2,1)S(1)}, u32[]{:S(2)}, u32[]{:S(2)}) collective-permute-start(bf16[64,640]{1,0:T(8,128)(2,1)S(1)} %get-tuple-element.75.refs_21_), channel_id=1, source_target_pairs={{0,1},{1,0},{2,3},{3,2},{4,5},{5,4},{6,7},{7,6},{8,9},{9,8},{10,11... | collective-permute-start | bytes 245768 | tf_op jit(solution)/shard_map/ppermute | solution.py:596
  132.3 4.5 %collective-permute-start.43 = (bf16[64,640]{1,0:T(8,128)(2,1)S(1)}, bf16[64,640]{1,0:T(8,128)(2,1)S(1)}, u32[]{:S(2)}, u32[]{:S(2)}) collective-permute-start(bf16[64,640]{1,0:T(8,128)(2,1)S(1)} %collective-permute-done.39.refs_23_), channel_id=1, source_target_pairs={{0,1},{1,0},{2,3},{3,2},{4,5},{5,4},{6,7},{7,6},{8,9},{9,8},{10,11... | collective-permute-start | bytes 245768 | tf_op jit(solution)/shard_map/ppermute | solution.py:596
  133.2 3.6 %collective-permute-start.42 = (bf16[64,640]{1,0:T(8,128)(2,1)S(1)}, bf16[64,640]{1,0:T(8,128)(2,1)S(1)}, u32[]{:S(2)}, u32[]{:S(2)}) collective-permute-start(bf16[64,640]{1,0:T(8,128)(2,1)S(1)} %collective-permute-done.38.refs_22_), channel_id=1, source_target_pairs={{0,1},{1,0},{2,3},{3,2},{4,5},{5,4},{6,7},{7,6},{8,9},{9,8},{10,11... | collective-permute-start | bytes 245768 | tf_op jit(solution)/shard_map/ppermute | solution.py:596
  134.1 2.7 %collective-permute-start.44 = (bf16[64,640]{1,0:T(8,128)(2,1)S(1)}, bf16[64,640]{1,0:T(8,128)(2,1)S(1)}, u32[]{:S(2)}, u32[]{:S(2)}) collective-permute-start(bf16[64,640]{1,0:T(8,128)(2,1)S(1)} %collective-permute-done.40.refs_24_), channel_id=1, source_target_pairs={{0,1},{1,0},{2,3},{3,2},{4,5},{5,4},{6,7},{7,6},{8,9},{9,8},{10,11... | collective-permute-start | bytes 245768 | tf_op jit(solution)/shard_map/ppermute | solution.py:596

commit v2 on v1

--- a/solution.py
+++ b/solution.py
@@ -264,11 +264,19 @@
             at += plan.share
 
 
-def piece_body(plan, ranks, w_lat, gain, cgain, piece):
+def piece_body(plan, ranks, w_lat, gain, cgain, piece, gain_s, cgain_s, sems):
     at = pl.multiple_of(ranks[1] * plan.part, 16)
-    piece[: plan.part, :] = w_lat[pl.ds(at, plan.part), :]
-    piece[plan.part : plan.part + 1, :] = gain[...]
-    piece[plan.part + 1 : plan.part + 2, : plan.ccol] = cgain[...]
+    moves = [
+        pltpu.make_async_copy(w_lat.at[pl.ds(at, plan.part), :], piece.at[pl.ds(0, plan.part), :], sems.at[0]),
+        pltpu.make_async_copy(gain, gain_s, sems.at[1]),
+        pltpu.make_async_copy(cgain, cgain_s, sems.at[2]),
+    ]
+    for move in moves:
+        move.start()
+    for move in moves:
+        move.wait()
+    piece[plan.part : plan.part + 1, :] = gain_s[...]
+    piece[plan.part + 1 : plan.part + 2, : plan.ccol] = cgain_s[...]
 
 
 def assemble_latent(plan, t, lat, w_s):
@@ -279,7 +287,7 @@
 
 
 def forward_body(plan, ranks, x, wq, lat, wexp, table, outs):
-    (sent, pay, v_ref, p_ref, chat_ref, rc_ref, gain_ref, cgain_ref, x_own, wlat, g_s, cg_s, n_s, c_s) = outs
+    (sent, pay, v_ref, p_ref, chat_ref, rc_ref, gain_ref, cgain_ref, wlat, g_s, cg_s, n_s, c_s) = outs
     n = plan.n
     j, t = ranks[0], ranks[1]
     core = lax.rem(t, 2)
@@ -351,8 +359,6 @@
         pay[:, plan.o_kn + h * NOPE : plan.o_kn + (h + 1) * NOPE] = kn_all[h]
     pay[:, plan.o_q + plan.heads * NOPE : plan.o_kn] = qr_cat
     pay[:, plan.o_kr :] = kr
-    for start, at in share_rows(plan, core):
-        x_own[at, :] = x[pl.ds(start, plan.share), :]
 
 
 def key_parts(plan, pay, h):
@@ -559,7 +565,7 @@
     return out
 
 
-def kernel_call(body, groups, out_groups, scratch, flops):
+def kernel_call(body, groups, out_groups, scratch, flops, inputs=pltpu.VMEM):
     def flat(items):
         return [leaf for item in items for leaf in (item if isinstance(item, list) else [item])]
 
@@ -573,7 +579,7 @@
     ins = flat(groups)
     call = pl.pallas_call(
         kernel,
-        in_specs=[pl.BlockSpec(memory_space=pltpu.SMEM)] + [vmem] * (len(ins) - 1),
+        in_specs=[pl.BlockSpec(memory_space=pltpu.SMEM)] + [pl.BlockSpec(memory_space=inputs)] * (len(ins) - 1),
         out_specs=[vmem] * len(outs),
         out_shape=outs,
         scratch_shapes=scratch,
@@ -621,17 +627,33 @@
     def shape(dims, kind=BF16):
         return jax.ShapeDtypeStruct(dims, kind)
 
-    def pick(ranks, w_lat, gain, cgain, piece):
-        piece_body(plan, ranks, w_lat, gain, cgain, piece)
-
-    def stack(ranks, blocks, target):
+    def pick(*refs):
+        piece_body(plan, *refs)
+
+    def stack(ranks, blocks, target, gain_ref, gain_s):
         for k, block in enumerate(blocks):
             target[k * (plan.part + 16) : (k + 1) * (plan.part + 16), :] = block[...]
+            gain_s[ranks[0] ^ k] = block[plan.part : plan.part + 16, :].astype(F32)[:1]
+        for b in range(n):
+            gain_ref[:, b * plan.wcol : (b + 1) * plan.wcol] = gain_s[b]
 
     tall = plan.part + 16
-    (piece,) = kernel_call(pick, [ranks, w_latent[0].T, gain, compressed_gain], [shape((tall, plan.wcol))], [], 10**4)
+    (piece,) = kernel_call(
+        pick,
+        [ranks, w_latent[0].T, gain, compressed_gain],
+        [shape((tall, plan.wcol))],
+        [pltpu.VMEM((1, plan.wcol), BF16), pltpu.VMEM((1, plan.ccol), BF16), pltpu.SemaphoreType.DMA((3,))],
+        10**4,
+        pltpu.HBM,
+    )
     blocks = gathered(piece, "dp", n)
-    (stacked,) = kernel_call(stack, [ranks, blocks], [shape((n * tall, plan.wcol))], [], 10**4)
+    stacked, gain_all = kernel_call(
+        stack,
+        [ranks, blocks],
+        [shape((n * tall, plan.wcol)), shape((1, plan.width), F32)],
+        [pltpu.VMEM((n, 1, plan.wcol), F32)],
+        10**4,
+    )
     lat = gathered(stacked, "tensor", nt)
     wq = gathered(w_query[0], "dp", n)
     wexp = gathered(expand_weight[0], "dp", n)
@@ -643,22 +665,32 @@
     cos, sin = np.cos(angle), np.sin(angle)
     table = jnp.asarray(np.concatenate([cos, cos, -sin, sin], axis=1), F32)
 
-    def prepare(ranks, *refs):
-        count = len(refs) // 2
-        for source, target in zip(refs[:count], refs[count:]):
-            target[...] = source[...]
-
-    def local(values):
+    def prepare(ranks, sources, targets, *rest):
+        sems = rest[-1]
+        moves = [pltpu.make_async_copy(a, b, sems.at[i]) for i, (a, b) in enumerate(zip(sources, targets))]
+        for move in moves:
+            move.start()
+        for move in moves:
+            move.wait()
+        if len(rest) > 1:
+            for start, at in share_rows(plan, lax.rem(ranks[1], 2)):
+                rest[0][at, :] = targets[0][pl.ds(start, plan.share), :]
+
+    def local(values, extra):
         shapes = [shape(v.shape, v.dtype) for v in values]
-        return kernel_call(prepare, [ranks] + values, shapes, [], 10**4)
-
-    x, wq[0], wexp[0], table = local([x, wq[0], wexp[0], table])
-    top, wout[0] = local([top, wout[0]])
+        sems = [pltpu.SemaphoreType.DMA((len(values),))]
+        return kernel_call(prepare, [ranks, values], [shapes] + extra, sems, 10**4, pltpu.HBM)
+
+    (x, wq[0], wexp[0], table), x_own = local([x, wq[0], wexp[0], table], [shape((plan.half, plan.width))])
+    ((top, wout[0]),) = local([top, wout[0]], [])
+    down = [(i, i - 1) for i in range(1, plan.n_pipe)]
+    x_above = lax.ppermute(x_own, "pipe", down)
+    gain_above = lax.ppermute(gain_all, "pipe", down)
 
     def forward(ranks, x, wq, lat, we, table, *outs):
         forward_body(plan, ranks, x, wq, lat, we, table, outs)
 
-    sent, pay, v, p, chat, rc, gain32, cgain32, x_own, wlat = kernel_call(
+    sent, pay, v, p, chat, rc, gain32, cgain32, wlat = kernel_call(
         forward,
         [ranks, x, wq, lat, wexp, table],
         [
@@ -670,7 +702,6 @@
             shape((rows, 1), F32),
             shape((1, plan.width), F32),
             shape((1, plan.rank), F32),
-            shape((plan.half, plan.width)),
             shape((n, plan.latent, plan.wcol)),
         ],
         [
@@ -710,26 +741,31 @@
         )
         (kept, given), up_own = got[0], got[1]
         chip = kept + flipped(given, "tensor", nt, 1)
-        sums = [chip]
-        for k in range(1, nt // 2):
-            pairs = [(i, (i + 2 * k) % nt) for i in range(nt)]
-            sums.append(lax.ppermute(chip, "tensor", pairs))
-        norm_out = [shape((plan.own if last else plan.half, plan.width))]
-        if last:
+        if not last:
+            sums = []
+            for k in range(nt // 2):
+                pairs = [(s * nt + i, r * nt + (i + 2 * k) % nt) for s, r in down for i in range(nt)]
+                sums.append(lax.ppermute(chip, ("pipe", "tensor"), pairs))
+            above = up_own if tick == 0 else lax.ppermute(up_own, "pipe", down)
+            norm_in = [ranks, sums, above, x_above, gain_above]
+            norm_out = [shape((plan.half, plan.width))]
+        else:
+            sums = [chip]
+            for k in range(1, nt // 2):
+                pairs = [(i, (i + 2 * k) % nt) for i in range(nt)]
+                sums.append(lax.ppermute(chip, "tensor", pairs))
             tail, ups = got[2], got[3]
-            norm_out.append(shape((plan.half, plan.latent + plan.spare)))
+            norm_in = [ranks, sums, up_own, x_own, gain32]
+            norm_out = [shape((plan.own, plan.width)), shape((plan.half, plan.latent + plan.spare))]
 
         def norm(ranks, sums, up_own, x_own, gain32, *rest):
             dx, dl, dx_s = rest if last else (rest[0], None, rest[1])
             norm_body(plan, last, ranks, sums, up_own, x_own, gain32, dx, dl, dx_s)
 
-        got = kernel_call(
-            norm, [ranks, sums, up_own, x_own, gain32], norm_out, [pltpu.VMEM((plan.half, plan.width), BF16)], 10**6
-        )
+        got = kernel_call(norm, norm_in, norm_out, [pltpu.VMEM((plan.half, plan.width), BF16)], 10**6)
         dx = got[0]
         if not last:
-            below = lax.ppermute(dx, "pipe", [(s, s - 1) for s in range(1, plan.n_pipe)])
-            pieces = [below, flipped(below, "tensor", nt, 1)]
+            pieces = [dx, flipped(dx, "tensor", nt, 1)]
     dl_own = gathered(got[1], "dp", n)
     dl_other = [flipped(block, "tensor", nt, 1) for block in dl_own]
     sent = handed(sent, "dp", n)

time: 139 us -> 133 us (0.957)
  waiting for transfers between devices: 67.7 us -> 57.3 us
  starting transfers between devices: 49.6 us -> 51.6 us
  local copies, waits for them, and re-layouts: 3.22 us -> 5 us
    ppermute x45, waiting for transfers between devices: 57.1 us -> 49.1 us  [flipped(): return lax.ppermute(value, axis, [(i, i ^ bit) for i in range(count)])]
    ppermute x2 -> x1, waiting for transfers between devices: 5.01 us -> 0.01 us  [token_shards(): sums.append(lax.ppermute(chip, 'tensor', pairs))]
    ppermute x1 -> x4, starting transfers between devices: 1.29 us -> 5.16 us  [the longest x2 2.58 us: token_shards(): sums.append(lax.ppermute(chip, ('pipe', 'tensor'), pairs))]
    ppermute x1 -> x4, waiting for transfers between devices: 5.56 us -> 8.21 us  [the longest x1 5.19 us: token_shards(): gain_above = lax.ppermute(gain_all, 'pipe', down)]
    unnamed x18, local copies, waits for them, and re-layouts: 3.22 us -> 5 us
  transfers between devices with their start and end apart: 48 -> 50, of which waited for: 24 -> 20; matrix products, arithmetic and copies ran while one was open for 0% -> 0% of each run, Pallas kernels for 6% -> 7%
where the time goes in v2:
time: 133 us
  waiting for transfers between devices  57.3 us (43%)
  starting transfers between devices  51.6 us (39%)
  Pallas kernels  18.2 us (14%)
  local copies, waits for them, and re-layouts  5 us (4%)
    ppermute x45, waiting for transfers between devices, flipped(): return lax.ppermute(value, axis, [(i, i ^ bit) for i in range(count)])  49.1 us
    ppermute x45, starting transfers between devices, flipped(): return lax.ppermute(value, axis, [(i, i ^ bit) for i in range(count)])  45.8 us
    pallas_call x11, Pallas kernels, kernel_call(): got = call(*ins)  18.2 us
    ppermute x1, waiting for transfers between devices, token_shards(): gain_above = lax.ppermute(gain_all, 'pipe', down)  5.19 us
    unnamed x18, local copies, waits for them, and re-layouts  5 us
    ppermute x1, waiting for transfers between devices, token_shards(): x_above = lax.ppermute(x_own, 'pipe', down)  3.01 us
  transfers between devices with their start and end apart: 50, of which 20 were waited for; matrix products, arithmetic and copies ran while one was open for 0% of the time, Pallas kernels for 7%

profile of v2, /device:TPU:0, one launch (start us, length us, event | category | flops | bytes accessed | tf_op | source)
XLA Modules:
  0.0 133.1 jit_solution(7572235986735804739)
XLA Ops:
  0.7 1.0 copy-done
  1.7 0.7 copy-done.7
  2.4 0.7 copy-done.8
  3.0 0.7 shard_map.146.refs_1_
  3.7 4.1 %collective-permute-start.4 = (bf16[160,256]{1,0:T(8,128)(2,1)S(1)}, bf16[160,256]{1,0:T(8,128)(2,1)S(1)}, u32[]{:S(2)}, u32[]{:S(2)}) collective-permute-start(bf16[160,256]{1,0:T(8,128)(2,1)S(1)} %shard_map.146.refs_1_), channel_id=1, source_target_pairs={{0,8},{4,12},{8,0},{12,4},{1,9},{5,13},{9,1},{13,5},{2,10},{6,14},... | collective-permute-start | bytes 245768 | tf_op jit(solution)/shard_map/ppermute | solution.py:602
  7.8 1.6 %collective-permute-start.3 = (bf16[160,256]{1,0:T(8,128)(2,1)S(1)}, bf16[160,256]{1,0:T(8,128)(2,1)S(1)}, u32[]{:S(2)}, u32[]{:S(2)}) collective-permute-start(bf16[160,256]{1,0:T(8,128)(2,1)S(1)} %shard_map.146.refs_1_), channel_id=1, source_target_pairs={{0,4},{4,0},{8,12},{12,8},{1,5},{5,1},{9,13},{13,9},{2,6},{6,2},{1... | collective-permute-start | bytes 245768 | tf_op jit(solution)/shard_map/ppermute | solution.py:602
  9.4 2.2 %collective-permute-done.4.refs_3_ = bf16[160,256]{1,0:T(8,128)(2,1)S(1)} collective-permute-done((bf16[160,256]{1,0:T(8,128)(2,1)S(1)}, bf16[160,256]{1,0:T(8,128)(2,1)S(1)}, u32[]{:S(2)}, u32[]{:S(2)}) %collective-permute-start.4) | collective-permute-done | bytes 81952 | tf_op jit(solution)/shard_map/ppermute | solution.py:602
  11.6 1.2 collective-permute-start.5
  12.8 3.2 %collective-permute-done.5.refs_4_ = bf16[160,256]{1,0:T(8,128)(2,1)S(1)} collective-permute-done((bf16[160,256]{1,0:T(8,128)(2,1)S(1)}, bf16[160,256]{1,0:T(8,128)(2,1)S(1)}, u32[]{:S(2)}, u32[]{:S(2)}) %collective-permute-start.5) | collective-permute-done | bytes 81952 | tf_op jit(solution)/shard_map/ppermute | solution.py:602
  16.0 0.6 shard_map.147
  16.6 1.9 %collective-permute-start.7 = (bf16[640,256]{1,0:T(8,128)(2,1)S(1)}, bf16[640,256]{1,0:T(8,128)(2,1)S(1)}, u32[]{:S(2)}, u32[]{:S(2)}) collective-permute-start(bf16[640,256]{1,0:T(8,128)(2,1)S(1)} %get-tuple-element.50.refs_6_), channel_id=1, source_target_pairs={{0,2},{1,3},{2,0},{3,1},{4,6},{5,7},{6,4},{7,5},{8,10},{9,11},{10,... | collective-permute-start | bytes 983048 | tf_op jit(solution)/shard_map/ppermute | solution.py:602
  18.5 2.2 %collective-permute-start.10 = (bf16[128,512]{1,0:T(8,128)(2,1)}, bf16[128,512]{1,0:T(8,128)(2,1)S(1)}, u32[]{:S(2)}, u32[]{:S(2)}) collective-permute-start(bf16[128,512]{1,0:T(8,128)(2,1)} %bitcast.27), channel_id=1, source_target_pairs={{0,8},{4,12},{8,0},{12,4},{1,9},{5,13},{9,1},{13,5},{2,10},{6,14},... | collective-permute-start | bytes 393224 | tf_op jit(solution)/shard_map/ppermute | solution.py:602
  20.7 2.0 %collective-permute-start.9 = (bf16[128,512]{1,0:T(8,128)(2,1)}, bf16[128,512]{1,0:T(8,128)(2,1)S(1)}, u32[]{:S(2)}, u32[]{:S(2)}) collective-permute-start(bf16[128,512]{1,0:T(8,128)(2,1)} %bitcast.28), channel_id=1, source_target_pairs={{0,4},{4,0},{8,12},{12,8},{1,5},{5,1},{9,13},{13,9},{2,6},{6,2},{1... | collective-permute-start | bytes 393224 | tf_op jit(solution)/shard_map/ppermute | solution.py:602
  22.7 2.9 %collective-permute-start.13 = (bf16[256,256]{1,0:T(8,128)(2,1)}, bf16[256,256]{1,0:T(8,128)(2,1)S(1)}, u32[]{:S(2)}, u32[]{:S(2)}) collective-permute-start(bf16[256,256]{1,0:T(8,128)(2,1)} %bitcast.24), channel_id=1, source_target_pairs={{0,8},{4,12},{8,0},{12,4},{1,9},{5,13},{9,1},{13,5},{2,10},{6,14},... | collective-permute-start | bytes 393224 | tf_op jit(solution)/shard_map/ppermute | solution.py:602
  25.6 3.9 %collective-permute-done.10.refs_12_.refs_15_.refs_17_ = bf16[128,512]{1,0:T(8,128)(2,1)S(1)} collective-permute-done((bf16[128,512]{1,0:T(8,128)(2,1)}, bf16[128,512]{1,0:T(8,128)(2,1)S(1)}, u32[]{:S(2)}, u32[]{:S(2)}) %collective-permute-start.10) | collective-permute-done | bytes 131104 | tf_op jit(solution)/shard_map/ppermute | solution.py:602
  29.5 0.5 collective-permute-start.8
  30.0 5.4 %collective-permute-start = (bf16[256,384]{1,0:T(8,128)(2,1)}, bf16[256,384]{1,0:T(8,128)(2,1)S(1)}, u32[]{:S(2)}, u32[]{:S(2)}) collective-permute-start(bf16[256,384]{1,0:T(8,128)(2,1)} %bitcast.22), channel_id=1, source_target_pairs={{0,4},{4,0},{8,12},{12,8},{1,5},{5,1},{9,13},{13,9},{2,6},{6,2},{1... | collective-permute-start | bytes 589832 | tf_op jit(solution)/shard_map/ppermute | solution.py:602
  35.5 5.1 %collective-permute-done.13.refs_19_.refs_21_ = bf16[256,256]{1,0:T(8,128)(2,1)S(1)} collective-permute-done((bf16[256,256]{1,0:T(8,128)(2,1)}, bf16[256,256]{1,0:T(8,128)(2,1)S(1)}, u32[]{:S(2)}, u32[]{:S(2)}) %collective-permute-start.13) | collective-permute-done | bytes 131104 | tf_op jit(solution)/shard_map/ppermute | solution.py:602
  40.6 0.7 collective-permute-start.11
  41.3 1.3 collective-permute-start.2
  42.6 2.1 %collective-permute-done.refs_3_.refs_9_.refs_11_ = bf16[256,384]{1,0:T(8,128)(2,1)S(1)} collective-permute-done((bf16[256,384]{1,0:T(8,128)(2,1)}, bf16[256,384]{1,0:T(8,128)(2,1)S(1)}, u32[]{:S(2)}, u32[]{:S(2)}) %collective-permute-start) | collective-permute-done | bytes 196640 | tf_op jit(solution)/shard_map/ppermute | solution.py:602
  44.7 2.8 %collective-permute-done.11.refs_13_.refs_16_.refs_18_ = bf16[128,512]{1,0:T(8,128)(2,1)S(1)} collective-permute-done((bf16[128,512]{1,0:T(8,128)(2,1)S(1)}, bf16[128,512]{1,0:T(8,128)(2,1)S(1)}, u32[]{:S(2)}, u32[]{:S(2)}) %collective-permute-start.11) | collective-permute-done | bytes 131104 | tf_op jit(solution)/shard_map/ppermute | solution.py:602
  47.6 0.9 copy-done.1
  48.6 0.9 copy-done.4
  49.5 0.7 shard_map.144
  50.3 0.8 copy-done.6
  51.1 1.1 shard_map.145
  52.3 2.7 %shard_map.148 = (bf16[64,384]{1,0:T(8,128)(2,1)S(1)}, bf16[64,384]{1,0:T(8,128)(2,1)S(1)}, bf16[64,384]{1,0:T(8,128)(2,1)S(1)}, bf16[64,384]{1,0:T(8,128)(2,1)S...) custom-call(s32[3]{0:T(128)S(1)} %pad_add_fusion.refs_0_, ...), custom_call_target="tpu_custom_call" | custom-call | flops 500000000 | bytes 4194304 | tf_op jit(solution)/shard_map/pallas_call | solution.py:589
  55.0 2.3 %collective-permute-done.14.refs_20_.refs_22_ = bf16[256,256]{1,0:T(8,128)(2,1)S(1)} collective-permute-done((bf16[256,256]{1,0:T(8,128)(2,1)S(1)}, bf16[256,256]{1,0:T(8,128)(2,1)S(1)}, u32[]{:S(2)}, u32[]{:S(2)}) %collective-permute-start.14) | collective-permute-done | bytes 131104 | tf_op jit(solution)/shard_map/ppermute | solution.py:602
  57.3 2.7 %shard_map.149 = (bf16[64,1024]{1,0:T(8,128)(2,1)S(1)}, bf16[64,1024]{1,0:T(8,128)(2,1)S(1)}, bf16[64,1024]{1,0:T(8,128)(2,1)S(1)}) custom-call(s32[3]{0:T(128)S(1)} %pad_add_fusion.refs_0_, bf16[128,1024]{1,0:T(8,128)(2,1)S(1)} %get-tuple-element.47.refs_1_, bf16[128,960]{1,0:T(8,128)(2,1)S(1)} %get-tuple-element.53.refs_2_.refs_4_.refs_9_, ...), custom_call_target="tpu_custom_call" | custom-call | flops 1000000000 | bytes 4194304 | tf_op jit(solution)/shard_map/pallas_call | solution.py:589
  60.1 1.3 collective-permute-start.18
  61.5 1.3 collective-permute-start.16
  62.8 1.3 collective-permute-start.17
  64.1 1.3 collective-permute-start.19
  65.4 3.0 %collective-permute-done.18.refs_4_ = bf16[64,1024]{1,0:T(8,128)(2,1)S(1)} collective-permute-done((bf16[64,1024]{1,0:T(8,128)(2,1)S(1)}, bf16[64,1024]{1,0:T(8,128)(2,1)S(1)}, u32[]{:S(2)}, u32[]{:S(2)}) %collective-permute-start.18) | collective-permute-done | bytes 131104 | tf_op jit(solution)/shard_map/ppermute | solution.py:687
  68.4 5.2 %collective-permute-done.19.refs_5_ = f32[1,1024]{1,0:T(1,128)S(1)} collective-permute-done((f32[1,1024]{1,0:T(1,128)S(1)}, f32[1,1024]{1,0:T(1,128)S(1)}, u32[]{:S(2)}, u32[]{:S(2)}) %collective-permute-start.19) | collective-permute-done | bytes 4128 | tf_op jit(solution)/shard_map/ppermute | solution.py:688
  73.6 0.8 shard_map.150.refs_2_
  74.5 1.3 %collective-permute-done.20.refs_3_ = bf16[64,1024]{1,0:T(8,128)(2,1)S(1)} collective-permute-done((bf16[64,1024]{1,0:T(8,128)(2,1)S(1)}, bf16[64,1024]{1,0:T(8,128)(2,1)S(1)}, u32[]{:S(2)}, u32[]{:S(2)}) %collective-permute-start.20) | collective-permute-done | bytes 131104 | tf_op jit(solution)/shard_map/ppermute | solution.py:602
  75.8 2.8 %shard_map.151 = (bf16[64,1664]{1,0:T(8,128)(2,1)S(1)}, bf16[64,1664]{1,0:T(8,128)(2,1)S(1)}, bf16[64,1024]{1,0:T(8,128)(2,1)S(1)}, bf16[128,384]{1,0:T(8,128)(2...) custom-call(s32[3]{0:T(128)S(1)} %pad_add_fusion.refs_0_, ...), custom_call_target="tpu_custom_call" | custom-call | flops 1000000000 | bytes 4194304 | tf_op jit(solution)/shard_map/pallas_call | solution.py:589
  78.8 1.7 %collective-permute-start.31 = (bf16[128,960]{1,0:T(8,128)(2,1)S(1)}, bf16[128,960]{1,0:T(8,128)(2,1)S(1)}, u32[]{:S(2)}, u32[]{:S(2)}) collective-permute-start(bf16[128,960]{1,0:T(8,128)(2,1)S(1)} %get-tuple-element.53.refs_2_.refs_4_.refs_9_), channel_id=1, source_target_pairs={{0,8},{4,12},{8,0},{12,4},{1,9},{5,13},{9,1},{13,5},{2,10},{6,14},... | collective-permute-start | bytes 737288 | tf_op jit(solution)/shard_map/ppermute | solution.py:602
  80.4 2.4 %collective-permute-start.30 = (bf16[128,960]{1,0:T(8,128)(2,1)S(1)}, bf16[128,960]{1,0:T(8,128)(2,1)S(1)}, u32[]{:S(2)}, u32[]{:S(2)}) collective-permute-start(bf16[128,960]{1,0:T(8,128)(2,1)S(1)} %get-tuple-element.53.refs_2_.refs_4_.refs_9_), channel_id=1, source_target_pairs={{0,4},{4,0},{8,12},{12,8},{1,5},{5,1},{9,13},{13,9},{2,6},{6,2},{1... | collective-permute-start | bytes 737288 | tf_op jit(solution)/shard_map/ppermute | solution.py:602
  82.9 0.6 collective-permute-start.22
  83.5 0.9 collective-permute-start.24
  84.4 11.8 %collective-permute-done.23.refs_2_ = bf16[64,384]{1,0:T(8,128)(2,1)S(1)} collective-permute-done((bf16[64,384]{1,0:T(8,128)(2,1)S(1)}, bf16[64,384]{1,0:T(8,128)(2,1)S(1)}, u32[]{:S(2)}, u32[]{:S(2)}) %collective-permute-start.23) | collective-permute-done | bytes 49184 | tf_op jit(solution)/shard_map/ppermute | solution.py:602
  96.2 2.4 %collective-permute-start.25 = (bf16[64,384]{1,0:T(8,128)(2,1)S(1)}, bf16[64,384]{1,0:T(8,128)(2,1)S(1)}, u32[]{:S(2)}, u32[]{:S(2)}) collective-permute-start(bf16[64,384]{1,0:T(8,128)(2,1)S(1)} %get-tuple-element.74), channel_id=1, source_target_pairs={{0,12},{4,8},{8,4},{12,0},{1,13},{5,9},{9,5},{13,1},{2,14},{6,10},... | collective-permute-start | bytes 147464 | tf_op jit(solution)/shard_map/ppermute | solution.py:602
  98.6 3.5 %collective-permute-done.25.refs_4_ = bf16[64,384]{1,0:T(8,128)(2,1)S(1)} collective-permute-done((bf16[64,384]{1,0:T(8,128)(2,1)S(1)}, bf16[64,384]{1,0:T(8,128)(2,1)S(1)}, u32[]{:S(2)}, u32[]{:S(2)}) %collective-permute-start.25) | collective-permute-done | bytes 49184 | tf_op jit(solution)/shard_map/ppermute | solution.py:602
  102.1 0.5 collective-permute-start.28
  102.6 0.7 collective-permute-done.27.refs_6_
  103.5 2.2 %collective-permute-start.48 = (bf16[128,384]{1,0:T(8,128)(2,1)S(1)}, bf16[128,384]{1,0:T(8,128)(2,1)S(1)}, u32[]{:S(2)}, u32[]{:S(2)}) collective-permute-start(bf16[128,384]{1,0:T(8,128)(2,1)S(1)} %get-tuple-element.81.refs_13_), channel_id=1, source_target_pairs={{0,8},{4,12},{8,0},{12,4},{1,9},{5,13},{9,1},{13,5},{2,10},{6,14},... | collective-permute-start | bytes 294920 | tf_op jit(solution)/shard_map/ppermute | solution.py:602
  105.6 0.8 collective-permute-start.33
  106.4 1.2 collective-permute-start.34
  107.6 2.4 %collective-permute-start.35 = (bf16[64,256]{1,0:T(8,128)(2,1)S(1)}, bf16[64,256]{1,0:T(8,128)(2,1)S(1)}, u32[]{:S(2)}, u32[]{:S(2)}) collective-permute-start(bf16[64,256]{1,0:T(8,128)(2,1)S(1)} %get-tuple-element.78), channel_id=1, source_target_pairs={{0,12},{4,8},{8,4},{12,0},{1,13},{5,9},{9,5},{13,1},{2,14},{6,10},... | collective-permute-start | bytes 98312 | tf_op jit(solution)/shard_map/ppermute | solution.py:602
  110.0 1.4 %shard_map.152 = (bf16[32,1024]{1,0:T(8,128)(2,1)}, bf16[64,640]{1,0:T(8,128)(2,1)S(1)}) custom-call(s32[3]{0:T(128)S(1)} %pad_add_fusion.refs_0_, bf16[64,1664]{1,0:T(8,128)(2,1)S(1)} %add.7.refs_1_, bf16[64,1664]{1,0:T(8,128)(2,1)S(1)} %collective-permute-done.22.refs_2_, bf16[64,1024]{1,0:T(8,128)(2,1)S(1)} %get-tuple-element.68.refs_3_, ...), custom_call_target="tpu_custom_call" | custom-call | flops 1000000 | bytes 4194304 | tf_op jit(solution)/shard_map/pallas_call | solution.py:589
  111.5 2.9 %collective-permute-done.33.refs_14_ = bf16[64,256]{1,0:T(8,128)(2,1)S(1)} collective-permute-done((bf16[64,256]{1,0:T(8,128)(2,1)S(1)}, bf16[64,256]{1,0:T(8,128)(2,1)S(1)}, u32[]{:S(2)}, u32[]{:S(2)}) %collective-permute-start.33) | collective-permute-done | bytes 32800 | tf_op jit(solution)/shard_map/ppermute | solution.py:602
  114.4 1.2 collective-permute-start.41
  116.1 0.7 collective-permute-done.36.refs_17_
  117.0 2.4 %collective-permute-start.47 = (bf16[128,384]{1,0:T(8,128)(2,1)S(1)}, bf16[128,384]{1,0:T(8,128)(2,1)S(1)}, u32[]{:S(2)}, u32[]{:S(2)}) collective-permute-start(bf16[128,384]{1,0:T(8,128)(2,1)S(1)} %get-tuple-element.81.refs_13_), channel_id=1, source_target_pairs={{0,4},{4,0},{8,12},{12,8},{1,5},{5,1},{9,13},{13,9},{2,6},{6,2},{1... | collective-permute-start | bytes 294920 | tf_op jit(solution)/shard_map/ppermute | solution.py:602
  119.5 2.0 %collective-permute-start.40 = (bf16[64,640]{1,0:T(8,128)(2,1)S(1)}, bf16[64,640]{1,0:T(8,128)(2,1)S(1)}, u32[]{:S(2)}, u32[]{:S(2)}) collective-permute-start(bf16[64,640]{1,0:T(8,128)(2,1)S(1)} %get-tuple-element.79.refs_21_), channel_id=1, source_target_pairs={{0,4},{4,0},{8,12},{12,8},{1,5},{5,1},{9,13},{13,9},{2,6},{6,2},{1... | collective-permute-start | bytes 245768 | tf_op jit(solution)/shard_map/ppermute | solution.py:602
  121.5 1.5 %collective-permute-done.47.refs_14_ = bf16[128,384]{1,0:T(8,128)(2,1)S(1)} collective-permute-done((bf16[128,384]{1,0:T(8,128)(2,1)S(1)}, bf16[128,384]{1,0:T(8,128)(2,1)S(1)}, u32[]{:S(2)}, u32[]{:S(2)}) %collective-permute-start.47) | collective-permute-done | bytes 98336 | tf_op jit(solution)/shard_map/ppermute | solution.py:602
  123.6 1.6 %collective-permute-done.49.refs_16_ = bf16[128,384]{1,0:T(8,128)(2,1)S(1)} collective-permute-done((bf16[128,384]{1,0:T(8,128)(2,1)S(1)}, bf16[128,384]{1,0:T(8,128)(2,1)S(1)}, u32[]{:S(2)}, u32[]{:S(2)}) %collective-permute-start.49) | collective-permute-done | bytes 98336 | tf_op jit(solution)/shard_map/ppermute | solution.py:602
  125.2 1.8 %collective-permute-done.40.refs_22_ = bf16[64,640]{1,0:T(8,128)(2,1)S(1)} collective-permute-done((bf16[64,640]{1,0:T(8,128)(2,1)S(1)}, bf16[64,640]{1,0:T(8,128)(2,1)S(1)}, u32[]{:S(2)}, u32[]{:S(2)}) %collective-permute-start.40) | collective-permute-done | bytes 81952 | tf_op jit(solution)/shard_map/ppermute | solution.py:602
  126.9 1.4 %collective-permute-done.42.refs_24_ = bf16[64,640]{1,0:T(8,128)(2,1)S(1)} collective-permute-done((bf16[64,640]{1,0:T(8,128)(2,1)S(1)}, bf16[64,640]{1,0:T(8,128)(2,1)S(1)}, u32[]{:S(2)}, u32[]{:S(2)}) %collective-permute-start.42) | collective-permute-done | bytes 81952 | tf_op jit(solution)/shard_map/ppermute | solution.py:602
  128.3 2.7 %shard_map.154 = (f32[256,384]{1,0:T(8,128)}, f32[128,512]{1,0:T(8,128)}) custom-call(s32[3]{0:T(128)S(1)} %pad_add_fusion.refs_0_, bf16[64,384]{1,0:T(8,128)(2,1)S(1)} %get-tuple-element.71.refs_1_, bf16[64,384]{1,0:T(8,128)(2,1)S(1)} %collective-permute-done.23.refs_2_, bf16[64,384]{1,0:T(8,128)(2,1)S(1)} %collective-permute-done.24.refs_3_, ...), custom_call_target="tpu_custom_call" | custom-call | flops 1000000000 | bytes 4194304 | tf_op jit(solution)/shard_map/pallas_call | solution.py:589
  131.1 2.0 %shard_map.153 = (f32[1,256]{1,0:T(1,128)}, f32[576,256]{1,0:T(8,128)}, f32[1,128]{1,0:T(1,128)}, f32[256,256]{1,0:T(8,128)}) custom-call(s32[3]{0:T(128)S(1)} %pad_add_fusion.refs_0_, bf16[64,384]{1,0:T(8,128)(2,1)S(1)} %get-tuple-element.71.refs_1_, bf16[64,384]{1,0:T(8,128)(2,1)S(1)} %collective-permute-done.23.refs_2_, ...), custom_call_target="tpu_custom_call" | custom-call | flops 1000000000 | bytes 4194304 | tf_op jit(solution)/shard_map/pallas_call | solution.py:589
  (68 shorter events, 2.3 us)
Async XLA Ops:
  0.7 1.0 copy-start
  1.7 0.7 copy-start.7
  2.4 0.7 copy-start.8
  3.0 47.2 %copy-start.2 = (bf16[1,2,64,1024]{3,2,1,0:T(8,128)(2,1)S(1)}, bf16[1,2,64,1024]{3,2,1,0:T(8,128)(2,1)}, u32[]{:S(2)}) copy-start(bf16[1,2,64,1024]{3,2,1,0:T(8,128)(2,1)} %param.9) | copy-start | bytes 786436
  3.0 47.3 %copy-start.3 = (bf16[1,256,384]{2,1,0:T(8,128)(2,1)S(1)}, bf16[1,256,384]{2,1,0:T(8,128)(2,1)}, u32[]{:S(2)}) copy-start(bf16[1,256,384]{2,1,0:T(8,128)(2,1)} %param.12) | copy-start | bytes 589828
  3.0 47.3 %copy-start.5 = (bf16[1,128,512]{2,1,0:T(8,128)(2,1)S(1)}, bf16[1,128,512]{2,1,0:T(8,128)(2,1)}, u32[]{:S(2)}) copy-start(bf16[1,128,512]{2,1,0:T(8,128)(2,1)} %param.15) | copy-start | bytes 393220
  3.7 7.9 %collective-permute-start.4 = (bf16[160,256]{1,0:T(8,128)(2,1)S(1)}, bf16[160,256]{1,0:T(8,128)(2,1)S(1)}, u32[]{:S(2)}, u32[]{:S(2)}) collective-permute-start(bf16[160,256]{1,0:T(8,128)(2,1)S(1)} %shard_map.146.refs_1_), channel_id=1, source_target_pairs={{0,8},{4,12},{8,0},{12,4},{1,9},{5,13},{9,1},{13,5},{2,10},{6,14},... | collective-permute-start | bytes 245768 | tf_op jit(solution)/shard_map/ppermute | solution.py:602
  7.8 5.0 %collective-permute-start.3 = (bf16[160,256]{1,0:T(8,128)(2,1)S(1)}, bf16[160,256]{1,0:T(8,128)(2,1)S(1)}, u32[]{:S(2)}, u32[]{:S(2)}) collective-permute-start(bf16[160,256]{1,0:T(8,128)(2,1)S(1)} %shard_map.146.refs_1_), channel_id=1, source_target_pairs={{0,4},{4,0},{8,12},{12,8},{1,5},{5,1},{9,13},{13,9},{2,6},{6,2},{1... | collective-permute-start | bytes 245768 | tf_op jit(solution)/shard_map/ppermute | solution.py:602
  11.6 4.4 %collective-permute-start.5 = (bf16[160,256]{1,0:T(8,128)(2,1)S(1)}, bf16[160,256]{1,0:T(8,128)(2,1)S(1)}, u32[]{:S(2)}, u32[]{:S(2)}) collective-permute-start(bf16[160,256]{1,0:T(8,128)(2,1)S(1)} %collective-permute-done.4.refs_3_), channel_id=1, source_target_pairs={{0,4},{4,0},{8,12},{12,8},{1,5},{5,1},{9,13},{13,9},{2,6},{6,2},{1... | collective-permute-start | bytes 245768 | tf_op jit(solution)/shard_map/ppermute | solution.py:602
  16.6 12.9 %collective-permute-start.7 = (bf16[640,256]{1,0:T(8,128)(2,1)S(1)}, bf16[640,256]{1,0:T(8,128)(2,1)S(1)}, u32[]{:S(2)}, u32[]{:S(2)}) collective-permute-start(bf16[640,256]{1,0:T(8,128)(2,1)S(1)} %get-tuple-element.50.refs_6_), channel_id=1, source_target_pairs={{0,2},{1,3},{2,0},{3,1},{4,6},{5,7},{6,4},{7,5},{8,10},{9,11},{10,... | collective-permute-start | bytes 983048 | tf_op jit(solution)/shard_map/ppermute | solution.py:602
  18.5 11.0 %collective-permute-start.10 = (bf16[128,512]{1,0:T(8,128)(2,1)}, bf16[128,512]{1,0:T(8,128)(2,1)S(1)}, u32[]{:S(2)}, u32[]{:S(2)}) collective-permute-start(bf16[128,512]{1,0:T(8,128)(2,1)} %bitcast.27), channel_id=1, source_target_pairs={{0,8},{4,12},{8,0},{12,4},{1,9},{5,13},{9,1},{13,5},{2,10},{6,14},... | collective-permute-start | bytes 393224 | tf_op jit(solution)/shard_map/ppermute | solution.py:602
  20.7 9.3 %collective-permute-start.9 = (bf16[128,512]{1,0:T(8,128)(2,1)}, bf16[128,512]{1,0:T(8,128)(2,1)S(1)}, u32[]{:S(2)}, u32[]{:S(2)}) collective-permute-start(bf16[128,512]{1,0:T(8,128)(2,1)} %bitcast.28), channel_id=1, source_target_pairs={{0,4},{4,0},{8,12},{12,8},{1,5},{5,1},{9,13},{13,9},{2,6},{6,2},{1... | collective-permute-start | bytes 393224 | tf_op jit(solution)/shard_map/ppermute | solution.py:602
  22.7 18.6 %collective-permute-start.1 = (bf16[256,384]{1,0:T(8,128)(2,1)}, bf16[256,384]{1,0:T(8,128)(2,1)S(1)}, u32[]{:S(2)}, u32[]{:S(2)}) collective-permute-start(bf16[256,384]{1,0:T(8,128)(2,1)} %bitcast.21), channel_id=1, source_target_pairs={{0,8},{4,12},{8,0},{12,4},{1,9},{5,13},{9,1},{13,5},{2,10},{6,14},... | collective-permute-start | bytes 589832 | tf_op jit(solution)/shard_map/ppermute | solution.py:602
  22.7 17.8 %collective-permute-start.13 = (bf16[256,256]{1,0:T(8,128)(2,1)}, bf16[256,256]{1,0:T(8,128)(2,1)S(1)}, u32[]{:S(2)}, u32[]{:S(2)}) collective-permute-start(bf16[256,256]{1,0:T(8,128)(2,1)} %bitcast.24), channel_id=1, source_target_pairs={{0,8},{4,12},{8,0},{12,4},{1,9},{5,13},{9,1},{13,5},{2,10},{6,14},... | collective-permute-start | bytes 393224 | tf_op jit(solution)/shard_map/ppermute | solution.py:602
  29.5 22.7 %collective-permute-start.6 = (bf16[640,256]{1,0:T(8,128)(2,1)S(1)}, bf16[640,256]{1,0:T(8,128)(2,1)S(1)}, u32[]{:S(2)}, u32[]{:S(2)}) collective-permute-start(bf16[640,256]{1,0:T(8,128)(2,1)S(1)} %get-tuple-element.50.refs_6_), channel_id=1, source_target_pairs={{0,1},{1,0},{2,3},{3,2},{4,5},{5,4},{6,7},{7,6},{8,9},{9,8},{10,11... | collective-permute-start | bytes 983048 | tf_op jit(solution)/shard_map/ppermute | solution.py:602
  29.5 22.7 %collective-permute-start.8 = (bf16[640,256]{1,0:T(8,128)(2,1)S(1)}, bf16[640,256]{1,0:T(8,128)(2,1)S(1)}, u32[]{:S(2)}, u32[]{:S(2)}) collective-permute-start(bf16[640,256]{1,0:T(8,128)(2,1)S(1)} %collective-permute-done.7.refs_8_), channel_id=1, source_target_pairs={{0,1},{1,0},{2,3},{3,2},{4,5},{5,4},{6,7},{7,6},{8,9},{9,8},{10,11... | collective-permute-start | bytes 983048 | tf_op jit(solution)/shard_map/ppermute | solution.py:602
  30.0 14.7 %collective-permute-start = (bf16[256,384]{1,0:T(8,128)(2,1)}, bf16[256,384]{1,0:T(8,128)(2,1)S(1)}, u32[]{:S(2)}, u32[]{:S(2)}) collective-permute-start(bf16[256,384]{1,0:T(8,128)(2,1)} %bitcast.22), channel_id=1, source_target_pairs={{0,4},{4,0},{8,12},{12,8},{1,5},{5,1},{9,13},{13,9},{2,6},{6,2},{1... | collective-permute-start | bytes 589832 | tf_op jit(solution)/shard_map/ppermute | solution.py:602
  40.6 7.0 %collective-permute-start.11 = (bf16[128,512]{1,0:T(8,128)(2,1)S(1)}, bf16[128,512]{1,0:T(8,128)(2,1)S(1)}, u32[]{:S(2)}, u32[]{:S(2)}) collective-permute-start(bf16[128,512]{1,0:T(8,128)(2,1)S(1)} %collective-permute-done.10.refs_12_.refs_15_.refs_17_), channel_id=1, source_target_pairs={{0,4},{4,0},{8,12},{12,8},{1,5},{5,1},{9,13},{13,9},{2,6},{6,2},{1... | collective-permute-start | bytes 393224 | tf_op jit(solution)/shard_map/ppermute | solution.py:602
  41.3 11.0 %collective-permute-start.2 = (bf16[256,384]{1,0:T(8,128)(2,1)S(1)}, bf16[256,384]{1,0:T(8,128)(2,1)S(1)}, u32[]{:S(2)}, u32[]{:S(2)}) collective-permute-start(bf16[256,384]{1,0:T(8,128)(2,1)S(1)} %collective-permute-done.1.refs_4_.refs_10_.refs_12_), channel_id=1, source_target_pairs={{0,4},{4,0},{8,12},{12,8},{1,5},{5,1},{9,13},{13,9},{2,6},{6,2},{1... | collective-permute-start | bytes 589832 | tf_op jit(solution)/shard_map/ppermute | solution.py:602
  44.7 10.2 %collective-permute-start.12 = (bf16[256,256]{1,0:T(8,128)(2,1)}, bf16[256,256]{1,0:T(8,128)(2,1)S(1)}, u32[]{:S(2)}, u32[]{:S(2)}) collective-permute-start(bf16[256,256]{1,0:T(8,128)(2,1)} %bitcast.25), channel_id=1, source_target_pairs={{0,4},{4,0},{8,12},{12,8},{1,5},{5,1},{9,13},{13,9},{2,6},{6,2},{1... | collective-permute-start | bytes 393224 | tf_op jit(solution)/shard_map/ppermute | solution.py:602
  47.5 9.8 %collective-permute-start.14 = (bf16[256,256]{1,0:T(8,128)(2,1)S(1)}, bf16[256,256]{1,0:T(8,128)(2,1)S(1)}, u32[]{:S(2)}, u32[]{:S(2)}) collective-permute-start(bf16[256,256]{1,0:T(8,128)(2,1)S(1)} %collective-permute-done.13.refs_19_.refs_21_), channel_id=1, source_target_pairs={{0,4},{4,0},{8,12},{12,8},{1,5},{5,1},{9,13},{13,9},{2,6},{6,2},{1... | collective-permute-start | bytes 393224 | tf_op jit(solution)/shard_map/ppermute | solution.py:602
  47.6 0.9 copy-start.1
  48.6 0.9 copy-start.4
  50.3 0.8 copy-start.6
  60.0 1.4 %collective-permute-start.15 = (bf16[64,1024]{1,0:T(8,128)(2,1)S(1)}, bf16[64,1024]{1,0:T(8,128)(2,1)S(1)}, u32[]{:S(2)}, u32[]{:S(2)}) collective-permute-start(bf16[64,1024]{1,0:T(8,128)(2,1)S(1)} %get-tuple-element.62), channel_id=1, source_target_pairs={{0,1},{1,0},{2,3},{3,2},{4,5},{5,4},{6,7},{7,6},{8,9},{9,8},{10,11... | collective-permute-start | bytes 393224 | tf_op jit(solution)/shard_map/ppermute | solution.py:602
  60.1 8.2 %collective-permute-start.18 = (bf16[64,1024]{1,0:T(8,128)(2,1)S(1)}, bf16[64,1024]{1,0:T(8,128)(2,1)S(1)}, u32[]{:S(2)}, u32[]{:S(2)}) collective-permute-start(bf16[64,1024]{1,0:T(8,128)(2,1)S(1)} %get-tuple-element.64.refs_4_), channel_id=1, source_target_pairs={{16,0},{17,1},{18,2},{19,3},{20,4},{21,5},{22,6},{23,7},{24,8},{25... | collective-permute-start | bytes 393224 | tf_op jit(solution)/shard_map/ppermute | solution.py:687
  61.5 12.1 %collective-permute-start.16 = (bf16[64,1024]{1,0:T(8,128)(2,1)S(1)}, bf16[64,1024]{1,0:T(8,128)(2,1)S(1)}, u32[]{:S(2)}, u32[]{:S(2)}) collective-permute-start(bf16[64,1024]{1,0:T(8,128)(2,1)S(1)} %add.6), channel_id=1, source_target_pairs={{16,0},{17,1},{18,2},{19,3},{20,4},{21,5},{22,6},{23,7},{24,8},{25... | collective-permute-start | bytes 393224 | tf_op jit(solution)/shard_map/ppermute | solution.py:748
  62.8 10.8 %collective-permute-start.17 = (bf16[64,1024]{1,0:T(8,128)(2,1)S(1)}, bf16[64,1024]{1,0:T(8,128)(2,1)S(1)}, u32[]{:S(2)}, u32[]{:S(2)}) collective-permute-start(bf16[64,1024]{1,0:T(8,128)(2,1)S(1)} %add.6), channel_id=1, source_target_pairs={{16,2},{17,3},{18,0},{19,1},{20,6},{21,7},{22,4},{23,5},{24,10},{2... | collective-permute-start | bytes 393224 | tf_op jit(solution)/shard_map/ppermute | solution.py:748
  64.1 9.5 %collective-permute-start.19 = (f32[1,1024]{1,0:T(1,128)S(1)}, f32[1,1024]{1,0:T(1,128)S(1)}, u32[]{:S(2)}, u32[]{:S(2)}) collective-permute-start(f32[1,1024]{1,0:T(1,128)S(1)} %get-tuple-element.65), channel_id=1, source_target_pairs={{16,0},{17,1},{18,2},{19,3},{20,4},{21,5},{22,6},{23,7},{24,8},{25... | collective-permute-start | bytes 12296 | tf_op jit(solution)/shard_map/ppermute | solution.py:688
  74.4 1.4 %collective-permute-start.20 = (bf16[64,1024]{1,0:T(8,128)(2,1)S(1)}, bf16[64,1024]{1,0:T(8,128)(2,1)S(1)}, u32[]{:S(2)}, u32[]{:S(2)}) collective-permute-start(bf16[64,1024]{1,0:T(8,128)(2,1)S(1)} %shard_map.150.refs_2_), channel_id=1, source_target_pairs={{0,1},{1,0},{2,3},{3,2},{4,5},{5,4},{6,7},{7,6},{8,9},{9,8},{10,11... | collective-permute-start | bytes 393224 | tf_op jit(solution)/shard_map/ppermute | solution.py:602
  78.6 4.3 %collective-permute-start.21 = (bf16[64,1664]{1,0:T(8,128)(2,1)S(1)}, bf16[64,1664]{1,0:T(8,128)(2,1)S(1)}, u32[]{:S(2)}, u32[]{:S(2)}) collective-permute-start(bf16[64,1664]{1,0:T(8,128)(2,1)S(1)} %get-tuple-element.67), channel_id=1, source_target_pairs={{0,1},{1,0},{2,3},{3,2},{4,5},{5,4},{6,7},{7,6},{8,9},{9,8},{10,11... | collective-permute-start | bytes 638984 | tf_op jit(solution)/shard_map/ppermute | solution.py:602
  78.8 23.8 %collective-permute-start.31 = (bf16[128,960]{1,0:T(8,128)(2,1)S(1)}, bf16[128,960]{1,0:T(8,128)(2,1)S(1)}, u32[]{:S(2)}, u32[]{:S(2)}) collective-permute-start(bf16[128,960]{1,0:T(8,128)(2,1)S(1)} %get-tuple-element.53.refs_2_.refs_4_.refs_9_), channel_id=1, source_target_pairs={{0,8},{4,12},{8,0},{12,4},{1,9},{5,13},{9,1},{13,5},{2,10},{6,14},... | collective-permute-start | bytes 737288 | tf_op jit(solution)/shard_map/ppermute | solution.py:602
  80.4 26.0 %collective-permute-start.30 = (bf16[128,960]{1,0:T(8,128)(2,1)S(1)}, bf16[128,960]{1,0:T(8,128)(2,1)S(1)}, u32[]{:S(2)}, u32[]{:S(2)}) collective-permute-start(bf16[128,960]{1,0:T(8,128)(2,1)S(1)} %get-tuple-element.53.refs_2_.refs_4_.refs_9_), channel_id=1, source_target_pairs={{0,4},{4,0},{8,12},{12,8},{1,5},{5,1},{9,13},{13,9},{2,6},{6,2},{1... | collective-permute-start | bytes 737288 | tf_op jit(solution)/shard_map/ppermute | solution.py:602
  82.8 13.3 %collective-permute-start.23 = (bf16[64,384]{1,0:T(8,128)(2,1)S(1)}, bf16[64,384]{1,0:T(8,128)(2,1)S(1)}, u32[]{:S(2)}, u32[]{:S(2)}) collective-permute-start(bf16[64,384]{1,0:T(8,128)(2,1)S(1)} %get-tuple-element.72), channel_id=1, source_target_pairs={{0,4},{4,0},{8,12},{12,8},{1,5},{5,1},{9,13},{13,9},{2,6},{6,2},{1... | collective-permute-start | bytes 147464 | tf_op jit(solution)/shard_map/ppermute | solution.py:602
  82.9 24.7 %collective-permute-start.22 = (bf16[64,1664]{1,0:T(8,128)(2,1)S(1)}, bf16[64,1664]{1,0:T(8,128)(2,1)S(1)}, u32[]{:S(2)}, u32[]{:S(2)}) collective-permute-start(bf16[64,1664]{1,0:T(8,128)(2,1)S(1)} %add.7.refs_1_), channel_id=1, source_target_pairs={{0,2},{1,3},{2,0},{3,1},{4,6},{5,7},{6,4},{7,5},{8,10},{9,11},{10,... | collective-permute-start | bytes 638984 | tf_op jit(solution)/shard_map/ppermute | solution.py:756
  83.5 15.1 %collective-permute-start.24 = (bf16[64,384]{1,0:T(8,128)(2,1)S(1)}, bf16[64,384]{1,0:T(8,128)(2,1)S(1)}, u32[]{:S(2)}, u32[]{:S(2)}) collective-permute-start(bf16[64,384]{1,0:T(8,128)(2,1)S(1)} %get-tuple-element.73), channel_id=1, source_target_pairs={{0,8},{4,12},{8,0},{12,4},{1,9},{5,13},{9,1},{13,5},{2,10},{6,14},... | collective-permute-start | bytes 147464 | tf_op jit(solution)/shard_map/ppermute | solution.py:602
  96.2 5.9 %collective-permute-start.25 = (bf16[64,384]{1,0:T(8,128)(2,1)S(1)}, bf16[64,384]{1,0:T(8,128)(2,1)S(1)}, u32[]{:S(2)}, u32[]{:S(2)}) collective-permute-start(bf16[64,384]{1,0:T(8,128)(2,1)S(1)} %get-tuple-element.74), channel_id=1, source_target_pairs={{0,12},{4,8},{8,4},{12,0},{1,13},{5,9},{9,5},{13,1},{2,14},{6,10},... | collective-permute-start | bytes 147464 | tf_op jit(solution)/shard_map/ppermute | solution.py:602
  98.6 3.5 %collective-permute-start.26 = (bf16[64,384]{1,0:T(8,128)(2,1)S(1)}, bf16[64,384]{1,0:T(8,128)(2,1)S(1)}, u32[]{:S(2)}, u32[]{:S(2)}) collective-permute-start(bf16[64,384]{1,0:T(8,128)(2,1)S(1)} %get-tuple-element.71.refs_1_), channel_id=1, source_target_pairs={{0,1},{1,0},{2,3},{3,2},{4,5},{5,4},{6,7},{7,6},{8,9},{9,8},{10,11... | collective-permute-start | bytes 147464 | tf_op jit(solution)/shard_map/ppermute | solution.py:602
  102.1 1.2 collective-permute-start.27
  102.1 1.4 %collective-permute-start.28 = (bf16[64,384]{1,0:T(8,128)(2,1)S(1)}, bf16[64,384]{1,0:T(8,128)(2,1)S(1)}, u32[]{:S(2)}, u32[]{:S(2)}) collective-permute-start(bf16[64,384]{1,0:T(8,128)(2,1)S(1)} %collective-permute-done.24.refs_3_), channel_id=1, source_target_pairs={{0,1},{1,0},{2,3},{3,2},{4,5},{5,4},{6,7},{7,6},{8,9},{9,8},{10,11... | collective-permute-start | bytes 147464 | tf_op jit(solution)/shard_map/ppermute | solution.py:602
  102.6 20.5 %collective-permute-start.32 = (bf16[128,960]{1,0:T(8,128)(2,1)S(1)}, bf16[128,960]{1,0:T(8,128)(2,1)S(1)}, u32[]{:S(2)}, u32[]{:S(2)}) collective-permute-start(bf16[128,960]{1,0:T(8,128)(2,1)S(1)} %collective-permute-done.31.refs_11_), channel_id=1, source_target_pairs={{0,4},{4,0},{8,12},{12,8},{1,5},{5,1},{9,13},{13,9},{2,6},{6,2},{1... | collective-permute-start | bytes 737288 | tf_op jit(solution)/shard_map/ppermute | solution.py:602
  103.3 2.3 %collective-permute-start.29 = (bf16[64,384]{1,0:T(8,128)(2,1)S(1)}, bf16[64,384]{1,0:T(8,128)(2,1)S(1)}, u32[]{:S(2)}, u32[]{:S(2)}) collective-permute-start(bf16[64,384]{1,0:T(8,128)(2,1)S(1)} %collective-permute-done.25.refs_4_), channel_id=1, source_target_pairs={{0,1},{1,0},{2,3},{3,2},{4,5},{5,4},{6,7},{7,6},{8,9},{9,8},{10,11... | collective-permute-start | bytes 147464 | tf_op jit(solution)/shard_map/ppermute | solution.py:602
  103.5 16.0 %collective-permute-start.48 = (bf16[128,384]{1,0:T(8,128)(2,1)S(1)}, bf16[128,384]{1,0:T(8,128)(2,1)S(1)}, u32[]{:S(2)}, u32[]{:S(2)}) collective-permute-start(bf16[128,384]{1,0:T(8,128)(2,1)S(1)} %get-tuple-element.81.refs_13_), channel_id=1, source_target_pairs={{0,8},{4,12},{8,0},{12,4},{1,9},{5,13},{9,1},{13,5},{2,10},{6,14},... | collective-permute-start | bytes 294920 | tf_op jit(solution)/shard_map/ppermute | solution.py:602
  105.6 8.7 %collective-permute-start.33 = (bf16[64,256]{1,0:T(8,128)(2,1)S(1)}, bf16[64,256]{1,0:T(8,128)(2,1)S(1)}, u32[]{:S(2)}, u32[]{:S(2)}) collective-permute-start(bf16[64,256]{1,0:T(8,128)(2,1)S(1)} %get-tuple-element.76), channel_id=1, source_target_pairs={{0,4},{4,0},{8,12},{12,8},{1,5},{5,1},{9,13},{13,9},{2,6},{6,2},{1... | collective-permute-start | bytes 98312 | tf_op jit(solution)/shard_map/ppermute | solution.py:602
  106.4 9.2 %collective-permute-start.34 = (bf16[64,256]{1,0:T(8,128)(2,1)S(1)}, bf16[64,256]{1,0:T(8,128)(2,1)S(1)}, u32[]{:S(2)}, u32[]{:S(2)}) collective-permute-start(bf16[64,256]{1,0:T(8,128)(2,1)S(1)} %get-tuple-element.77), channel_id=1, source_target_pairs={{0,8},{4,12},{8,0},{12,4},{1,9},{5,13},{9,1},{13,5},{2,10},{6,14},... | collective-permute-start | bytes 98312 | tf_op jit(solution)/shard_map/ppermute | solution.py:602
  107.6 8.1 %collective-permute-start.35 = (bf16[64,256]{1,0:T(8,128)(2,1)S(1)}, bf16[64,256]{1,0:T(8,128)(2,1)S(1)}, u32[]{:S(2)}, u32[]{:S(2)}) collective-permute-start(bf16[64,256]{1,0:T(8,128)(2,1)S(1)} %get-tuple-element.78), channel_id=1, source_target_pairs={{0,12},{4,8},{8,4},{12,0},{1,13},{5,9},{9,5},{13,1},{2,14},{6,10},... | collective-permute-start | bytes 98312 | tf_op jit(solution)/shard_map/ppermute | solution.py:602
  114.4 7.1 %collective-permute-start.41 = (bf16[64,640]{1,0:T(8,128)(2,1)S(1)}, bf16[64,640]{1,0:T(8,128)(2,1)S(1)}, u32[]{:S(2)}, u32[]{:S(2)}) collective-permute-start(bf16[64,640]{1,0:T(8,128)(2,1)S(1)} %get-tuple-element.79.refs_21_), channel_id=1, source_target_pairs={{0,8},{4,12},{8,0},{12,4},{1,9},{5,13},{9,1},{13,5},{2,10},{6,14},... | collective-permute-start | bytes 245768 | tf_op jit(solution)/shard_map/ppermute | solution.py:602
  115.6 1.2 collective-permute-start.36
  115.7 1.2 collective-permute-start.37
  116.8 2.7 %collective-permute-start.38 = (bf16[64,256]{1,0:T(8,128)(2,1)S(1)}, bf16[64,256]{1,0:T(8,128)(2,1)S(1)}, u32[]{:S(2)}, u32[]{:S(2)}) collective-permute-start(bf16[64,256]{1,0:T(8,128)(2,1)S(1)} %collective-permute-done.34.refs_15_), channel_id=1, source_target_pairs={{0,1},{1,0},{2,3},{3,2},{4,5},{5,4},{6,7},{7,6},{8,9},{9,8},{10,11... | collective-permute-start | bytes 98312 | tf_op jit(solution)/shard_map/ppermute | solution.py:602
  117.0 6.1 %collective-permute-start.47 = (bf16[128,384]{1,0:T(8,128)(2,1)S(1)}, bf16[128,384]{1,0:T(8,128)(2,1)S(1)}, u32[]{:S(2)}, u32[]{:S(2)}) collective-permute-start(bf16[128,384]{1,0:T(8,128)(2,1)S(1)} %get-tuple-element.81.refs_13_), channel_id=1, source_target_pairs={{0,4},{4,0},{8,12},{12,8},{1,5},{5,1},{9,13},{13,9},{2,6},{6,2},{1... | collective-permute-start | bytes 294920 | tf_op jit(solution)/shard_map/ppermute | solution.py:602
  119.4 5.7 %collective-permute-start.49 = (bf16[128,384]{1,0:T(8,128)(2,1)S(1)}, bf16[128,384]{1,0:T(8,128)(2,1)S(1)}, u32[]{:S(2)}, u32[]{:S(2)}) collective-permute-start(bf16[128,384]{1,0:T(8,128)(2,1)S(1)} %collective-permute-done.48.refs_15_), channel_id=1, source_target_pairs={{0,4},{4,0},{8,12},{12,8},{1,5},{5,1},{9,13},{13,9},{2,6},{6,2},{1... | collective-permute-start | bytes 294920 | tf_op jit(solution)/shard_map/ppermute | solution.py:602
  119.5 7.4 %collective-permute-start.40 = (bf16[64,640]{1,0:T(8,128)(2,1)S(1)}, bf16[64,640]{1,0:T(8,128)(2,1)S(1)}, u32[]{:S(2)}, u32[]{:S(2)}) collective-permute-start(bf16[64,640]{1,0:T(8,128)(2,1)S(1)} %get-tuple-element.79.refs_21_), channel_id=1, source_target_pairs={{0,4},{4,0},{8,12},{12,8},{1,5},{5,1},{9,13},{13,9},{2,6},{6,2},{1... | collective-permute-start | bytes 245768 | tf_op jit(solution)/shard_map/ppermute | solution.py:602
  121.5 6.9 %collective-permute-start.42 = (bf16[64,640]{1,0:T(8,128)(2,1)S(1)}, bf16[64,640]{1,0:T(8,128)(2,1)S(1)}, u32[]{:S(2)}, u32[]{:S(2)}) collective-permute-start(bf16[64,640]{1,0:T(8,128)(2,1)S(1)} %collective-permute-done.41.refs_23_), channel_id=1, source_target_pairs={{0,4},{4,0},{8,12},{12,8},{1,5},{5,1},{9,13},{13,9},{2,6},{6,2},{1... | collective-permute-start | bytes 245768 | tf_op jit(solution)/shard_map/ppermute | solution.py:602
  123.1 8.0 %collective-permute-start.39 = (bf16[64,256]{1,0:T(8,128)(2,1)S(1)}, bf16[64,256]{1,0:T(8,128)(2,1)S(1)}, u32[]{:S(2)}, u32[]{:S(2)}) collective-permute-start(bf16[64,256]{1,0:T(8,128)(2,1)S(1)} %collective-permute-done.35.refs_16_), channel_id=1, source_target_pairs={{0,1},{1,0},{2,3},{3,2},{4,5},{5,4},{6,7},{7,6},{8,9},{9,8},{10,11... | collective-permute-start | bytes 98312 | tf_op jit(solution)/shard_map/ppermute | solution.py:602
  123.1 8.0 %collective-permute-start.43 = (bf16[64,640]{1,0:T(8,128)(2,1)S(1)}, bf16[64,640]{1,0:T(8,128)(2,1)S(1)}, u32[]{:S(2)}, u32[]{:S(2)}) collective-permute-start(bf16[64,640]{1,0:T(8,128)(2,1)S(1)} %get-tuple-element.79.refs_21_), channel_id=1, source_target_pairs={{0,1},{1,0},{2,3},{3,2},{4,5},{5,4},{6,7},{7,6},{8,9},{9,8},{10,11... | collective-permute-start | bytes 245768 | tf_op jit(solution)/shard_map/ppermute | solution.py:602
  125.2 5.9 %collective-permute-start.45 = (bf16[64,640]{1,0:T(8,128)(2,1)S(1)}, bf16[64,640]{1,0:T(8,128)(2,1)S(1)}, u32[]{:S(2)}, u32[]{:S(2)}) collective-permute-start(bf16[64,640]{1,0:T(8,128)(2,1)S(1)} %collective-permute-done.41.refs_23_), channel_id=1, source_target_pairs={{0,1},{1,0},{2,3},{3,2},{4,5},{5,4},{6,7},{7,6},{8,9},{9,8},{10,11... | collective-permute-start | bytes 245768 | tf_op jit(solution)/shard_map/ppermute | solution.py:602
  126.9 4.1 %collective-permute-start.44 = (bf16[64,640]{1,0:T(8,128)(2,1)S(1)}, bf16[64,640]{1,0:T(8,128)(2,1)S(1)}, u32[]{:S(2)}, u32[]{:S(2)}) collective-permute-start(bf16[64,640]{1,0:T(8,128)(2,1)S(1)} %collective-permute-done.40.refs_22_), channel_id=1, source_target_pairs={{0,1},{1,0},{2,3},{3,2},{4,5},{5,4},{6,7},{7,6},{8,9},{9,8},{10,11... | collective-permute-start | bytes 245768 | tf_op jit(solution)/shard_map/ppermute | solution.py:602
  128.3 2.7 %collective-permute-start.46 = (bf16[64,640]{1,0:T(8,128)(2,1)S(1)}, bf16[64,640]{1,0:T(8,128)(2,1)S(1)}, u32[]{:S(2)}, u32[]{:S(2)}) collective-permute-start(bf16[64,640]{1,0:T(8,128)(2,1)S(1)} %collective-permute-done.42.refs_24_), channel_id=1, source_target_pairs={{0,1},{1,0},{2,3},{3,2},{4,5},{5,4},{6,7},{7,6},{8,9},{9,8},{10,11... | collective-permute-start | bytes 245768 | tf_op jit(solution)/shard_map/ppermute | solution.py:602
